TPU v7x, 128 devices: a whole 4x4x4 slice. The times are simulated.
128 devices in a mesh: dp: 32 (over y, x, z_hi), mp: 4 (over z_lo, core).
Axes of the slice: x: 4, y: 4, z: 4 (z_hi: 2, z_lo: 2; z = z_hi * 2 + z_lo), core: 2. Of those that a mesh axis runs over, the one named last changes fastest.
Arguments:
- page_pool: bfloat16 [2048, 128, 512], P('dp'), may hold values from -6 to 6
- move_count: int32 [32, 32], P('dp'), may hold values from 0 to 2, as said below
- send_slots: int32 [1024, 2], P('dp'), may hold values from 0 to 63, as said below
- page_table: int32 [2048, 16], P('dp'), may hold values from 0 to 127, as said below
- history_len: int32 [2048], P('dp'), may hold values from 1 to 2048, as said below
- queries: bfloat16 [2048, 8, 256], P('dp', 'mp'), may hold values from -6 to 6
- new_entry: bfloat16 [2048, 512], P('dp'), may hold values from -6 to 6
- residual: bfloat16 [2048, 2048], P('dp'), may hold values from -30 to 30
- out_proj: bfloat16 [2048, 2048], P('mp'), may hold values from -0.125 to 0.125
- ffn_gain: float32 [2048], replicated, may hold values from -0.5 to 0.5
- gate_proj: bfloat16 [2048, 16384], P(None, ('dp', 'mp')), may hold values from -0.125 to 0.125
- up_proj: bfloat16 [2048, 16384], P(None, ('dp', 'mp')), may hold values from -0.125 to 0.125
- down_proj: bfloat16 [16384, 2048], P(('dp', 'mp')), may hold values from -0.046875 to 0.046875
Outputs:
- arrived: bfloat16 [2048, 128, 512], P('dp')
- layer_out: bfloat16 [2048, 2048], P('dp')
Inputs may be any that keep to these rules, and one draw needn't show every extreme that they name: `move_count`: zero on the diagonal; in every draw one device receives exactly 2 pages from every other device. `send_slots`: only the first move_count[s, d] entries of row s * 32 + d are sent. `page_table`: for a game of device d, an entry e >= 64 equals 64 + s * 2 + c with c < move_count[s, d]. `history_len`: some game of some device reaches 2048 in every draw.
All inputs are finite; a program needn't handle non-finite values.
Results may differ from a plain program's by a relative error of at most 0.0075.
Values may be sent and summed in bfloat16 or wider, within the bound.
No kernel may reach another device: no remote copies, remote signals or barrier semaphores. Data moves between devices by JAX's collectives and lax.ppermute only.
A program may use at most 128 MiB of HBM per device.

v0:
```python
import math

import jax
import jax.numpy as jnp
from jax import lax
from jax.sharding import PartitionSpec as P


def copy_for_each(array, axis):
    peers = lax.axis_size(axis)
    return lax.all_to_all(
        jnp.broadcast_to(array[None], (peers, *array.shape)), axis, 0, 0, tiled=True
    )


def taken_together(array, axis):
    everything = copy_for_each(array, axis)
    return jnp.sum(everything, axis=0)


def in_blocks(array, dim, peers):
    lengths = array.shape
    tiles = array.reshape(*lengths[:dim], peers, lengths[dim] // peers, *lengths[dim + 1 :])
    return jnp.moveaxis(tiles, dim, 0)


def sum_at_owner(array, axis, dim):
    tiles = in_blocks(array, dim, lax.axis_size(axis))
    arrived = lax.all_to_all(tiles, axis, split_axis=0, concat_axis=0, tiled=True)
    return arrived.astype(jnp.float32).sum(axis=0)


def attend_block(query_blk, page_rows, length_blk, entry_blk):
    head_size = query_blk.shape[-1]
    keys = page_rows[:, :, :head_size]
    values = page_rows[:, :, head_size:]
    factor = 1.0 / math.sqrt(head_size)
    scores = (
        jnp.einsum("bhd,btd->bht", query_blk, keys, preferred_element_type=jnp.float32) * factor
    )
    own = (
        jnp.einsum(
            "bhd,bd->bh", query_blk, entry_blk[:, :head_size], preferred_element_type=jnp.float32
        )
        * factor
    )
    places = jnp.arange(page_rows.shape[1], dtype=jnp.int32)
    valid = places[None, None, :] < length_blk[:, None, None]
    scores = jnp.where(valid, scores, jnp.float32(-1e30))
    biggest = jnp.maximum(jnp.max(scores, axis=-1), own)
    probs = jnp.where(valid, jnp.exp(scores - biggest[..., None]), jnp.float32(0.0))
    prob_own = jnp.exp(own - biggest)
    denom = jnp.sum(probs, axis=-1) + prob_own
    weights = (probs / denom[..., None]).astype(jnp.bfloat16)
    weight_own = (prob_own / denom).astype(jnp.bfloat16)
    result = jnp.einsum("bht,btd->bhd", weights, values, preferred_element_type=jnp.float32)
    result = result + weight_own.astype(jnp.float32)[..., None] * entry_blk[
        :, None, head_size:
    ].astype(jnp.float32)
    return result.astype(jnp.bfloat16)


def local(
    page_pool,
    move_count,
    send_slots,
    page_table,
    history_len,
    queries,
    new_entry,
    residual,
    out_proj,
    ffn_gain,
    gate_proj,
    up_proj,
    down_proj,
):
    senders = lax.axis_size("dp")
    groups = lax.axis_size("mp")
    games = queries.shape[0]
    local_heads = queries.shape[1]
    head_size = queries.shape[2]
    page_len = page_pool.shape[1]
    width = page_pool.shape[2]
    slot_count = send_slots.shape[1]
    table_len = page_table.shape[1]
    live = jnp.arange(slot_count, dtype=jnp.int32)[None, :] < move_count[0][:, None]
    quarter = page_len // groups
    token_part = lax.dynamic_slice_in_dim(page_pool, lax.axis_index("mp") * quarter, quarter, 1)
    outgoing = token_part[send_slots]
    outgoing = jnp.where(live[:, :, None, None], outgoing, jnp.zeros((), jnp.bfloat16))
    partial_pages = lax.all_to_all(outgoing, "dp", split_axis=0, concat_axis=0, tiled=True)
    received = lax.all_gather(partial_pages, "mp", axis=2, tiled=True)
    arrived = received.reshape(senders * slot_count, page_len, width)
    every_page = jnp.concatenate([page_pool, arrived], axis=0)
    block = math.gcd(games, 8)
    table = page_table.reshape(-1, block, table_len)
    lengths = history_len.reshape(-1, block)
    query_dev = queries.reshape(-1, block, local_heads, head_size)
    entry_dev = new_entry.reshape(-1, block, width)

    def one_block(items):
        table_blk, length_blk, query_blk, entry_blk = items
        page_rows = every_page[table_blk].reshape(block, table_len * page_len, width)
        return attend_block(query_blk, page_rows, length_blk, entry_blk)

    attended = lax.map(one_block, (table, lengths, query_dev, entry_dev)).reshape(
        games, local_heads * head_size
    )
    head_part = jnp.dot(attended, out_proj, preferred_element_type=jnp.float32)
    stream_in = residual.astype(jnp.float32) + taken_together(head_part, "mp")
    scale_row = lax.rsqrt(jnp.mean(stream_in * stream_in, axis=-1, keepdims=True) + 1e-06)
    normed = (stream_in * scale_row * (1.0 + ffn_gain)).astype(jnp.bfloat16)
    piece = lax.all_gather(normed, "dp", axis=0, tiled=True)
    gate = jnp.dot(piece, gate_proj, preferred_element_type=jnp.float32)
    up_val = jnp.dot(piece, up_proj, preferred_element_type=jnp.float32)
    hidden = (jax.nn.gelu(gate, approximate=True) * up_val).astype(jnp.bfloat16)
    partial_out = sum_at_owner(
        jnp.dot(hidden, down_proj, preferred_element_type=jnp.float32).astype(jnp.bfloat16), "dp", 0
    )
    mixed = lax.psum(partial_out, "mp")
    layer_out = (stream_in + mixed).astype(jnp.bfloat16)
    return (arrived, layer_out)


def solution(mesh):
    in_specs = (
        P("dp", None, None),
        P("dp", None),
        P("dp", None),
        P("dp", None),
        P("dp"),
        P("dp", "mp", None),
        P("dp", None),
        P("dp", None),
        P("mp", None),
        P(),
        P(None, ("dp", "mp")),
        P(None, ("dp", "mp")),
        P(("dp", "mp"), None),
    )
    out_specs = (P("dp", None, None), P("dp", None))
    return jax.shard_map(local, mesh=mesh, in_specs=in_specs, out_specs=out_specs, check_vma=False)
```

profile of v0, /device:TPU:1, one launch (start us, length us, event | category | flops | bytes accessed | tf_op | source)
XLA Modules:
  0.0 678.5 jit_solution(8073125660301408105)
XLA Ops:
  17.6 40.7 %all_to_all.15 = bf16[32,2,32,512]{3,2,1,0:T(8,128)(2,1)} all-to-all(bf16[32,2,32,512]{3,2,1,0:T(8,128)(2,1)S(1)} %broadcast_select_fusion), channel_id=1, replica_groups=mesh['dp'=32,'mp'=4] {'dp'}, dimensions={0} | all-to-all | bytes 4194304 | tf_op jit(solution)/shard_map/all_to_all | solution.py:92
  58.5 78.7 %all-gather.3.cloned.1.call-done = bf16[32,2,128,512]{3,2,1,0:T(8,128)(2,1)} async-done(((bf16[32,2,32,512]{3,2,1,0:T(8,128)(2,1)}), bf16[32,2,128,512]{3,2,1,0:T(8,128)(2,1)}) %all-gather.3.cloned.1.call-update) | async-done | bytes 8388624 | tf_op jit(solution)/shard_map/all_gather | solution.py:93
  137.2 13.8 %pad_maximum_fusion = bf16[128,128,512]{2,1,0:T(8,128)(2,1)} fusion(bf16[64,128,512]{2,1,0:T(8,128)(2,1)} %bitcast.59, bf16[64,128,512]{2,1,0:T(8,128)(2,1)} %param.15), kind=kLoop, calls=%fused_computation.35 | loop fusion | flops 8388608 | bytes 33554432 | tf_op jit(solution)/shard_map/concatenate | solution.py:95
  150.9 212.0 %while.10 = (s32[]{:T(128)}, bf16[8,8,2,256]{3,2,1,0:T(2,128)(2,1)S(1)}, s32[8,8]{1,0:T(8,128)S(1)}, bf16[8,8,2,256]{3,2,1,0:T(2,128)(2,1)}, s32[8,8,16]{2,1,0:T...) while((s32[]{:T(128)}, bf16[8,8,2,256]{3,2,1,0:T(2,128)(2,1)S(1)}, ...), condition=%wide.region_3.4_spmd, body=%wide.region_0.3_spmd.sunk | while | flops 33922544 | bytes 50886080 | solution.py:107
  151.0 14.1 %gather_fusion = bf16[128,128,512]{2,1,0:T(8,128)(2,1)} fusion(bf16[128,128,512]{2,1,0:T(8,128)(2,1)} %get-tuple-element.136, s32[1024]{0:T(1024)S(1)} %pad_clamp_fusion.3), kind=kCustom, calls=%fused_computation.clone.1 | custom fusion | bytes 33554944 | tf_op jit(solution)/shard_map/while/body/eval_jaxpr/gather | solution.py:104
  177.5 14.0 %gather_fusion = bf16[128,128,512]{2,1,0:T(8,128)(2,1)} fusion(bf16[128,128,512]{2,1,0:T(8,128)(2,1)} %get-tuple-element.136, s32[1024]{0:T(1024)S(1)} %pad_clamp_fusion.3), kind=kCustom, calls=%fused_computation.clone.1 | custom fusion | bytes 33554944 | tf_op jit(solution)/shard_map/while/body/eval_jaxpr/gather | solution.py:104
  191.7 5.8 fusion.71
  204.0 14.1 %gather_fusion = bf16[128,128,512]{2,1,0:T(8,128)(2,1)} fusion(bf16[128,128,512]{2,1,0:T(8,128)(2,1)} %get-tuple-element.136, s32[1024]{0:T(1024)S(1)} %pad_clamp_fusion.3), kind=kCustom, calls=%fused_computation.clone.1 | custom fusion | bytes 33554944 | tf_op jit(solution)/shard_map/while/body/eval_jaxpr/gather | solution.py:104
  218.2 5.8 fusion.71
  230.5 14.1 %gather_fusion = bf16[128,128,512]{2,1,0:T(8,128)(2,1)} fusion(bf16[128,128,512]{2,1,0:T(8,128)(2,1)} %get-tuple-element.136, s32[1024]{0:T(1024)S(1)} %pad_clamp_fusion.3), kind=kCustom, calls=%fused_computation.clone.1 | custom fusion | bytes 33554944 | tf_op jit(solution)/shard_map/while/body/eval_jaxpr/gather | solution.py:104
  244.7 5.8 fusion.71
  257.0 14.1 %gather_fusion = bf16[128,128,512]{2,1,0:T(8,128)(2,1)} fusion(bf16[128,128,512]{2,1,0:T(8,128)(2,1)} %get-tuple-element.136, s32[1024]{0:T(1024)S(1)} %pad_clamp_fusion.3), kind=kCustom, calls=%fused_computation.clone.1 | custom fusion | bytes 33554944 | tf_op jit(solution)/shard_map/while/body/eval_jaxpr/gather | solution.py:104
  271.2 5.8 fusion.71
  283.5 14.1 %gather_fusion = bf16[128,128,512]{2,1,0:T(8,128)(2,1)} fusion(bf16[128,128,512]{2,1,0:T(8,128)(2,1)} %get-tuple-element.136, s32[1024]{0:T(1024)S(1)} %pad_clamp_fusion.3), kind=kCustom, calls=%fused_computation.clone.1 | custom fusion | bytes 33554944 | tf_op jit(solution)/shard_map/while/body/eval_jaxpr/gather | solution.py:104
  297.7 5.8 fusion.71
  310.0 14.1 %gather_fusion = bf16[128,128,512]{2,1,0:T(8,128)(2,1)} fusion(bf16[128,128,512]{2,1,0:T(8,128)(2,1)} %get-tuple-element.136, s32[1024]{0:T(1024)S(1)} %pad_clamp_fusion.3), kind=kCustom, calls=%fused_computation.clone.1 | custom fusion | bytes 33554944 | tf_op jit(solution)/shard_map/while/body/eval_jaxpr/gather | solution.py:104
  336.5 14.1 %gather_fusion = bf16[128,128,512]{2,1,0:T(8,128)(2,1)} fusion(bf16[128,128,512]{2,1,0:T(8,128)(2,1)} %get-tuple-element.136, s32[1024]{0:T(1024)S(1)} %pad_clamp_fusion.3), kind=kCustom, calls=%fused_computation.clone.1 | custom fusion | bytes 33554944 | tf_op jit(solution)/shard_map/while/body/eval_jaxpr/gather | solution.py:104
  369.5 23.6 %all-to-all-done.1 = f32[4,64,2048]{2,1,0:T(8,128)} async-done(((f32[4,64,2048]{2,1,0:T(8,128)}), f32[4,64,2048]{2,1,0:T(8,128)}, u32[]{:S(2)}, u32[]{:S(2)}) %all-to-all-start.1) | async-done | bytes 2097184 | tf_op jit(solution)/shard_map/all_to_all | solution.py:11
  395.9 105.3 %all-gather.5.cloned.1.call-done = bf16[2048,2048]{1,0:T(8,128)(2,1)} async-done(((bf16[64,2048]{1,0:T(8,128)(2,1)}), bf16[2048,2048]{1,0:T(8,128)(2,1)}) %all-gather.5.cloned.1.call-update) | async-done | bytes 8388624 | tf_op jit(solution)/shard_map/all_gather | solution.py:114
  501.3 6.8 %fusion.51 = f32[2048,128]{1,0:T(8,128)} fusion(bf16[2048,2048]{1,0:T(8,128)(2,1)} %all-gather.5.cloned.1.call-done, bf16[2048,128]{1,0:T(8,128)(2,1)} %param.25), kind=kOutput, calls=%fused_computation.69 | convolution fusion | flops 1073741824 | bytes 9961472 | tf_op jit(solution)/shard_map/dot_general | solution.py:115
  508.1 13.2 %convolution_convert_fusion = bf16[2048,2048]{1,0:T(8,128)(2,1)} fusion(bf16[128,2048]{1,0:T(8,128)(2,1)S(1)} %copy-done.2, bf16[2048,2048]{1,0:T(8,128)(2,1)} %all-gather.5.cloned.1.call-done, bf16[2048,128]{1,0:T(8,128)(2,1)} %param.26, f32[2048,128]{1,0:T(8,128)} %fusion.51), kind=kOutput, calls=%fused_computation.37 | convolution fusion | flops 2154299392 | bytes 18874368 | tf_op jit(solution)/shard_map/dot_general | solution.py:119
  521.3 102.2 %all_to_all.16 = bf16[32,64,2048]{2,1,0:T(8,128)(2,1)S(1)} all-to-all(bf16[32,64,2048]{2,1,0:T(8,128)(2,1)} %bitcast.58), channel_id=1, replica_groups=mesh['dp'=32,'mp'=4] {'dp'}, dimensions={0} | all-to-all | bytes 16777216 | tf_op jit(solution)/shard_map/all_to_all | solution.py:29
  626.4 36.0 %all-reduce.2.cloned.1.call-done = f32[64,2048]{1,0:T(8,128)} async-done(((f32[64,2048]{1,0:T(8,128)}), f32[64,2048]{1,0:T(8,128)}) %all-reduce.2.cloned.1.call-update) | async-done | bytes 524304 | tf_op jit(solution)/shard_map/psum | solution.py:121
  664.2 7.8 %copy.39 = bf16[64,128,512]{2,1,0:T(8,128)(2,1)} copy(bf16[64,128,512]{2,1,0:T(8,128)(2,1)} %bitcast.60) | data formatting | bytes 16777216
  (139 shorter events, 95.3 us)
Async XLA Ops:
  7.2 355.8 %copy-start = (bf16[512,2048]{1,0:T(8,128)(2,1)S(1)}, bf16[512,2048]{1,0:T(8,128)(2,1)}, u32[]{:S(2)}) copy-start(bf16[512,2048]{1,0:T(8,128)(2,1)} %param.23) | copy-start | bytes 6291460
  7.2 130.0 %all-gather.3.cloned.1.call-start = ((), (), s32[]{:S(2)}) async-start(), calls=%async_computation.3 | async-start | bytes 10485760 | tf_op jit(solution)/shard_map/all_gather | solution.py:93
  12.2 46.1 %copy-start.3 = (s32[64,16]{0,1:T(8,128)S(1)}, s32[64,16]{0,1:T(8,128)}, u32[]{:S(2)}) copy-start(s32[64,16]{0,1:T(8,128)} %param.18) | copy-start | bytes 12292
  12.2 46.2 %copy-start.5 = (s32[64]{0:T(128)S(1)}, s32[64]{0:T(128)}, u32[]{:S(2)}) copy-start(s32[64]{0:T(128)} %param.19) | copy-start | bytes 772
  362.9 6.6 copy-start.4
  362.9 31.9 %copy-start.1 = (bf16[64,2048]{1,0:T(8,128)(2,1)S(1)}, bf16[64,2048]{1,0:T(8,128)(2,1)}, u32[]{:S(2)}) copy-start(bf16[64,2048]{1,0:T(8,128)(2,1)} %param.22) | copy-start | bytes 786436
  365.0 28.1 %all-to-all-start.1 = ((f32[4,64,2048]{2,1,0:T(8,128)}), f32[4,64,2048]{2,1,0:T(8,128)}, u32[]{:S(2)}, u32[]{:S(2)}) async-start(f32[4,64,2048]{2,1,0:T(8,128)} %broadcast_in_dim.61), calls=%async_computation.1 | async-start | bytes 4194304 | tf_op jit(solution)/shard_map/all_to_all | solution.py:11
  369.4 138.7 %copy-start.2 = (bf16[128,2048]{1,0:T(8,128)(2,1)S(1)}, bf16[128,2048]{1,0:T(8,128)(2,1)}, u32[]{:S(2)}) copy-start(bf16[128,2048]{1,0:T(8,128)(2,1)} %param.27) | copy-start | bytes 1572868
  369.4 131.8 %all-gather.5.cloned.1.call-start = ((), (), s32[]{:S(2)}) async-start(), calls=%async_computation.4 | async-start | bytes 8650752 | tf_op jit(solution)/shard_map/all_gather | solution.py:114
  395.9 266.5 %all-reduce.2.cloned.1.call-start = ((), (), s32[]{:S(2)}) async-start(), calls=%async_computation.5 | async-start | bytes 1048576 | tf_op jit(solution)/shard_map/psum | solution.py:121
Sparse Core Ops, SparseCore 0:
  58.4 78.7 all-gather.2
  396.0 105.2 all-gather.4
  626.5 35.8 all-reduce.1
where the time goes:
time: 681 us; the launch traced here: 679 us
  waiting for transfers between devices  244 us (36%)
  blocking collectives  143 us (21%)
  local copies, waits for them, and re-layouts  135 us (20%)
  matrix products  110 us (16%)
  other arithmetic  27.9 us (4%)
  between operations  13.9 us (2%)
    gather x8, local copies, waits for them, and re-layouts, one_block(): every_page[table_blk].reshape(block, table_len * page_len, width)  113 us
    all_gather x1, waiting for transfers between devices, local(): piece = lax.all_gather(normed, 'dp', axis=0, tiled=True)  105 us
    all_to_all x1, blocking collectives, sum_at_owner(): lax.all_to_all(tiles, axis, split_axis=0, concat_axis=0, tiled=True)  102 us
    all_gather x1, waiting for transfers between devices, local(): received = lax.all_gather(partial_pages, 'mp', axis=2, tiled=True)  78.7 us
    dot_general x8, matrix products, attend_block(): jnp.einsum('bhd,btd->bht', query_blk, keys, preferred_element_type=jnp.fl...  46 us
    all_to_all x1, blocking collectives, local(): lax.all_to_all(outgoing, 'dp', split_axis=0, concat_axis=0, tiled=True)  40.7 us
    dot_general x8, matrix products, attend_block(): jnp.einsum('bht,btd->bhd', weights, values, preferred_element_type=jnp.fl...  37.1 us
    psum x1, waiting for transfers between devices, local(): mixed = lax.psum(partial_out, 'mp')  36 us
  transfers between devices with their start and end apart: 4, of which 4 were waited for; matrix products, arithmetic and copies ran while one was open for 0% of the time, Pallas kernels for 0%

commit v1 on v0

v1 whole, which is shorter than its diff:
```python
import jax
import jax.numpy as jnp
from jax import lax
from jax.experimental import pallas as pl
from jax.experimental.pallas import tpu as pltpu
from jax.sharding import PartitionSpec as P

NEG = -1e30
BF = jnp.bfloat16
F32 = jnp.float32
VLIM = 60 * 1024 * 1024


def params(**kw):
    return pltpu.CompilerParams(vmem_limit_bytes=VLIM, **kw)


def cost(us):
    return pl.CostEstimate(flops=int(us * 4e8), bytes_accessed=int(us * 2e6), transcendentals=0)


def outgoing_kernel(half_ref, slot_ref, count_ref, pool_ref, out_ref, sems):
    pages, rows, _ = out_ref.shape
    caps = pages // count_ref.shape[0]
    first = pl.multiple_of(half_ref[0] * rows, rows)

    def copy(i):
        src = pool_ref.at[slot_ref[i], pl.ds(first, rows), :]
        return pltpu.make_async_copy(src, out_ref.at[i], sems.at[i])

    for i in range(pages):
        copy(i).start()
    for i in range(pages):
        copy(i).wait()

        @pl.when(i % caps >= count_ref[i // caps])
        def _():
            out_ref[i] = jnp.zeros(out_ref.shape[1:], out_ref.dtype)


def outgoing_pages(half, slots, counts, pool):
    pages = slots.shape[0]
    rows = pool.shape[1] // 2
    return pl.pallas_call(
        outgoing_kernel,
        grid_spec=pltpu.PrefetchScalarGridSpec(
            num_scalar_prefetch=3,
            grid=(1,),
            in_specs=[pl.BlockSpec(memory_space=pl.ANY)],
            out_specs=pl.BlockSpec((pages, rows, pool.shape[2]), lambda i, *_: (0, 0, 0)),
            scratch_shapes=[pltpu.SemaphoreType.DMA((pages,))],
        ),
        out_shape=jax.ShapeDtypeStruct((pages, rows, pool.shape[2]), pool.dtype),
        compiler_params=params(),
        cost_estimate=cost(3),
        name="outgoing",
    )(half, slots, counts, pool)


def attend_kernel(
    half_ref, qa_ref, qb_ref, entry_ref, tab_ref, len_ref, pool_ref, got_ref,
    keep_ref, send_ref, acc, stat, full, part,
):
    i = pl.program_id(0)
    steps = pl.num_programs(0)
    pages, rows, width = pool_ref.shape
    hd = width // 2
    mine = qa_ref.shape[0]
    lanes = 2 * mine
    games = entry_ref.shape[0]
    q = jnp.concatenate([qa_ref[...], qb_ref[...]], axis=0)

    @pl.when(i == 0)
    def _():
        entries = full.shape[0]
        page_id = lax.broadcasted_iota(jnp.int32, (entries, lanes), 0)
        whole = jnp.zeros((entries, lanes), F32)
        rest = jnp.zeros((entries, lanes), jnp.int32)
        for j in range(tab_ref.shape[0]):
            hit = page_id == tab_ref[j : j + 1, :]
            kept = len_ref[...] - j * 2 * rows
            whole += jnp.where(hit & (kept >= 2 * rows), 1.0, 0.0)
            rest += jnp.where(hit & (kept > 0) & (kept < 2 * rows), kept, 0)
        full[...] = whole
        part[...] = rest - half_ref[0] * rows
        s = lax.dot_general(
            entry_ref[:, :hd], q, (((1,), (1,)), ((), ())), preferred_element_type=F32
        )
        game = lax.broadcasted_iota(jnp.int32, (games, lanes), 0)
        lane = lax.broadcasted_iota(jnp.int32, (games, lanes), 1)
        own = (lane < mine) & (lax.rem(lane, games) == game)
        top = jnp.max(jnp.where(own, s, NEG), axis=0, keepdims=True)
        p = jnp.where(own, 1.0, 0.0)
        stat[0:1, :] = top
        stat[1:2, :] = jnp.sum(p, axis=0, keepdims=True)
        acc[...] = lax.dot_general(
            entry_ref[:, hd:], p.astype(BF), (((0,), (0,)), ((), ())), preferred_element_type=F32
        )

    def chunk(block):
        keys = block[:, :, :hd].reshape(pages * rows, hd)
        values = block[:, :, hd:].reshape(pages * rows, hd)
        s = lax.dot_general(keys, q, (((1,), (1,)), ((), ())), preferred_element_type=F32)
        spot = lax.broadcasted_iota(jnp.int32, (rows, lanes), 0)
        old = stat[0:1, :]
        top = old
        counts = []
        masked = []
        base = i * pages
        for j in range(pages):
            c = full[pl.ds(base + j, 1), :] + jnp.where(
                spot < part[pl.ds(base + j, 1), :], 1.0, 0.0
            )
            sj = jnp.where(c > 0.0, s[j * rows : (j + 1) * rows, :], NEG)
            top = jnp.maximum(top, jnp.max(sj, axis=0, keepdims=True))
            counts.append(c)
            masked.append(sj)
        shrink = jnp.exp(old - top)
        total = stat[1:2, :] * shrink
        probs = []
        for j in range(pages):
            p = jnp.exp(masked[j] - top) * counts[j]
            total += jnp.sum(p, axis=0, keepdims=True)
            probs.append(p.astype(BF))
        p = jnp.concatenate(probs, axis=0)
        stat[0:1, :] = top
        stat[1:2, :] = total
        acc[...] = acc[...] * shrink + lax.dot_general(
            values, p, (((0,), (0,)), ((), ())), preferred_element_type=F32
        )

    @pl.when(i < steps // 2)
    def _():
        chunk(pool_ref)

    @pl.when(i >= steps // 2)
    def _():
        chunk(got_ref)

    @pl.when(i == steps - 1)
    def _():
        for k, out in enumerate((keep_ref, send_ref)):
            out[:hd, :] = acc[:, k * mine : (k + 1) * mine]
            out[hd : hd + 8, :] = stat[:, k * mine : (k + 1) * mine]


def attend(half, q_mine, q_peer, entry, table, lengths, pool, got):
    slots, rows, width = got.shape
    mine, hd = q_mine.shape
    block = 8
    half_steps = slots // block
    whole = lambda shape: pl.BlockSpec(shape, lambda i, *_: (0,) * len(shape))
    out = jax.ShapeDtypeStruct((hd + 8, mine), F32)
    return pl.pallas_call(
        attend_kernel,
        grid_spec=pltpu.PrefetchScalarGridSpec(
            num_scalar_prefetch=1,
            grid=(2 * half_steps,),
            in_specs=[
                whole(q_mine.shape),
                whole(q_peer.shape),
                whole(entry.shape),
                whole(table.shape),
                whole(lengths.shape),
                pl.BlockSpec(
                    (block, rows, width), lambda i, h: (jnp.minimum(i, half_steps - 1), h[0], 0)
                ),
                pl.BlockSpec(
                    (block, rows, width), lambda i, h: (jnp.maximum(i - half_steps, 0), 0, 0)
                ),
            ],
            out_specs=[whole(out.shape), whole(out.shape)],
            scratch_shapes=[
                pltpu.VMEM((hd, 2 * mine), F32),
                pltpu.VMEM((8, 2 * mine), F32),
                pltpu.VMEM((2 * slots, 2 * mine), F32),
                pltpu.VMEM((2 * slots, 2 * mine), jnp.int32),
            ],
        ),
        out_shape=[out, out],
        compiler_params=params(),
        cost_estimate=cost(8),
        name="attend",
    )(half, q_mine, q_peer, entry, table, lengths, pool, got)


def project_kernel(mine_ref, a_ref, b_ref, w_ref, keep_ref, send_ref, scratch):
    hd = a_ref.shape[0] - 8
    ma, mb = a_ref[hd : hd + 1, :], b_ref[hd : hd + 1, :]
    top = jnp.maximum(ma, mb)
    wa, wb = jnp.exp(ma - top), jnp.exp(mb - top)
    den = a_ref[hd + 1 : hd + 2, :] * wa + b_ref[hd + 1 : hd + 2, :] * wb
    att = (a_ref[:hd, :] * wa + b_ref[:hd, :] * wb) / den
    att = att.T.astype(BF)
    games = scratch.shape[0]
    out = jnp.zeros(scratch.shape, F32)
    for h in range(att.shape[0] // games):
        out += jnp.dot(
            att[h * games : (h + 1) * games, :],
            w_ref[h * hd : (h + 1) * hd, :],
            preferred_element_type=F32,
        )
    scratch[...] = out
    rows = keep_ref.shape[1]
    m = mine_ref[0]
    core = lax.rem(m, 2)
    side = m // 2
    for ref, c in ((keep_ref, core), (send_ref, 1 - core)):
        for k, z in enumerate((side, 1 - side)):
            first = pl.multiple_of((z * 2 + c) * rows, rows)
            ref[k] = scratch[pl.ds(first, rows), :]


def project(mine, a, b, w, games):
    rows = games // 4
    whole = lambda shape: pl.BlockSpec(shape, lambda i, *_: (0,) * len(shape))
    out = jax.ShapeDtypeStruct((2, rows, w.shape[1]), F32)
    return pl.pallas_call(
        project_kernel,
        grid_spec=pltpu.PrefetchScalarGridSpec(
            num_scalar_prefetch=1,
            grid=(1,),
            in_specs=[whole(a.shape), whole(b.shape), whole(w.shape)],
            out_specs=[whole(out.shape), whole(out.shape)],
            scratch_shapes=[pltpu.VMEM((games, w.shape[1]), F32)],
        ),
        out_shape=[out, out],
        compiler_params=params(),
        cost_estimate=cost(3),
        name="project",
    )(mine, a, b, w)


def norm_kernel(mine_ref, keep_ref, got_ref, side_ref, res_ref, gain_ref, copies_ref, stream_ref):
    stream = res_ref[...].astype(F32) + ((keep_ref[0] + got_ref[0]) + side_ref[...])
    scale = lax.rsqrt(jnp.mean(stream * stream, axis=-1, keepdims=True) + 1e-06)
    normed = (stream * scale * (1.0 + gain_ref[...])).astype(BF)
    stream_ref[...] = stream
    for k in range(copies_ref.shape[0]):
        copies_ref[k] = normed


def norm(mine, keep, got, side, residual, gain, peers):
    _, rows, d = keep.shape
    whole = lambda shape: pl.BlockSpec(shape, lambda i, *_: (0,) * len(shape))
    outs = [
        jax.ShapeDtypeStruct((peers, rows, d), BF),
        jax.ShapeDtypeStruct((rows, d), F32),
    ]
    return pl.pallas_call(
        norm_kernel,
        grid_spec=pltpu.PrefetchScalarGridSpec(
            num_scalar_prefetch=1,
            grid=(1,),
            in_specs=[
                pl.BlockSpec((1, rows, d), lambda i, *_: (0, 0, 0)),
                pl.BlockSpec((1, rows, d), lambda i, *_: (0, 0, 0)),
                whole(side.shape),
                pl.BlockSpec((rows, d), lambda i, m: (m[0], 0)),
                whole(gain.shape),
            ],
            out_specs=[whole(o.shape) for o in outs],
        ),
        out_shape=outs,
        compiler_params=params(),
        cost_estimate=cost(2),
        name="norm",
    )(mine, keep, got, side, residual, gain)


def ffn_kernel(*refs):
    n = (len(refs) - 7) // 3
    x_ref = refs[0]
    w = [refs[1 + 3 * b : 4 + 3 * b] for b in range(n)]
    out_ref, x, gu, down, hid, sem_x, sem_w = refs[1 + 3 * n :]
    unit = gu.shape[2] // 2

    def copies(b):
        g, u, d = w[b]
        return (
            pltpu.make_async_copy(g, gu.at[b, :, pl.ds(0, unit)], sem_w.at[3 * b]),
            pltpu.make_async_copy(u, gu.at[b, :, pl.ds(unit, unit)], sem_w.at[3 * b + 1]),
            pltpu.make_async_copy(d, down.at[pl.ds(b * unit, unit), :], sem_w.at[3 * b + 2]),
        )

    load_x = pltpu.make_async_copy(x_ref, x, sem_x)
    load_x.start()
    for b in range(n):
        for c in copies(b):
            c.start()
    load_x.wait()
    for b in range(n):
        for c in copies(b)[:2]:
            c.wait()
        both = jnp.dot(x[...], gu[b], preferred_element_type=F32)
        gate = both[:, :unit]
        hid[:, b * unit : (b + 1) * unit] = (
            jax.nn.gelu(gate, approximate=True) * both[:, unit:]
        ).astype(BF)
    for b in range(n):
        copies(b)[2].wait()
    cols = 256

    @pl.loop(0, out_ref.shape[1] // cols)
    def _(k):
        at = pl.ds(pl.multiple_of(k * cols, cols), cols)
        out_ref[:, at] = jnp.dot(hid[...], down[:, at], preferred_element_type=F32).astype(BF)


def ffn(x, weights):
    n = len(weights)
    rows, d = x.shape
    unit = weights[0][0].shape[1]
    any_spec = pl.BlockSpec(memory_space=pl.ANY)
    return pl.pallas_call(
        ffn_kernel,
        in_specs=[any_spec] * (1 + 3 * n),
        out_specs=pl.BlockSpec(memory_space=pltpu.VMEM),
        out_shape=jax.ShapeDtypeStruct((rows, d), BF),
        scratch_shapes=[
            pltpu.VMEM((rows, d), BF),
            pltpu.VMEM((n, d, 2 * unit), BF),
            pltpu.VMEM((n * unit, d), BF),
            pltpu.VMEM((rows, n * unit), BF),
            pltpu.SemaphoreType.DMA,
            pltpu.SemaphoreType.DMA((3 * n,)),
        ],
        compiler_params=params(),
        cost_estimate=cost(8),
        name="ffn",
    )(x, *[a for block in weights for a in block])


def finish_kernel(parts_ref, stream_ref, out_ref):
    total = parts_ref[0].astype(F32)
    for k in range(1, parts_ref.shape[0]):
        total += parts_ref[k].astype(F32)
    out_ref[...] = (stream_ref[...] + total).astype(BF)


def finish(parts, stream):
    return pl.pallas_call(
        finish_kernel,
        out_shape=jax.ShapeDtypeStruct(stream.shape, BF),
        compiler_params=params(),
        cost_estimate=cost(2),
        name="finish",
    )(parts, stream)


def assemble_kernel(half_ref, mine_ref, peer_ref, out_ref):
    rows = mine_ref.shape[1]
    for ref, h in ((mine_ref, half_ref[0]), (peer_ref, 1 - half_ref[0])):
        out_ref[:, pl.ds(pl.multiple_of(h * rows, rows), rows), :] = ref[...]


def assemble(half, mine, peer):
    pages, rows, width = mine.shape
    block = 8
    spec = pl.BlockSpec((block, rows, width), lambda i, *_: (i, 0, 0))
    return pl.pallas_call(
        assemble_kernel,
        grid_spec=pltpu.PrefetchScalarGridSpec(
            num_scalar_prefetch=1,
            grid=(pages // block,),
            in_specs=[spec, spec],
            out_specs=pl.BlockSpec((block, 2 * rows, width), lambda i, *_: (i, 0, 0)),
        ),
        out_shape=jax.ShapeDtypeStruct((pages, 2 * rows, width), mine.dtype),
        compiler_params=params(),
        cost_estimate=cost(6),
        name="assemble",
    )(half, mine, peer)


def local(
    page_pool, move_count, send_slots, page_table, history_len, queries, new_entry, residual,
    out_proj, ffn_gain, gate_proj, up_proj, down_proj,
):
    axes = ("dp", "mp")
    n_dp, n_mp = lax.axis_size("dp"), lax.axis_size("mp")
    devices = n_dp * n_mp
    games, heads, hd = queries.shape
    page_len, width = page_pool.shape[1:]
    mine = lax.axis_index("mp").reshape(1)
    half = mine % 2
    swap = lambda bit: [(k, k ^ bit) for k in range(devices)]
    core, side, across = swap(1), swap(2), swap(8)
    send = lambda a, pairs: lax.ppermute(a, axes, pairs)

    out_pages = outgoing_pages(half, send_slots.reshape(-1), move_count.reshape(-1), page_pool)
    got = lax.all_to_all(
        out_pages.reshape(n_dp, -1, page_len // 2, width), "dp", 0, 0, tiled=True
    ).reshape(out_pages.shape)

    q_mine = (queries.transpose(1, 0, 2) * jnp.asarray(hd**-0.5, BF)).reshape(heads * games, hd)
    q_peer = send(q_mine, core)
    copies = 2 * heads
    table = jnp.tile(page_table.T, (1, copies))
    lengths = jnp.tile(history_len[None, :], (1, copies))

    weights = (gate_proj, up_proj, down_proj)
    w_core = tuple(send(a, core) for a in weights)
    late, got = lax.optimization_barrier((weights, got))
    w_far = tuple(send(a, across) for a in late)
    w_far_core = tuple(send(a, core) for a in w_far)

    keep, give = attend(half, q_mine, q_peer, new_entry, table, lengths, page_pool, got)
    other = send(give, core)
    got_peer = send(got, core)
    hold, pass_on = project(mine, keep, other, out_proj, games)
    hold_got = send(pass_on, core)
    side_got = send(hold[1] + hold_got[1], side)
    arrived = assemble(half, got, got_peer)

    groups = [
        [k for k in range(devices) if k % 2 == c and (k >> 3) % 2 == x]
        for x in range(2)
        for c in range(2)
    ]
    peers = len(groups[0])
    spread, stream = norm(
        mine, hold, hold_got, side_got, residual, ffn_gain.reshape(1, -1), peers
    )
    rows, d = stream.shape
    x = lax.all_to_all(spread, axes, 0, 0, tiled=True, axis_index_groups=groups)
    parts = ffn(x.reshape(peers * rows, d), [weights, w_core, w_far, w_far_core])
    back = lax.all_to_all(
        parts.reshape(peers, rows, d), axes, 0, 0, tiled=True, axis_index_groups=groups
    )
    quarter = finish(back, stream)
    layer_out = lax.all_gather(quarter, "mp", axis=0, tiled=True)
    return arrived, layer_out


def solution(mesh):
    in_specs = (
        P("dp", None, None),
        P("dp", None),
        P("dp", None),
        P("dp", None),
        P("dp"),
        P("dp", "mp", None),
        P("dp", None),
        P("dp", None),
        P("mp", None),
        P(),
        P(None, ("dp", "mp")),
        P(None, ("dp", "mp")),
        P(("dp", "mp"), None),
    )
    out_specs = (P("dp", None, None), P("dp", None))
    return jax.shard_map(local, mesh=mesh, in_specs=in_specs, out_specs=out_specs, check_vma=False)
```

time: 681 us -> 247 us (0.36)
  blocking collectives: 143 us -> 7.41 us
  local copies, waits for them, and re-layouts: 135 us -> 8.85 us
  waiting for transfers between devices: 244 us -> 128 us
  matrix products: 110 us -> 0 us
  Pallas kernels: 0 us -> 52.2 us
  starting transfers between devices: 4.55 us -> 46.7 us
  other arithmetic: 27.9 us -> 1.07 us
  between operations: 13.9 us -> 0.85 us
    all_gather x2 -> x0, waiting for transfers between devices: 184 us -> none  [the longest x1 105 us: local(): piece = lax.all_gather(normed, 'dp', axis=0, tiled=True)]
    all_to_all x2 -> x0, blocking collectives: 143 us -> none  [the longest x1 102 us: sum_at_owner(): lax.all_to_all(tiles, axis, split_axis=0, concat_axis=0, tiled=True)]
    gather x9 -> x0, local copies, waits for them, and re-layouts: 116 us -> none  [the longest x8 113 us: one_block(): every_page[table_blk].reshape(block, table_len * page_len, width)]
    dot_general x27 -> x0, matrix products: 110 us -> none  [the longest x8 46 us: attend_block(): jnp.einsum('bhd,btd->bht', query_blk, keys, preferred_element_type=jnp.fl...]
    all_to_all x1 -> x3, waiting for transfers between devices: 23.6 us -> 77.8 us  [the longest x1 58.3 us: local(): lax.all_to_all(out_pages.reshape(n_dp, -1, page_len // 2, width), 'dp', 0...]
    pallas_call x0 -> x7, Pallas kernels: none -> 52.2 us  [the longest x1 17.3 us: attend(): pl.pallas_call(attend_kernel, grid_spec=pltpu.PrefetchScalarGridSpec(num_...]
    ppermute x0 -> x14, waiting for transfers between devices: none -> 50.6 us  [local(): send = lambda a, pairs: lax.ppermute(a, axes, pairs)]
    psum x1 -> x0, waiting for transfers between devices: 36 us -> none  [local(): mixed = lax.psum(partial_out, 'mp')]
  transfers between devices with their start and end apart: 4 -> 17, of which waited for: 4 -> 9; matrix products, arithmetic and copies ran while one was open for 0% -> 1% of each run, Pallas kernels for 0% -> 10%
where the time goes in v1:
time: 247 us; the launch traced here: 245 us
  waiting for transfers between devices  128 us (52%)
  Pallas kernels  52.2 us (21%)
  starting transfers between devices  46.7 us (19%)
  local copies, waits for them, and re-layouts  8.85 us (4%)
  blocking collectives  7.41 us (3%)
    all_to_all x1, waiting for transfers between devices, local(): lax.all_to_all(out_pages.reshape(n_dp, -1, page_len // 2, width), 'dp', 0...  58.3 us
    ppermute x14, waiting for transfers between devices, local(): send = lambda a, pairs: lax.ppermute(a, axes, pairs)  50.6 us
    ppermute x14, starting transfers between devices, local(): send = lambda a, pairs: lax.ppermute(a, axes, pairs)  20.4 us
    all_to_all x1, waiting for transfers between devices, local(): lax.all_to_all(parts.reshape(peers, rows, d), axes, 0, 0, tiled=True, axi...  19.5 us
    pallas_call x1, Pallas kernels, attend(): pl.pallas_call(attend_kernel, grid_spec=pltpu.PrefetchScalarGridSpec(num_...  17.3 us
    pallas_call x1, Pallas kernels, ffn(): pl.pallas_call(ffn_kernel, in_specs=[any_spec] * (1 + 3 * n), out_specs=p...  12.3 us
    all_to_all x1, starting transfers between devices, local(): lax.all_to_all(out_pages.reshape(n_dp, -1, page_len // 2, width), 'dp', 0...  11.5 us
    all_to_all x1, starting transfers between devices, local(): lax.all_to_all(parts.reshape(peers, rows, d), axes, 0, 0, tiled=True, axi...  10.8 us
  transfers between devices with their start and end apart: 17, of which 9 were waited for; matrix products, arithmetic and copies ran while one was open for 1% of the time, Pallas kernels for 10%

profile of v1, /device:TPU:1, one launch (start us, length us, event | category | flops | bytes accessed | tf_op | source)
XLA Modules:
  0.0 245.5 jit_solution(16799004873965814395)
XLA Ops:
  2.0 5.5 %outgoing.1 = bf16[64,64,512]{2,1,0:T(8,128)(2,1)} custom-call(s32[1]{0:T(128)S(6)} %select_n.7.half_ref, s32[64]{0:T(128)} %reshape.45.slot_ref, s32[32]{0:T(128)} %bitcast.19, bf16[64,128,512]{2,1,0:T(8,128)(2,1)} %pool_ref.3), custom_call_target="tpu_custom_call" | custom-call | flops 1200000000 | bytes 6000000 | tf_op jit(solution)/shard_map/outgoing/pallas_call | solution.py:44
  7.5 11.5 %all-to-all-start = ((bf16[32,2,64,512]{3,2,1,0:T(8,128)(2,1)}), bf16[32,2,64,512]{3,2,1,0:T(8,128)(2,1)}, u32[]{:S(2)}, u32[]{:S(2)}) async-start(bf16[32,2,64,512]{3,2,1,0:T(8,128)(2,1)} %bitcast.13), calls=%async_computation | async-start | bytes 8388608 | tf_op jit(solution)/shard_map/all_to_all | solution.py:392
  21.6 58.3 %all-to-all-done = bf16[32,2,64,512]{3,2,1,0:T(8,128)(2,1)} async-done(((bf16[32,2,64,512]{3,2,1,0:T(8,128)(2,1)}), bf16[32,2,64,512]{3,2,1,0:T(8,128)(2,1)}, u32[]{:S(2)}, u32[]{:S(2)}) %all-to-all-start) | async-done | bytes 4194336 | tf_op jit(solution)/shard_map/all_to_all | solution.py:392
  80.5 17.3 %attend.1 = (f32[264,128]{1,0:T(8,128)}, f32[264,128]{1,0:T(8,128)}) custom-call(s32[1]{0:T(128)S(6)} %select_n.7.half_ref, bf16[128,256]{1,0:T(8,128)(2,1)} %bitcast.17, bf16[128,256]{1,0:T(8,128)(2,1)} %copy-done.5, bf16[64,512]{1,0:T(8,128)(2,1)} %entry_ref.1, s32[16,256]{1,0:T(8,128)} %tile.18.tab_ref, s32[1,256]{1,0:T(1,128)} %tile.20.len_ref, ...), custom_call_target="tpu_custom_call" | custom-call | flops 3200000000 | bytes 16000000 | tf_op jit(solution)/shard_map/attend/pallas_call | solution.py:154
  97.8 1.8 collective-permute-start.2
  101.4 3.1 %project.1 = (f32[2,16,2048]{2,1,0:T(8,128)}, f32[2,16,2048]{2,1,0:T(8,128)}) custom-call(s32[1]{0:T(128)} %bitcast.mine_ref, f32[264,128]{1,0:T(8,128)} %get-tuple-element.13.a_ref, f32[264,128]{1,0:T(8,128)} %copy-done.18, bf16[512,2048]{1,0:T(8,128)(2,1)} %w_ref.1), custom_call_target="tpu_custom_call" | custom-call | flops 1200000000 | bytes 6000000 | tf_op jit(solution)/shard_map/project/pallas_call | solution.py:218
  104.9 1.4 collective-permute-done.3.got_ref
  108.8 3.3 %collective-permute-done.4.side_ref = f32[16,2048]{1,0:T(8,128)S(1)} collective-permute-done((f32[16,2048]{1,0:T(8,128)S(1)}, f32[16,2048]{1,0:T(8,128)S(1)}, u32[]{:S(2)}, u32[]{:S(2)}) %collective-permute-start.4) | collective-permute-done | bytes 131104 | tf_op jit(solution)/shard_map/ppermute | solution.py:389
  112.7 2.6 %norm.1 = (bf16[32,16,2048]{2,1,0:T(8,128)(2,1)}, f32[16,2048]{1,0:T(8,128)}) custom-call(s32[1]{0:T(128)} %bitcast.mine_ref, f32[2,16,2048]{2,1,0:T(8,128)} %get-tuple-element.15.keep_ref, f32[2,16,2048]{2,1,0:T(8,128)} %copy-done.3, f32[16,2048]{1,0:T(8,128)} %copy-done.19, bf16[64,2048]{1,0:T(8,128)(2,1)} %res_ref.1, f32[1,2048]{1,0:T(1,128)} %bitcast.20), custom_call_target="tpu_custom_call" | custom-call | flops 800000000 | bytes 4000000 | tf_op jit(solution)/shard_map/norm/pallas_call | solution.py:250
  115.4 4.0 %all-to-all-start.1 = ((bf16[32,16,2048]{2,1,0:T(8,128)(2,1)}), bf16[32,16,2048]{2,1,0:T(8,128)(2,1)S(1)}, u32[]{:S(2)}, u32[]{:S(2)}) async-start(bf16[32,16,2048]{2,1,0:T(8,128)(2,1)} %get-tuple-element.17), calls=%async_computation.1 | async-start | bytes 4194304 | tf_op jit(solution)/shard_map/all_to_all | solution.py:426
  120.8 2.0 collective-permute-start.8
  122.9 1.4 collective-permute-start.10
  125.6 28.8 %collective-permute-done.8.refs_7_ = bf16[2048,128]{1,0:T(8,128)(2,1)S(1)} collective-permute-done((bf16[2048,128]{1,0:T(8,128)(2,1)S(1)}, bf16[2048,128]{1,0:T(8,128)(2,1)S(1)}, u32[]{:S(2)}, u32[]{:S(2)}) %collective-permute-start.8) | collective-permute-done | bytes 524320 | tf_op jit(solution)/shard_map/ppermute | solution.py:389
  154.4 3.7 %collective-permute-start.11 = (bf16[2048,128]{1,0:T(8,128)(2,1)S(1)}, bf16[2048,128]{1,0:T(8,128)(2,1)S(1)}, u32[]{:S(2)}, u32[]{:S(2)}) collective-permute-start(bf16[2048,128]{1,0:T(8,128)(2,1)S(1)} %collective-permute-done.8.refs_7_), channel_id=1, source_target_pairs={{0,1},{1,0},{2,3},{3,2},{4,5},{5,4},{6,7},{7,6},{8,9},{9,8},{10,11... | collective-permute-start | bytes 1572872 | tf_op jit(solution)/shard_map/ppermute | solution.py:389
  158.1 7.5 %collective-permute-done.9.refs_8_ = bf16[2048,128]{1,0:T(8,128)(2,1)S(1)} collective-permute-done((bf16[2048,128]{1,0:T(8,128)(2,1)S(1)}, bf16[2048,128]{1,0:T(8,128)(2,1)S(1)}, u32[]{:S(2)}, u32[]{:S(2)}) %collective-permute-start.9) | collective-permute-done | bytes 524320 | tf_op jit(solution)/shard_map/ppermute | solution.py:389
  165.6 3.7 %collective-permute-start.12 = (bf16[2048,128]{1,0:T(8,128)(2,1)S(1)}, bf16[2048,128]{1,0:T(8,128)(2,1)S(1)}, u32[]{:S(2)}, u32[]{:S(2)}) collective-permute-start(bf16[2048,128]{1,0:T(8,128)(2,1)S(1)} %collective-permute-done.9.refs_8_), channel_id=1, source_target_pairs={{0,1},{1,0},{2,3},{3,2},{4,5},{5,4},{6,7},{7,6},{8,9},{9,8},{10,11... | collective-permute-start | bytes 1572872 | tf_op jit(solution)/shard_map/ppermute | solution.py:389
  169.4 7.5 %collective-permute-done.10.refs_9_ = bf16[128,2048]{1,0:T(8,128)(2,1)S(1)} collective-permute-done((bf16[128,2048]{1,0:T(8,128)(2,1)}, bf16[128,2048]{1,0:T(8,128)(2,1)S(1)}, u32[]{:S(2)}, u32[]{:S(2)}) %collective-permute-start.10) | collective-permute-done | bytes 524320 | tf_op jit(solution)/shard_map/ppermute | solution.py:389
  176.9 2.1 collective-permute-start.13
  181.9 12.3 %ffn.1 = bf16[512,2048]{1,0:T(8,128)(2,1)} custom-call(bf16[512,2048]{1,0:T(8,128)(2,1)} %bitcast.14, bf16[2048,128]{1,0:T(8,128)(2,1)} %refs_1_.1, bf16[2048,128]{1,0:T(8,128)(2,1)} %refs_2_.1, bf16[128,2048]{1,0:T(8,128)(2,1)} %refs_3_.1, bf16[2048,128]{1,0:T(8,128)(2,1)} %copy-done.10, bf16[2048,128]{1,0:T(8,128)(2,1)} %copy-done.11, ...), custom_call_target="tpu_custom_call" | custom-call | flops 3200000000 | bytes 16000000 | tf_op jit(solution)/shard_map/ffn/pallas_call | solution.py:315
  194.2 10.8 %all-to-all-start.2 = ((bf16[32,16,2048]{2,1,0:T(8,128)(2,1)}), bf16[32,16,2048]{2,1,0:T(8,128)(2,1)S(1)}, u32[]{:S(2)}, u32[]{:S(2)}) async-start(bf16[32,16,2048]{2,1,0:T(8,128)(2,1)} %bitcast.15), calls=%async_computation.2 | async-start | bytes 4194304 | tf_op jit(solution)/shard_map/all_to_all | solution.py:428
  205.1 8.9 %assemble.1 = bf16[64,128,512]{2,1,0:T(8,128)(2,1)} custom-call(s32[1]{0:T(128)S(6)} %select_n.7.half_ref, bf16[64,64,512]{2,1,0:T(8,128)(2,1)} %bitcast.3.mine_ref.got_ref, bf16[64,64,512]{2,1,0:T(8,128)(2,1)} %collective-permute-done.peer_ref), custom_call_target="tpu_custom_call" | custom-call | flops 2400000000 | bytes 12000000 | tf_op jit(solution)/shard_map/assemble/pallas_call | solution.py:361
  213.9 19.5 %all-to-all-done.2.parts_ref = bf16[32,16,2048]{2,1,0:T(8,128)(2,1)S(1)} async-done(((bf16[32,16,2048]{2,1,0:T(8,128)(2,1)}), bf16[32,16,2048]{2,1,0:T(8,128)(2,1)S(1)}, u32[]{:S(2)}, u32[]{:S(2)}) %all-to-all-start.2) | async-done | bytes 2097184 | tf_op jit(solution)/shard_map/all_to_all | solution.py:428
  234.8 2.5 %finish.1 = bf16[16,2048]{1,0:T(8,128)(2,1)} custom-call(bf16[32,16,2048]{2,1,0:T(8,128)(2,1)} %copy-done.1, f32[16,2048]{1,0:T(8,128)} %get-tuple-element.21.stream_ref), custom_call_target="tpu_custom_call" | custom-call | flops 800000000 | bytes 4000000 | tf_op jit(solution)/shard_map/finish/pallas_call | solution.py:342
  237.4 7.4 %all_gather.3 = bf16[64,2048]{1,0:T(8,128)(2,1)S(1)} all-gather(bf16[16,2048]{1,0:T(8,128)(2,1)} %finish.1), channel_id=1, replica_groups=mesh['dp'=32,'mp'=4] {'mp'}, dimensions={0}, use_global_device_ids=true | all-gather | bytes 327680 | tf_op jit(solution)/shard_map/all_gather | solution.py:432
  (68 shorter events, 17.5 us)
Async XLA Ops:
  7.5 72.3 %all-to-all-start = ((bf16[32,2,64,512]{3,2,1,0:T(8,128)(2,1)}), bf16[32,2,64,512]{3,2,1,0:T(8,128)(2,1)}, u32[]{:S(2)}, u32[]{:S(2)}) async-start(bf16[32,2,64,512]{3,2,1,0:T(8,128)(2,1)} %bitcast.13), calls=%async_computation | async-start | bytes 8388608 | tf_op jit(solution)/shard_map/all_to_all | solution.py:392
  19.1 60.7 %copy-start.2 = (bf16[2,64,256]{2,1,0:T(8,128)(2,1)}, bf16[2,64,256]{2,1,0:T(8,128)(2,1)S(1)}, u32[]{:S(2)}) copy-start(bf16[2,64,256]{2,1,0:T(8,128)(2,1)S(1)} %copy.18) | copy-start | bytes 196612
  19.1 60.7 %collective-permute-start.1 = (bf16[128,256]{1,0:T(8,128)(2,1)S(1)}, bf16[128,256]{1,0:T(8,128)(2,1)S(1)}, u32[]{:S(2)}, u32[]{:S(2)}) collective-permute-start(bf16[128,256]{1,0:T(8,128)(2,1)S(1)} %bitcast.16), channel_id=1, source_target_pairs={{0,1},{1,0},{2,3},{3,2},{4,5},{5,4},{6,7},{7,6},{8,9},{9,8},{10,11... | collective-permute-start | bytes 196616 | tf_op jit(solution)/shard_map/ppermute | solution.py:389
  97.8 3.0 %collective-permute-start.2 = (f32[264,128]{1,0:T(8,128)}, f32[264,128]{1,0:T(8,128)S(1)}, u32[]{:S(2)}, u32[]{:S(2)}) collective-permute-start(f32[264,128]{1,0:T(8,128)} %get-tuple-element.14), channel_id=1, source_target_pairs={{0,1},{1,0},{2,3},{3,2},{4,5},{5,4},{6,7},{7,6},{8,9},{9,8},{10,11... | collective-permute-start | bytes 405512 | tf_op jit(solution)/shard_map/ppermute | solution.py:389
  104.5 14.9 %copy-start.8 = (bf16[2048,128]{1,0:T(8,128)(2,1)S(1)}, bf16[2048,128]{1,0:T(8,128)(2,1)}, u32[]{:S(2)}) copy-start(bf16[2048,128]{1,0:T(8,128)(2,1)} %refs_1_.1) | copy-start | bytes 1572868
  104.5 16.2 %copy-start.9 = (bf16[2048,128]{1,0:T(8,128)(2,1)S(1)}, bf16[2048,128]{1,0:T(8,128)(2,1)}, u32[]{:S(2)}) copy-start(bf16[2048,128]{1,0:T(8,128)(2,1)} %refs_2_.1) | copy-start | bytes 1572868
  104.5 1.7 collective-permute-start.3
  107.3 4.8 %collective-permute-start.4 = (f32[16,2048]{1,0:T(8,128)S(1)}, f32[16,2048]{1,0:T(8,128)S(1)}, u32[]{:S(2)}, u32[]{:S(2)}) collective-permute-start(f32[16,2048]{1,0:T(8,128)S(1)} %fusion), channel_id=1, source_target_pairs={{0,2},{1,3},{2,0},{3,1},{4,6},{5,7},{6,4},{7,5},{8,10},{9,11},{10,... | collective-permute-start | bytes 393224 | tf_op jit(solution)/shard_map/ppermute | solution.py:389
  108.1 96.9 %collective-permute-start = (bf16[64,64,512]{2,1,0:T(8,128)(2,1)}, bf16[64,64,512]{2,1,0:T(8,128)(2,1)}, u32[]{:S(2)}, u32[]{:S(2)}) collective-permute-start(bf16[64,64,512]{2,1,0:T(8,128)(2,1)} %bitcast.3.mine_ref.got_ref), channel_id=1, source_target_pairs={{0,1},{1,0},{2,3},{3,2},{4,5},{5,4},{6,7},{7,6},{8,9},{9,8},{10,11... | collective-permute-start | bytes 12582920 | tf_op jit(solution)/shard_map/ppermute | solution.py:389
  115.4 65.2 %all-to-all-start.1 = ((bf16[32,16,2048]{2,1,0:T(8,128)(2,1)}), bf16[32,16,2048]{2,1,0:T(8,128)(2,1)S(1)}, u32[]{:S(2)}, u32[]{:S(2)}) async-start(bf16[32,16,2048]{2,1,0:T(8,128)(2,1)} %get-tuple-element.17), calls=%async_computation.1 | async-start | bytes 4194304 | tf_op jit(solution)/shard_map/all_to_all | solution.py:426
  119.4 3.5 %collective-permute-start.5 = (bf16[2048,128]{1,0:T(8,128)(2,1)S(1)}, bf16[2048,128]{1,0:T(8,128)(2,1)S(1)}, u32[]{:S(2)}, u32[]{:S(2)}) collective-permute-start(bf16[2048,128]{1,0:T(8,128)(2,1)S(1)} %copy-done.8), channel_id=1, source_target_pairs={{0,1},{1,0},{2,3},{3,2},{4,5},{5,4},{6,7},{7,6},{8,9},{9,8},{10,11... | collective-permute-start | bytes 1572872 | tf_op jit(solution)/shard_map/ppermute | solution.py:389
  120.7 3.6 %collective-permute-start.6 = (bf16[2048,128]{1,0:T(8,128)(2,1)S(1)}, bf16[2048,128]{1,0:T(8,128)(2,1)S(1)}, u32[]{:S(2)}, u32[]{:S(2)}) collective-permute-start(bf16[2048,128]{1,0:T(8,128)(2,1)S(1)} %copy-done.9), channel_id=1, source_target_pairs={{0,1},{1,0},{2,3},{3,2},{4,5},{5,4},{6,7},{7,6},{8,9},{9,8},{10,11... | collective-permute-start | bytes 1572872 | tf_op jit(solution)/shard_map/ppermute | solution.py:389
  120.8 33.6 %collective-permute-start.8 = (bf16[2048,128]{1,0:T(8,128)(2,1)S(1)}, bf16[2048,128]{1,0:T(8,128)(2,1)S(1)}, u32[]{:S(2)}, u32[]{:S(2)}) collective-permute-start(bf16[2048,128]{1,0:T(8,128)(2,1)S(1)} %copy-done.8), channel_id=1, source_target_pairs={{0,8},{1,9},{2,10},{3,11},{4,12},{5,13},{6,14},{7,15},{8,0},{9,1},... | collective-permute-start | bytes 1572872 | tf_op jit(solution)/shard_map/ppermute | solution.py:389
  122.9 42.8 %collective-permute-start.9 = (bf16[2048,128]{1,0:T(8,128)(2,1)S(1)}, bf16[2048,128]{1,0:T(8,128)(2,1)S(1)}, u32[]{:S(2)}, u32[]{:S(2)}) collective-permute-start(bf16[2048,128]{1,0:T(8,128)(2,1)S(1)} %copy-done.9), channel_id=1, source_target_pairs={{0,8},{1,9},{2,10},{3,11},{4,12},{5,13},{6,14},{7,15},{8,0},{9,1},... | collective-permute-start | bytes 1572872 | tf_op jit(solution)/shard_map/ppermute | solution.py:389
  122.9 56.1 %copy-start.10 = (bf16[2048,128]{1,0:T(8,128)(2,1)}, bf16[2048,128]{1,0:T(8,128)(2,1)S(1)}, u32[]{:S(2)}) copy-start(bf16[2048,128]{1,0:T(8,128)(2,1)S(1)} %collective-permute-done.5.refs_4_) | copy-start | bytes 1572868
  122.9 54.0 %collective-permute-start.10 = (bf16[128,2048]{1,0:T(8,128)(2,1)}, bf16[128,2048]{1,0:T(8,128)(2,1)S(1)}, u32[]{:S(2)}, u32[]{:S(2)}) collective-permute-start(bf16[128,2048]{1,0:T(8,128)(2,1)} %refs_3_.1), channel_id=1, source_target_pairs={{0,8},{1,9},{2,10},{3,11},{4,12},{5,13},{6,14},{7,15},{8,0},{9,1},... | collective-permute-start | bytes 1572872 | tf_op jit(solution)/shard_map/ppermute | solution.py:389
  124.3 54.7 %copy-start.11 = (bf16[2048,128]{1,0:T(8,128)(2,1)}, bf16[2048,128]{1,0:T(8,128)(2,1)S(1)}, u32[]{:S(2)}) copy-start(bf16[2048,128]{1,0:T(8,128)(2,1)S(1)} %collective-permute-done.6.refs_5_) | copy-start | bytes 1572868
  124.3 54.6 %collective-permute-start.7 = (bf16[128,2048]{1,0:T(8,128)(2,1)}, bf16[128,2048]{1,0:T(8,128)(2,1)S(1)}, u32[]{:S(2)}, u32[]{:S(2)}) collective-permute-start(bf16[128,2048]{1,0:T(8,128)(2,1)} %refs_3_.1), channel_id=1, source_target_pairs={{0,1},{1,0},{2,3},{3,2},{4,5},{5,4},{6,7},{7,6},{8,9},{9,8},{10,11... | collective-permute-start | bytes 1572872 | tf_op jit(solution)/shard_map/ppermute | solution.py:389
  154.4 24.6 %copy-start.12 = (bf16[2048,128]{1,0:T(8,128)(2,1)}, bf16[2048,128]{1,0:T(8,128)(2,1)S(1)}, u32[]{:S(2)}) copy-start(bf16[2048,128]{1,0:T(8,128)(2,1)S(1)} %collective-permute-done.8.refs_7_) | copy-start | bytes 1572868
  154.4 24.6 %collective-permute-start.11 = (bf16[2048,128]{1,0:T(8,128)(2,1)S(1)}, bf16[2048,128]{1,0:T(8,128)(2,1)S(1)}, u32[]{:S(2)}, u32[]{:S(2)}) collective-permute-start(bf16[2048,128]{1,0:T(8,128)(2,1)S(1)} %collective-permute-done.8.refs_7_), channel_id=1, source_target_pairs={{0,1},{1,0},{2,3},{3,2},{4,5},{5,4},{6,7},{7,6},{8,9},{9,8},{10,11... | collective-permute-start | bytes 1572872 | tf_op jit(solution)/shard_map/ppermute | solution.py:389
  165.6 13.4 %copy-start.13 = (bf16[2048,128]{1,0:T(8,128)(2,1)}, bf16[2048,128]{1,0:T(8,128)(2,1)S(1)}, u32[]{:S(2)}) copy-start(bf16[2048,128]{1,0:T(8,128)(2,1)S(1)} %collective-permute-done.9.refs_8_) | copy-start | bytes 1572868
  165.6 13.3 %collective-permute-start.12 = (bf16[2048,128]{1,0:T(8,128)(2,1)S(1)}, bf16[2048,128]{1,0:T(8,128)(2,1)S(1)}, u32[]{:S(2)}, u32[]{:S(2)}) collective-permute-start(bf16[2048,128]{1,0:T(8,128)(2,1)S(1)} %collective-permute-done.9.refs_8_), channel_id=1, source_target_pairs={{0,1},{1,0},{2,3},{3,2},{4,5},{5,4},{6,7},{7,6},{8,9},{9,8},{10,11... | collective-permute-start | bytes 1572872 | tf_op jit(solution)/shard_map/ppermute | solution.py:389
  176.9 3.7 %collective-permute-start.13 = (bf16[128,2048]{1,0:T(8,128)(2,1)S(1)}, bf16[128,2048]{1,0:T(8,128)(2,1)}, u32[]{:S(2)}, u32[]{:S(2)}) collective-permute-start(bf16[128,2048]{1,0:T(8,128)(2,1)S(1)} %collective-permute-done.10.refs_9_), channel_id=1, source_target_pairs={{0,1},{1,0},{2,3},{3,2},{4,5},{5,4},{6,7},{7,6},{8,9},{9,8},{10,11... | collective-permute-start | bytes 1572872 | tf_op jit(solution)/shard_map/ppermute | solution.py:389
  194.2 39.3 %all-to-all-start.2 = ((bf16[32,16,2048]{2,1,0:T(8,128)(2,1)}), bf16[32,16,2048]{2,1,0:T(8,128)(2,1)S(1)}, u32[]{:S(2)}, u32[]{:S(2)}) async-start(bf16[32,16,2048]{2,1,0:T(8,128)(2,1)} %bitcast.15), calls=%async_computation.2 | async-start | bytes 4194304 | tf_op jit(solution)/shard_map/all_to_all | solution.py:428
  (13 other events, 53.5 us)

commit v2 on v1

v2 whole, which is shorter than its diff:
```python
import jax
import jax.numpy as jnp
from jax import lax
from jax.experimental import pallas as pl
from jax.experimental.pallas import tpu as pltpu
from jax.sharding import PartitionSpec as P


NEG = -1e30
BF = jnp.bfloat16
F32 = jnp.float32
VLIM = 60 * 1024 * 1024


def params(**kw):
    return pltpu.CompilerParams(vmem_limit_bytes=VLIM, **kw)


def cost(us):
    return pl.CostEstimate(flops=int(us * 4e8), bytes_accessed=int(us * 2e6), transcendentals=0)


def outgoing_kernel(half_ref, slot_ref, count_ref, pool_ref, out_ref, sems):
    pages, rows, _ = out_ref.shape
    caps = pages // count_ref.shape[0]
    first = pl.multiple_of(half_ref[0] * rows, rows)

    def copy(i):
        src = pool_ref.at[slot_ref[i], pl.ds(first, rows), :]
        return pltpu.make_async_copy(src, out_ref.at[i], sems.at[i])

    copies = [copy(i) for i in range(pages)]
    for c in copies:
        c.start()
    for i, c in enumerate(copies):
        c.wait()

        @pl.when(i % caps >= count_ref[i // caps])
        def _():
            out_ref[i] = jnp.zeros(out_ref.shape[1:], out_ref.dtype)


def outgoing_pages(half, slots, counts, pool):
    pages = slots.shape[0]
    rows = pool.shape[1] // 2
    return pl.pallas_call(
        outgoing_kernel,
        grid_spec=pltpu.PrefetchScalarGridSpec(
            num_scalar_prefetch=3,
            grid=(1,),
            in_specs=[pl.BlockSpec(memory_space=pl.ANY)],
            out_specs=pl.BlockSpec((pages, rows, pool.shape[2]), lambda i, *_: (0, 0, 0)),
            scratch_shapes=[pltpu.SemaphoreType.DMA((pages,))],
        ),
        out_shape=jax.ShapeDtypeStruct((pages, rows, pool.shape[2]), pool.dtype),
        compiler_params=params(),
        cost_estimate=cost(3),
        name="outgoing",
    )(half, slots, counts, pool)


def chunk_step(block, base, qt, full, part, acc, stat):
    pages, rows, width = block.shape
    hd = width // 2
    lanes = qt.shape[1]
    keys = block[:, :, :hd].reshape(pages * rows, hd)
    values = block[:, :, hd:].reshape(pages * rows, hd)
    s = jnp.dot(keys, qt[...], preferred_element_type=F32)
    spot = lax.broadcasted_iota(jnp.int32, (rows, lanes), 0)
    old = stat[0:1, :]
    tops = jnp.full((8, lanes), NEG, F32)
    counts = []
    masked = []
    for j in range(pages):
        c = full[pl.ds(base + j, 1), :] + jnp.where(
            spot < part[pl.ds(base + j, 1), :], 1.0, 0.0
        )
        sj = jnp.where(c > 0.0, s[j * rows : (j + 1) * rows, :], NEG)
        tops = jnp.maximum(tops, jnp.max(sj.reshape(rows // 8, 8, lanes), axis=0))
        counts.append(c)
        masked.append(sj)
    top = jnp.maximum(old, jnp.max(tops, axis=0, keepdims=True))
    shrink = jnp.exp(old - top)
    sums = jnp.zeros((8, lanes), F32)
    probs = []
    for j in range(pages):
        p = jnp.exp(masked[j] - top) * counts[j]
        sums += jnp.sum(p.reshape(rows // 8, 8, lanes), axis=0)
        probs.append(p.astype(BF))
    p = jnp.concatenate(probs, axis=0)
    stat[0:1, :] = top
    stat[1:2, :] = stat[1:2, :] * shrink + jnp.sum(sums, axis=0, keepdims=True)
    acc[...] = acc[...] * shrink + lax.dot_general(
        values, p, (((0,), (0,)), ((), ())), preferred_element_type=F32
    )


def tables(first, half, rows, tab_ref, len_ref, full, part):
    entries, lanes = full.shape
    page_id = lax.broadcasted_iota(jnp.int32, (entries, lanes), 0) + first
    whole = jnp.zeros((entries, lanes), F32)
    rest = jnp.zeros((entries, lanes), jnp.int32)
    for j in range(tab_ref.shape[0]):
        hit = page_id == tab_ref[j : j + 1, :]
        kept = len_ref[...] - j * 2 * rows
        whole += jnp.where(hit & (kept >= 2 * rows), 1.0, 0.0)
        rest += jnp.where(hit & (kept > 0) & (kept < 2 * rows), kept, 0)
    full[...] = whole
    part[...] = rest - half * rows


def resident_kernel(
    half_ref, qa_ref, qb_ref, entry_ref, tab_ref, len_ref, pool_ref,
    acc_ref, stat_ref, qt_ref, full, part,
):
    i = pl.program_id(0)
    pages, rows, width = pool_ref.shape
    hd = width // 2
    mine = qa_ref.shape[0]
    games = entry_ref.shape[0]

    @pl.when(i == 0)
    def _():
        q = jnp.concatenate([qa_ref[...], qb_ref[...]], axis=0)
        qt_ref[...] = q.T
        tables(0, half_ref[0], rows, tab_ref, len_ref, full, part)
        s = jnp.dot(entry_ref[:, :hd], qt_ref[...], preferred_element_type=F32)
        game = lax.broadcasted_iota(jnp.int32, s.shape, 0)
        lane = lax.broadcasted_iota(jnp.int32, s.shape, 1)
        own = (lane < mine) & (lax.rem(lane, games) == game)
        p = jnp.where(own, 1.0, 0.0)
        stat_ref[...] = jnp.zeros(stat_ref.shape, F32)
        stat_ref[0:1, :] = jnp.max(jnp.where(own, s, NEG), axis=0, keepdims=True)
        stat_ref[1:2, :] = jnp.sum(p, axis=0, keepdims=True)
        acc_ref[...] = lax.dot_general(
            entry_ref[:, hd:], p.astype(BF), (((0,), (0,)), ((), ())), preferred_element_type=F32
        )

    chunk_step(pool_ref, i * pages, qt_ref, full, part, acc_ref, stat_ref)


def resident(half, q_mine, q_peer, entry, table, lengths, pool):
    slots, page_len, width = pool.shape
    rows = page_len // 2
    mine, hd = q_mine.shape
    lanes = 2 * mine
    block = 16
    whole = lambda shape: pl.BlockSpec(shape, lambda i, *_: (0,) * len(shape))
    outs = [
        jax.ShapeDtypeStruct((hd, lanes), F32),
        jax.ShapeDtypeStruct((8, lanes), F32),
        jax.ShapeDtypeStruct((hd, lanes), BF),
    ]
    return pl.pallas_call(
        resident_kernel,
        grid_spec=pltpu.PrefetchScalarGridSpec(
            num_scalar_prefetch=1,
            grid=(slots // block,),
            in_specs=[
                whole(q_mine.shape),
                whole(q_peer.shape),
                whole(entry.shape),
                whole(table.shape),
                whole(lengths.shape),
                pl.BlockSpec((block, rows, width), lambda i, h: (i, h[0], 0)),
            ],
            out_specs=[whole(o.shape) for o in outs],
            scratch_shapes=[
                pltpu.VMEM((slots, lanes), F32),
                pltpu.VMEM((slots, lanes), jnp.int32),
            ],
        ),
        out_shape=outs,
        compiler_params=params(),
        cost_estimate=cost(8),
        name="resident",
    )(half, q_mine, q_peer, entry, table, lengths, pool)


def moved_kernel(
    half_ref, qt_ref, tab_ref, len_ref, acc_in, stat_in, got_ref,
    keep_ref, send_ref, acc, stat, full, part,
):
    i = pl.program_id(0)
    pages, rows, width = got_ref.shape
    hd = width // 2
    mine = qt_ref.shape[1] // 2

    @pl.when(i == 0)
    def _():
        tables(full.shape[0], half_ref[0], rows, tab_ref, len_ref, full, part)
        acc[...] = acc_in[...]
        stat[...] = stat_in[...]

    chunk_step(got_ref, i * pages, qt_ref, full, part, acc, stat)

    @pl.when(i == pl.num_programs(0) - 1)
    def _():
        for k, out in enumerate((keep_ref, send_ref)):
            out[:hd, :] = acc[:, k * mine : (k + 1) * mine]
            out[hd : hd + 8, :] = stat[:, k * mine : (k + 1) * mine]


def moved(half, qt, table, lengths, acc, stat, got):
    slots, rows, width = got.shape
    hd, lanes = qt.shape
    block = 16
    whole = lambda shape: pl.BlockSpec(shape, lambda i, *_: (0,) * len(shape))
    out = jax.ShapeDtypeStruct((hd + 8, lanes // 2), F32)
    return pl.pallas_call(
        moved_kernel,
        grid_spec=pltpu.PrefetchScalarGridSpec(
            num_scalar_prefetch=1,
            grid=(slots // block,),
            in_specs=[
                whole(qt.shape),
                whole(table.shape),
                whole(lengths.shape),
                whole(acc.shape),
                whole(stat.shape),
                pl.BlockSpec((block, rows, width), lambda i, *_: (i, 0, 0)),
            ],
            out_specs=[whole(out.shape), whole(out.shape)],
            scratch_shapes=[
                pltpu.VMEM((hd, lanes), F32),
                pltpu.VMEM((8, lanes), F32),
                pltpu.VMEM((slots, lanes), F32),
                pltpu.VMEM((slots, lanes), jnp.int32),
            ],
        ),
        out_shape=[out, out],
        compiler_params=params(),
        cost_estimate=cost(8),
        name="moved",
    )(half, qt, table, lengths, acc, stat, got)


def project_kernel(mine_ref, a_ref, b_ref, w_ref, keep_ref, send_ref, scratch):
    hd = a_ref.shape[0] - 8
    ma, mb = a_ref[hd : hd + 1, :], b_ref[hd : hd + 1, :]
    top = jnp.maximum(ma, mb)
    wa, wb = jnp.exp(ma - top), jnp.exp(mb - top)
    den = a_ref[hd + 1 : hd + 2, :] * wa + b_ref[hd + 1 : hd + 2, :] * wb
    att = (a_ref[:hd, :] * wa + b_ref[:hd, :] * wb) / den
    att = att.T.astype(BF)
    games = scratch.shape[0]
    out = jnp.zeros(scratch.shape, F32)
    for h in range(att.shape[0] // games):
        out += jnp.dot(
            att[h * games : (h + 1) * games, :],
            w_ref[h * hd : (h + 1) * hd, :],
            preferred_element_type=F32,
        )
    scratch[...] = out
    rows = keep_ref.shape[1]
    m = mine_ref[0]
    core = lax.rem(m, 2)
    side = m // 2
    for ref, c in ((keep_ref, core), (send_ref, 1 - core)):
        for k, z in enumerate((side, 1 - side)):
            first = pl.multiple_of((z * 2 + c) * rows, rows)
            ref[k] = scratch[pl.ds(first, rows), :]


def project(mine, a, b, w, games):
    rows = games // 4
    whole = lambda shape: pl.BlockSpec(shape, lambda i, *_: (0,) * len(shape))
    out = jax.ShapeDtypeStruct((2, rows, w.shape[1]), F32)
    return pl.pallas_call(
        project_kernel,
        grid_spec=pltpu.PrefetchScalarGridSpec(
            num_scalar_prefetch=1,
            grid=(1,),
            in_specs=[whole(a.shape), whole(b.shape), whole(w.shape)],
            out_specs=[whole(out.shape), whole(out.shape)],
            scratch_shapes=[pltpu.VMEM((games, w.shape[1]), F32)],
        ),
        out_shape=[out, out],
        compiler_params=params(),
        cost_estimate=cost(3),
        name="project",
    )(mine, a, b, w)


def norm_kernel(mine_ref, keep_ref, got_ref, side_ref, res_ref, gain_ref, copies_ref, stream_ref):
    stream = res_ref[...].astype(F32) + ((keep_ref[0] + got_ref[0]) + side_ref[...])
    scale = lax.rsqrt(jnp.mean(stream * stream, axis=-1, keepdims=True) + 1e-06)
    normed = (stream * scale * (1.0 + gain_ref[...])).astype(BF)
    stream_ref[...] = stream
    for k in range(copies_ref.shape[0]):
        copies_ref[k] = normed


def norm(mine, keep, got, side, residual, gain, peers):
    _, rows, d = keep.shape
    whole = lambda shape: pl.BlockSpec(shape, lambda i, *_: (0,) * len(shape))
    outs = [
        jax.ShapeDtypeStruct((peers, rows, d), BF),
        jax.ShapeDtypeStruct((rows, d), F32),
    ]
    return pl.pallas_call(
        norm_kernel,
        grid_spec=pltpu.PrefetchScalarGridSpec(
            num_scalar_prefetch=1,
            grid=(1,),
            in_specs=[
                pl.BlockSpec((1, rows, d), lambda i, *_: (0, 0, 0)),
                pl.BlockSpec((1, rows, d), lambda i, *_: (0, 0, 0)),
                whole(side.shape),
                pl.BlockSpec((rows, d), lambda i, m: (m[0], 0)),
                whole(gain.shape),
            ],
            out_specs=[whole(o.shape) for o in outs],
        ),
        out_shape=outs,
        compiler_params=params(),
        cost_estimate=cost(2),
        name="norm",
    )(mine, keep, got, side, residual, gain)


def ffn_kernel(*refs):
    n = (len(refs) - 5) // 3
    x_ref = refs[0]
    w = [refs[1 + 3 * b : 4 + 3 * b] for b in range(n)]
    out_ref, x, hid, sem = refs[1 + 3 * n :]
    rows = x.shape[0]
    unit = w[0][0].shape[1]
    parts = sem.shape[0]
    step = rows // parts

    def load(k):
        at = pl.ds(k * step, step)
        return pltpu.make_async_copy(x_ref.at[at, :], x.at[at, :], sem.at[k])

    for k in range(parts):
        load(k).start()
    for k in range(parts):
        load(k).wait()
        at = slice(k * step, (k + 1) * step)
        for b, (g, u, _) in enumerate(w):
            both = jnp.dot(
                x[at, :], jnp.concatenate([g[...], u[...]], axis=1), preferred_element_type=F32
            )
            hid[at, b * unit : (b + 1) * unit] = (
                jax.nn.gelu(both[:, :unit], approximate=True) * both[:, unit:]
            ).astype(BF)
    cols = 512

    @pl.loop(0, out_ref.shape[1] // cols)
    def _(k):
        at = pl.ds(pl.multiple_of(k * cols, cols), cols)
        down = jnp.concatenate([d[:, at] for _, _, d in w], axis=0)
        out_ref[:, at] = jnp.dot(hid[...], down, preferred_element_type=F32).astype(BF)


def ffn(x, weights):
    n = len(weights)
    rows, d = x.shape
    unit = weights[0][0].shape[1]
    vmem = pl.BlockSpec(memory_space=pltpu.VMEM)
    return pl.pallas_call(
        ffn_kernel,
        in_specs=[pl.BlockSpec(memory_space=pltpu.HBM)] + [vmem] * (3 * n),
        out_specs=vmem,
        out_shape=jax.ShapeDtypeStruct((rows, d), BF),
        scratch_shapes=[
            pltpu.VMEM((rows, d), BF),
            pltpu.VMEM((rows, n * unit), BF),
            pltpu.SemaphoreType.DMA((2,)),
        ],
        compiler_params=params(),
        cost_estimate=cost(8),
        name="ffn",
    )(x, *[a for block in weights for a in block])


def finish_kernel(parts_ref, stream_ref, out_ref, held, sems):
    n = sems.shape[0]
    step = held.shape[0] // n

    def load(k):
        at = pl.ds(k * step, step)
        return pltpu.make_async_copy(parts_ref.at[at], held.at[at], sems.at[k])

    for k in range(n):
        load(k).start()
    total = jnp.zeros(out_ref.shape, F32)
    for k in range(n):
        load(k).wait()
        for j in range(k * step, (k + 1) * step):
            total += held[j].astype(F32)
    out_ref[...] = (stream_ref[...] + total).astype(BF)


def finish(parts, stream):
    vmem = pl.BlockSpec(memory_space=pltpu.VMEM)
    return pl.pallas_call(
        finish_kernel,
        in_specs=[pl.BlockSpec(memory_space=pltpu.HBM), vmem],
        out_specs=vmem,
        out_shape=jax.ShapeDtypeStruct(stream.shape, BF),
        scratch_shapes=[pltpu.VMEM(parts.shape, BF), pltpu.SemaphoreType.DMA((4,))],
        compiler_params=params(),
        cost_estimate=cost(2),
        name="finish",
    )(parts, stream)


def assemble_kernel(half_ref, mine_ref, peer_ref, out_ref):
    rows = mine_ref.shape[1]
    for ref, h in ((mine_ref, half_ref[0]), (peer_ref, 1 - half_ref[0])):
        out_ref[:, pl.ds(pl.multiple_of(h * rows, rows), rows), :] = ref[...]


def assemble(half, mine, peer):
    pages, rows, width = mine.shape
    block = 8
    spec = pl.BlockSpec((block, rows, width), lambda i, *_: (i, 0, 0))
    return pl.pallas_call(
        assemble_kernel,
        grid_spec=pltpu.PrefetchScalarGridSpec(
            num_scalar_prefetch=1,
            grid=(pages // block,),
            in_specs=[spec, spec],
            out_specs=pl.BlockSpec((block, 2 * rows, width), lambda i, *_: (i, 0, 0)),
        ),
        out_shape=jax.ShapeDtypeStruct((pages, 2 * rows, width), mine.dtype),
        compiler_params=params(),
        cost_estimate=cost(6),
        name="assemble",
    )(half, mine, peer)


def step(
    page_pool, move_count, send_slots, page_table, history_len, queries, new_entry, residual,
    out_proj, ffn_gain, gate_proj, up_proj, down_proj,
):
    axes = ("dp", "mp")
    n_dp, n_mp = lax.axis_size("dp"), lax.axis_size("mp")
    devices = n_dp * n_mp
    games, heads, hd = queries.shape
    page_len, width = page_pool.shape[1:]
    mine = lax.axis_index("mp").reshape(1)
    half = mine % 2
    swap = lambda bit: [(k, k ^ bit) for k in range(devices)]
    core, side = swap(1), swap(2)
    send = lambda a, pairs: lax.ppermute(a, axes, pairs)
    groups = [
        [k for k in range(devices) if k % 2 == c and ((k >> 1) ^ (k >> 2)) % 2 == w]
        for w in range(2)
        for c in range(2)
    ]
    peers = len(groups[0])
    exchange = lambda a: lax.all_to_all(a, axes, 0, 0, tiled=True, axis_index_groups=groups)

    out_pages = outgoing_pages(half, send_slots.reshape(-1), move_count.reshape(-1), page_pool)
    got = exchange(out_pages.reshape(n_dp, -1, page_len // 2, width)).reshape(out_pages.shape)

    q_mine = (queries.transpose(1, 0, 2) * jnp.asarray(hd**-0.5, BF)).reshape(
        heads * games, hd
    )
    q_peer = send(q_mine, core)
    copies = 2 * heads
    table = jnp.tile(page_table.T, (1, copies))
    lengths = jnp.tile(history_len[None, :], (1, copies))

    weights = (gate_proj, up_proj, down_proj)
    w_side = tuple(send(a, side) for a in weights)
    w_core = tuple(send(a, core) for a in weights)
    w_last = tuple(send(a, core) for a in w_side)

    acc, stat, qt = resident(half, q_mine, q_peer, new_entry, table, lengths, page_pool)
    keep, give = moved(half, qt, table, lengths, acc, stat, got)
    other = send(give, core)
    got_peer = send(got, core)
    hold, pass_on = project(mine, keep, other, out_proj, games)
    hold_got = send(pass_on, core)
    side_got = send(hold[1] + hold_got[1], side)
    arrived = assemble(half, got, got_peer)

    spread, stream = norm(
        mine, hold, hold_got, side_got, residual, ffn_gain.reshape(1, -1), peers
    )
    rows, d = stream.shape
    x = exchange(spread)
    parts = ffn(x.reshape(peers * rows, d), [weights, w_core, w_side, w_last])
    back = exchange(parts.reshape(peers, rows, d))
    quarter = finish(back, stream)
    layer_out = lax.all_gather(quarter, "mp", axis=0, tiled=True)
    return arrived, layer_out


def solution(mesh):
    in_specs = (
        P("dp", None, None),
        P("dp", None),
        P("dp", None),
        P("dp", None),
        P("dp"),
        P("dp", "mp", None),
        P("dp", None),
        P("dp", None),
        P("mp", None),
        P(),
        P(None, ("dp", "mp")),
        P(None, ("dp", "mp")),
        P(("dp", "mp"), None),
    )
    out_specs = (P("dp", None, None), P("dp", None))
    return jax.shard_map(step, mesh=mesh, in_specs=in_specs, out_specs=out_specs, check_vma=False)
```

time: 247 us -> 213 us (0.86)
  waiting for transfers between devices: 128 us -> 110 us
  starting transfers between devices: 46.7 us -> 36.4 us
  Pallas kernels: 52.2 us -> 47.3 us
    ppermute x14, waiting for transfers between devices: 50.6 us -> 38.5 us  [step(): send = lambda a, pairs: lax.ppermute(a, axes, pairs)]
    ppermute x14, starting transfers between devices: 20.4 us -> 11.5 us  [step(): send = lambda a, pairs: lax.ppermute(a, axes, pairs)]
    all_to_all x3, waiting for transfers between devices: 77.8 us -> 71.6 us  [step(): lax.all_to_all(a, axes, 0, 0, tiled=True, axis_index_groups=groups)]
    pallas_call x3 -> x4, Pallas kernels: 32.1 us -> 27.2 us  [the longest x1 9.82 us: ffn(): pl.pallas_call(ffn_kernel, in_specs=[pl.BlockSpec(memory_space=pltpu.HBM)...]
  transfers between devices with their start and end apart: 17 -> 17, of which waited for: 9 -> 9; matrix products, arithmetic and copies ran while one was open for 1% -> 1% of each run, Pallas kernels for 10% -> 13%
where the time goes in v2:
time: 213 us; the launch traced here: 212 us
  waiting for transfers between devices  110 us (52%)
  Pallas kernels  47.3 us (22%)
  starting transfers between devices  36.4 us (17%)
  local copies, waits for them, and re-layouts  8.85 us (4%)
  blocking collectives  7.59 us (4%)
    all_to_all x3, waiting for transfers between devices, step(): lax.all_to_all(a, axes, 0, 0, tiled=True, axis_index_groups=groups)  71.6 us
    ppermute x14, waiting for transfers between devices, step(): send = lambda a, pairs: lax.ppermute(a, axes, pairs)  38.5 us
    all_to_all x3, starting transfers between devices, step(): lax.all_to_all(a, axes, 0, 0, tiled=True, axis_index_groups=groups)  24.9 us
    ppermute x14, starting transfers between devices, step(): send = lambda a, pairs: lax.ppermute(a, axes, pairs)  11.5 us
    pallas_call x1, Pallas kernels, ffn(): pl.pallas_call(ffn_kernel, in_specs=[pl.BlockSpec(memory_space=pltpu.HBM)...  9.82 us
    pallas_call x1, Pallas kernels, assemble(): pl.pallas_call(assemble_kernel, grid_spec=pltpu.PrefetchScalarGridSpec(nu...  8.88 us
    all_gather x1, blocking collectives, step(): layer_out = lax.all_gather(quarter, 'mp', axis=0, tiled=True)  7.59 us
    pallas_call x1, Pallas kernels, resident(): pl.pallas_call(resident_kernel, grid_spec=pltpu.PrefetchScalarGridSpec(nu...  7.16 us
  transfers between devices with their start and end apart: 17, of which 9 were waited for; matrix products, arithmetic and copies ran while one was open for 1% of the time, Pallas kernels for 13%

profile of v2, /device:TPU:1, one launch (start us, length us, event | category | flops | bytes accessed | tf_op | source)
XLA Modules:
  0.0 212.2 jit_solution(11201611683108555366)
XLA Ops:
  2.0 5.5 %outgoing.1 = bf16[64,64,512]{2,1,0:T(8,128)(2,1)} custom-call(s32[1]{0:T(128)S(6)} %select_n.7.half_ref, s32[64]{0:T(128)} %reshape.45.slot_ref, s32[32]{0:T(128)} %bitcast.19, bf16[64,128,512]{2,1,0:T(8,128)(2,1)} %pool_ref.3), custom_call_target="tpu_custom_call" | custom-call | flops 1200000000 | bytes 6000000 | tf_op jit(solution)/shard_map/outgoing/pallas_call | solution.py:46
  7.6 11.7 %all-to-all-start = ((bf16[32,2,64,512]{3,2,1,0:T(8,128)(2,1)}), bf16[32,2,64,512]{3,2,1,0:T(8,128)(2,1)}, u32[]{:S(2)}, u32[]{:S(2)}) async-start(bf16[32,2,64,512]{3,2,1,0:T(8,128)(2,1)} %bitcast.13), calls=%async_computation | async-start | bytes 8388608 | tf_op jit(solution)/shard_map/all_to_all | solution.py:455
  22.5 7.2 %resident.1 = (f32[256,256]{1,0:T(8,128)}, f32[8,256]{1,0:T(8,128)}, bf16[256,256]{1,0:T(8,128)(2,1)}) custom-call(s32[1]{0:T(128)S(6)} %select_n.7.half_ref, bf16[128,256]{1,0:T(8,128)(2,1)} %bitcast.17, bf16[128,256]{1,0:T(8,128)(2,1)} %copy-done.19, bf16[64,512]{1,0:T(8,128)(2,1)} %entry_ref.1, s32[16,256]{1,0:T(8,128)} %tile.18.tab_ref, ...), custom_call_target="tpu_custom_call" | custom-call | flops 3200000000 | bytes 16000000 | tf_op jit(solution)/shard_map/resident/pallas_call | solution.py:154
  29.6 50.1 %all-to-all-done = bf16[32,2,64,512]{3,2,1,0:T(8,128)(2,1)} async-done(((bf16[32,2,64,512]{3,2,1,0:T(8,128)(2,1)}), bf16[32,2,64,512]{3,2,1,0:T(8,128)(2,1)}, u32[]{:S(2)}, u32[]{:S(2)}) %all-to-all-start) | async-done | bytes 4194336 | tf_op jit(solution)/shard_map/all_to_all | solution.py:455
  79.7 7.1 %moved.1 = (f32[264,128]{1,0:T(8,128)}, f32[264,128]{1,0:T(8,128)}) custom-call(s32[1]{0:T(128)S(6)} %select_n.7.half_ref, bf16[256,256]{1,0:T(8,128)(2,1)} %get-tuple-element.11.qt_ref, s32[16,256]{1,0:T(8,128)} %tile.18.tab_ref, s32[1,256]{1,0:T(1,128)} %tile.20.len_ref, f32[256,256]{1,0:T(8,128)} %get-tuple-element.12.acc_in, ...), custom_call_target="tpu_custom_call" | custom-call | flops 3200000000 | bytes 16000000 | tf_op jit(solution)/shard_map/moved/pallas_call | solution.py:210
  86.8 2.2 %collective-permute-start.2 = (f32[264,128]{1,0:T(8,128)}, f32[264,128]{1,0:T(8,128)S(1)}, u32[]{:S(2)}, u32[]{:S(2)}) collective-permute-start(f32[264,128]{1,0:T(8,128)} %get-tuple-element.15), channel_id=1, source_target_pairs={{0,1},{1,0},{2,3},{3,2},{4,5},{5,4},{6,7},{7,6},{8,9},{9,8},{10,11... | collective-permute-start | bytes 405512 | tf_op jit(solution)/shard_map/ppermute | solution.py:448
  90.8 3.1 %project.1 = (f32[2,16,2048]{2,1,0:T(8,128)}, f32[2,16,2048]{2,1,0:T(8,128)}) custom-call(s32[1]{0:T(128)} %bitcast.mine_ref, f32[264,128]{1,0:T(8,128)} %get-tuple-element.14.a_ref, f32[264,128]{1,0:T(8,128)} %copy-done.17, bf16[512,2048]{1,0:T(8,128)(2,1)} %w_ref.1), custom_call_target="tpu_custom_call" | custom-call | flops 1200000000 | bytes 6000000 | tf_op jit(solution)/shard_map/project/pallas_call | solution.py:269
  94.3 1.4 collective-permute-done.3.got_ref
  97.2 4.2 %collective-permute-done.4.side_ref = f32[16,2048]{1,0:T(8,128)S(1)} collective-permute-done((f32[16,2048]{1,0:T(8,128)S(1)}, f32[16,2048]{1,0:T(8,128)S(1)}, u32[]{:S(2)}, u32[]{:S(2)}) %collective-permute-start.4) | collective-permute-done | bytes 131104 | tf_op jit(solution)/shard_map/ppermute | solution.py:448
  102.1 2.6 %norm.1 = (bf16[32,16,2048]{2,1,0:T(8,128)(2,1)}, f32[16,2048]{1,0:T(8,128)}) custom-call(s32[1]{0:T(128)} %bitcast.mine_ref, f32[2,16,2048]{2,1,0:T(8,128)} %get-tuple-element.16.keep_ref, f32[2,16,2048]{2,1,0:T(8,128)} %copy-done.2, f32[16,2048]{1,0:T(8,128)} %copy-done.18, bf16[64,2048]{1,0:T(8,128)(2,1)} %res_ref.1, f32[1,2048]{1,0:T(1,128)} %bitcast.20), custom_call_target="tpu_custom_call" | custom-call | flops 800000000 | bytes 4000000 | tf_op jit(solution)/shard_map/norm/pallas_call | solution.py:301
  104.8 4.0 %all-to-all-start.1 = ((bf16[32,16,2048]{2,1,0:T(8,128)(2,1)}), bf16[32,16,2048]{2,1,0:T(8,128)(2,1)S(1)}, u32[]{:S(2)}, u32[]{:S(2)}) async-start(bf16[32,16,2048]{2,1,0:T(8,128)(2,1)} %get-tuple-element.18), calls=%async_computation.1 | async-start | bytes 4194304 | tf_op jit(solution)/shard_map/all_to_all | solution.py:455
  110.5 1.5 collective-permute-start.9
  112.0 11.5 %collective-permute-done.8.refs_7_ = bf16[2048,128]{1,0:T(8,128)(2,1)S(1)} collective-permute-done((bf16[2048,128]{1,0:T(8,128)(2,1)S(1)}, bf16[2048,128]{1,0:T(8,128)(2,1)S(1)}, u32[]{:S(2)}, u32[]{:S(2)}) %collective-permute-start.8) | collective-permute-done | bytes 524320 | tf_op jit(solution)/shard_map/ppermute | solution.py:448
  123.5 1.5 collective-permute-start.7
  125.1 9.6 %collective-permute-done.9.refs_8_ = bf16[2048,128]{1,0:T(8,128)(2,1)S(1)} collective-permute-done((bf16[2048,128]{1,0:T(8,128)(2,1)S(1)}, bf16[2048,128]{1,0:T(8,128)(2,1)S(1)}, u32[]{:S(2)}, u32[]{:S(2)}) %collective-permute-start.9) | collective-permute-done | bytes 524320 | tf_op jit(solution)/shard_map/ppermute | solution.py:448
  134.7 1.5 collective-permute-start.12
  136.2 9.7 %collective-permute-done.10.refs_9_ = bf16[128,2048]{1,0:T(8,128)(2,1)S(1)} collective-permute-done((bf16[128,2048]{1,0:T(8,128)(2,1)}, bf16[128,2048]{1,0:T(8,128)(2,1)S(1)}, u32[]{:S(2)}, u32[]{:S(2)}) %collective-permute-start.10) | collective-permute-done | bytes 524320 | tf_op jit(solution)/shard_map/ppermute | solution.py:448
  149.9 9.8 %ffn.1 = bf16[512,2048]{1,0:T(8,128)(2,1)} custom-call(bf16[512,2048]{1,0:T(8,128)(2,1)} %bitcast.14, bf16[2048,128]{1,0:T(8,128)(2,1)} %refs_1_.1, bf16[2048,128]{1,0:T(8,128)(2,1)} %refs_2_.1, bf16[128,2048]{1,0:T(8,128)(2,1)} %refs_3_.1, bf16[2048,128]{1,0:T(8,128)(2,1)} %copy-done.9, bf16[2048,128]{1,0:T(8,128)(2,1)} %copy-done.11, ...), custom_call_target="tpu_custom_call" | custom-call | flops 3200000000 | bytes 16000000 | tf_op jit(solution)/shard_map/ffn/pallas_call | solution.py:362
  159.7 9.2 %all-to-all-start.2 = ((bf16[32,16,2048]{2,1,0:T(8,128)(2,1)}), bf16[32,16,2048]{2,1,0:T(8,128)(2,1)S(1)}, u32[]{:S(2)}, u32[]{:S(2)}) async-start(bf16[32,16,2048]{2,1,0:T(8,128)(2,1)} %bitcast.15), calls=%async_computation.2 | async-start | bytes 4194304 | tf_op jit(solution)/shard_map/all_to_all | solution.py:455
  169.0 8.9 %assemble.1 = bf16[64,128,512]{2,1,0:T(8,128)(2,1)} custom-call(s32[1]{0:T(128)S(6)} %select_n.7.half_ref, bf16[64,64,512]{2,1,0:T(8,128)(2,1)} %bitcast.3.mine_ref.got_ref, bf16[64,64,512]{2,1,0:T(8,128)(2,1)} %collective-permute-done.peer_ref), custom_call_target="tpu_custom_call" | custom-call | flops 2400000000 | bytes 12000000 | tf_op jit(solution)/shard_map/assemble/pallas_call | solution.py:420
  177.9 21.5 %all-to-all-done.2.parts_ref = bf16[32,16,2048]{2,1,0:T(8,128)(2,1)S(1)} async-done(((bf16[32,16,2048]{2,1,0:T(8,128)(2,1)}), bf16[32,16,2048]{2,1,0:T(8,128)(2,1)S(1)}, u32[]{:S(2)}, u32[]{:S(2)}) %all-to-all-start.2) | async-done | bytes 2097184 | tf_op jit(solution)/shard_map/all_to_all | solution.py:455
  199.4 1.4 copy-done.1
  200.7 3.2 %finish.1 = bf16[16,2048]{1,0:T(8,128)(2,1)} custom-call(bf16[32,16,2048]{2,1,0:T(8,128)(2,1)} %copy-done.1, f32[16,2048]{1,0:T(8,128)} %get-tuple-element.19.stream_ref), custom_call_target="tpu_custom_call" | custom-call | flops 800000000 | bytes 4000000 | tf_op jit(solution)/shard_map/finish/pallas_call | solution.py:398
  203.9 7.6 %all_gather.3 = bf16[64,2048]{1,0:T(8,128)(2,1)S(1)} all-gather(bf16[16,2048]{1,0:T(8,128)(2,1)} %finish.1), channel_id=1, replica_groups=mesh['dp'=32,'mp'=4] {'mp'}, dimensions={0}, use_global_device_ids=true | all-gather | bytes 327680 | tf_op jit(solution)/shard_map/all_gather | solution.py:490
  (69 shorter events, 15.5 us)
Async XLA Ops:
  7.5 13.0 %copy-start.6 = (s32[64]{0:T(128)S(1)}, s32[64]{0:T(128)}, u32[]{:S(2)}) copy-start(s32[64]{0:T(128)} %param.17) | copy-start | bytes 772
  7.6 13.6 %copy-start.5 = (s32[64,16]{0,1:T(8,128)S(1)}, s32[64,16]{0,1:T(8,128)}, u32[]{:S(2)}) copy-start(s32[64,16]{0,1:T(8,128)} %param.16) | copy-start | bytes 12292
  7.6 72.1 %all-to-all-start = ((bf16[32,2,64,512]{3,2,1,0:T(8,128)(2,1)}), bf16[32,2,64,512]{3,2,1,0:T(8,128)(2,1)}, u32[]{:S(2)}, u32[]{:S(2)}) async-start(bf16[32,2,64,512]{3,2,1,0:T(8,128)(2,1)} %bitcast.13), calls=%async_computation | async-start | bytes 8388608 | tf_op jit(solution)/shard_map/all_to_all | solution.py:455
  19.4 2.5 %collective-permute-start.1 = (bf16[128,256]{1,0:T(8,128)(2,1)S(1)}, bf16[128,256]{1,0:T(8,128)(2,1)S(1)}, u32[]{:S(2)}, u32[]{:S(2)}) collective-permute-start(bf16[128,256]{1,0:T(8,128)(2,1)S(1)} %bitcast.16), channel_id=1, source_target_pairs={{0,1},{1,0},{2,3},{3,2},{4,5},{5,4},{6,7},{7,6},{8,9},{9,8},{10,11... | collective-permute-start | bytes 196616 | tf_op jit(solution)/shard_map/ppermute | solution.py:448
  86.8 3.4 %collective-permute-start.2 = (f32[264,128]{1,0:T(8,128)}, f32[264,128]{1,0:T(8,128)S(1)}, u32[]{:S(2)}, u32[]{:S(2)}) collective-permute-start(f32[264,128]{1,0:T(8,128)} %get-tuple-element.15), channel_id=1, source_target_pairs={{0,1},{1,0},{2,3},{3,2},{4,5},{5,4},{6,7},{7,6},{8,9},{9,8},{10,11... | collective-permute-start | bytes 405512 | tf_op jit(solution)/shard_map/ppermute | solution.py:448
  93.9 14.9 %copy-start.7 = (bf16[2048,128]{1,0:T(8,128)(2,1)S(1)}, bf16[2048,128]{1,0:T(8,128)(2,1)}, u32[]{:S(2)}) copy-start(bf16[2048,128]{1,0:T(8,128)(2,1)} %refs_1_.1) | copy-start | bytes 1572868
  93.9 16.2 %copy-start.8 = (bf16[2048,128]{1,0:T(8,128)(2,1)S(1)}, bf16[2048,128]{1,0:T(8,128)(2,1)}, u32[]{:S(2)}) copy-start(bf16[2048,128]{1,0:T(8,128)(2,1)} %refs_2_.1) | copy-start | bytes 1572868
  93.9 1.7 collective-permute-start.3
  96.7 4.8 %collective-permute-start.4 = (f32[16,2048]{1,0:T(8,128)S(1)}, f32[16,2048]{1,0:T(8,128)S(1)}, u32[]{:S(2)}, u32[]{:S(2)}) collective-permute-start(f32[16,2048]{1,0:T(8,128)S(1)} %fusion), channel_id=1, source_target_pairs={{0,2},{1,3},{2,0},{3,1},{4,6},{5,7},{6,4},{7,5},{8,10},{9,11},{10,... | collective-permute-start | bytes 393224 | tf_op jit(solution)/shard_map/ppermute | solution.py:448
  96.8 72.2 %collective-permute-start = (bf16[64,64,512]{2,1,0:T(8,128)(2,1)}, bf16[64,64,512]{2,1,0:T(8,128)(2,1)}, u32[]{:S(2)}, u32[]{:S(2)}) collective-permute-start(bf16[64,64,512]{2,1,0:T(8,128)(2,1)} %bitcast.3.mine_ref.got_ref), channel_id=1, source_target_pairs={{0,1},{1,0},{2,3},{3,2},{4,5},{5,4},{6,7},{7,6},{8,9},{9,8},{10,11... | collective-permute-start | bytes 12582920 | tf_op jit(solution)/shard_map/ppermute | solution.py:448
  104.8 43.8 %all-to-all-start.1 = ((bf16[32,16,2048]{2,1,0:T(8,128)(2,1)}), bf16[32,16,2048]{2,1,0:T(8,128)(2,1)S(1)}, u32[]{:S(2)}, u32[]{:S(2)}) async-start(bf16[32,16,2048]{2,1,0:T(8,128)(2,1)} %get-tuple-element.18), calls=%async_computation.1 | async-start | bytes 4194304 | tf_op jit(solution)/shard_map/all_to_all | solution.py:455
  108.8 3.1 %collective-permute-start.5 = (bf16[2048,128]{1,0:T(8,128)(2,1)S(1)}, bf16[2048,128]{1,0:T(8,128)(2,1)S(1)}, u32[]{:S(2)}, u32[]{:S(2)}) collective-permute-start(bf16[2048,128]{1,0:T(8,128)(2,1)S(1)} %copy-done.7), channel_id=1, source_target_pairs={{0,1},{1,0},{2,3},{3,2},{4,5},{5,4},{6,7},{7,6},{8,9},{9,8},{10,11... | collective-permute-start | bytes 1572872 | tf_op jit(solution)/shard_map/ppermute | solution.py:448
  110.1 13.4 %collective-permute-start.8 = (bf16[2048,128]{1,0:T(8,128)(2,1)S(1)}, bf16[2048,128]{1,0:T(8,128)(2,1)S(1)}, u32[]{:S(2)}, u32[]{:S(2)}) collective-permute-start(bf16[2048,128]{1,0:T(8,128)(2,1)S(1)} %copy-done.7), channel_id=1, source_target_pairs={{0,2},{1,3},{2,0},{3,1},{4,6},{5,7},{6,4},{7,5},{8,10},{9,11},{10,... | collective-permute-start | bytes 1572872 | tf_op jit(solution)/shard_map/ppermute | solution.py:448
  110.1 14.9 %collective-permute-start.6 = (bf16[2048,128]{1,0:T(8,128)(2,1)S(1)}, bf16[2048,128]{1,0:T(8,128)(2,1)S(1)}, u32[]{:S(2)}, u32[]{:S(2)}) collective-permute-start(bf16[2048,128]{1,0:T(8,128)(2,1)S(1)} %copy-done.8), channel_id=1, source_target_pairs={{0,1},{1,0},{2,3},{3,2},{4,5},{5,4},{6,7},{7,6},{8,9},{9,8},{10,11... | collective-permute-start | bytes 1572872 | tf_op jit(solution)/shard_map/ppermute | solution.py:448
  110.5 24.2 %collective-permute-start.9 = (bf16[2048,128]{1,0:T(8,128)(2,1)S(1)}, bf16[2048,128]{1,0:T(8,128)(2,1)S(1)}, u32[]{:S(2)}, u32[]{:S(2)}) collective-permute-start(bf16[2048,128]{1,0:T(8,128)(2,1)S(1)} %copy-done.8), channel_id=1, source_target_pairs={{0,2},{1,3},{2,0},{3,1},{4,6},{5,7},{6,4},{7,5},{8,10},{9,11},{10,... | collective-permute-start | bytes 1572872 | tf_op jit(solution)/shard_map/ppermute | solution.py:448
  111.9 35.0 %copy-start.9 = (bf16[2048,128]{1,0:T(8,128)(2,1)}, bf16[2048,128]{1,0:T(8,128)(2,1)S(1)}, u32[]{:S(2)}) copy-start(bf16[2048,128]{1,0:T(8,128)(2,1)S(1)} %collective-permute-done.5.refs_4_) | copy-start | bytes 1572868
  111.9 34.0 %collective-permute-start.10 = (bf16[128,2048]{1,0:T(8,128)(2,1)}, bf16[128,2048]{1,0:T(8,128)(2,1)S(1)}, u32[]{:S(2)}, u32[]{:S(2)}) collective-permute-start(bf16[128,2048]{1,0:T(8,128)(2,1)} %refs_3_.1), channel_id=1, source_target_pairs={{0,2},{1,3},{2,0},{3,1},{4,6},{5,7},{6,4},{7,5},{8,10},{9,11},{10,... | collective-permute-start | bytes 1572872 | tf_op jit(solution)/shard_map/ppermute | solution.py:448
  123.5 23.5 %copy-start.10 = (bf16[2048,128]{1,0:T(8,128)(2,1)}, bf16[2048,128]{1,0:T(8,128)(2,1)S(1)}, u32[]{:S(2)}) copy-start(bf16[2048,128]{1,0:T(8,128)(2,1)S(1)} %collective-permute-done.8.refs_7_) | copy-start | bytes 1572868
  123.5 23.4 %collective-permute-start.7 = (bf16[128,2048]{1,0:T(8,128)(2,1)}, bf16[128,2048]{1,0:T(8,128)(2,1)S(1)}, u32[]{:S(2)}, u32[]{:S(2)}) collective-permute-start(bf16[128,2048]{1,0:T(8,128)(2,1)} %refs_3_.1), channel_id=1, source_target_pairs={{0,1},{1,0},{2,3},{3,2},{4,5},{5,4},{6,7},{7,6},{8,9},{9,8},{10,11... | collective-permute-start | bytes 1572872 | tf_op jit(solution)/shard_map/ppermute | solution.py:448
  125.0 22.0 %copy-start.11 = (bf16[2048,128]{1,0:T(8,128)(2,1)}, bf16[2048,128]{1,0:T(8,128)(2,1)S(1)}, u32[]{:S(2)}) copy-start(bf16[2048,128]{1,0:T(8,128)(2,1)S(1)} %collective-permute-done.6.refs_5_) | copy-start | bytes 1572868
  125.0 21.9 %collective-permute-start.11 = (bf16[2048,128]{1,0:T(8,128)(2,1)S(1)}, bf16[2048,128]{1,0:T(8,128)(2,1)S(1)}, u32[]{:S(2)}, u32[]{:S(2)}) collective-permute-start(bf16[2048,128]{1,0:T(8,128)(2,1)S(1)} %collective-permute-done.8.refs_7_), channel_id=1, source_target_pairs={{0,1},{1,0},{2,3},{3,2},{4,5},{5,4},{6,7},{7,6},{8,9},{9,8},{10,11... | collective-permute-start | bytes 1572872 | tf_op jit(solution)/shard_map/ppermute | solution.py:448
  134.7 12.2 %collective-permute-start.12 = (bf16[2048,128]{1,0:T(8,128)(2,1)S(1)}, bf16[2048,128]{1,0:T(8,128)(2,1)S(1)}, u32[]{:S(2)}, u32[]{:S(2)}) collective-permute-start(bf16[2048,128]{1,0:T(8,128)(2,1)S(1)} %collective-permute-done.9.refs_8_), channel_id=1, source_target_pairs={{0,1},{1,0},{2,3},{3,2},{4,5},{5,4},{6,7},{7,6},{8,9},{9,8},{10,11... | collective-permute-start | bytes 1572872 | tf_op jit(solution)/shard_map/ppermute | solution.py:448
  146.0 2.6 %collective-permute-start.13 = (bf16[128,2048]{1,0:T(8,128)(2,1)S(1)}, bf16[128,2048]{1,0:T(8,128)(2,1)}, u32[]{:S(2)}, u32[]{:S(2)}) collective-permute-start(bf16[128,2048]{1,0:T(8,128)(2,1)S(1)} %collective-permute-done.10.refs_9_), channel_id=1, source_target_pairs={{0,1},{1,0},{2,3},{3,2},{4,5},{5,4},{6,7},{7,6},{8,9},{9,8},{10,11... | collective-permute-start | bytes 1572872 | tf_op jit(solution)/shard_map/ppermute | solution.py:448
  159.7 39.6 %all-to-all-start.2 = ((bf16[32,16,2048]{2,1,0:T(8,128)(2,1)}), bf16[32,16,2048]{2,1,0:T(8,128)(2,1)S(1)}, u32[]{:S(2)}, u32[]{:S(2)}) async-start(bf16[32,16,2048]{2,1,0:T(8,128)(2,1)} %bitcast.15), calls=%async_computation.2 | async-start | bytes 4194304 | tf_op jit(solution)/shard_map/all_to_all | solution.py:455
  (13 other events, 41.3 us)

commit v3 on v2

--- a/solution.py
+++ b/solution.py
@@ -9,11 +9,10 @@
 NEG = -1e30
 BF = jnp.bfloat16
 F32 = jnp.float32
-VLIM = 60 * 1024 * 1024
-
-
-def params(**kw):
-    return pltpu.CompilerParams(vmem_limit_bytes=VLIM, **kw)
+
+
+def params(mib):
+    return pltpu.CompilerParams(vmem_limit_bytes=mib * 1024 * 1024)
 
 
 def cost(us):
@@ -53,7 +52,7 @@
             scratch_shapes=[pltpu.SemaphoreType.DMA((pages,))],
         ),
         out_shape=jax.ShapeDtypeStruct((pages, rows, pool.shape[2]), pool.dtype),
-        compiler_params=params(),
+        compiler_params=params(60),
         cost_estimate=cost(3),
         name="outgoing",
     )(half, slots, counts, pool)
@@ -171,7 +170,7 @@
             ],
         ),
         out_shape=outs,
-        compiler_params=params(),
+        compiler_params=params(60),
         cost_estimate=cost(8),
         name="resident",
     )(half, q_mine, q_peer, entry, table, lengths, pool)
@@ -229,7 +228,7 @@
             ],
         ),
         out_shape=[out, out],
-        compiler_params=params(),
+        compiler_params=params(20),
         cost_estimate=cost(8),
         name="moved",
     )(half, qt, table, lengths, acc, stat, got)
@@ -276,7 +275,7 @@
             scratch_shapes=[pltpu.VMEM((games, w.shape[1]), F32)],
         ),
         out_shape=[out, out],
-        compiler_params=params(),
+        compiler_params=params(10),
         cost_estimate=cost(3),
         name="project",
     )(mine, a, b, w)
@@ -313,38 +312,25 @@
             out_specs=[whole(o.shape) for o in outs],
         ),
         out_shape=outs,
-        compiler_params=params(),
+        compiler_params=params(6),
         cost_estimate=cost(2),
         name="norm",
     )(mine, keep, got, side, residual, gain)
 
 
 def ffn_kernel(*refs):
-    n = (len(refs) - 5) // 3
+    n = (len(refs) - 3) // 3
     x_ref = refs[0]
     w = [refs[1 + 3 * b : 4 + 3 * b] for b in range(n)]
-    out_ref, x, hid, sem = refs[1 + 3 * n :]
-    rows = x.shape[0]
+    out_ref, hid = refs[1 + 3 * n :]
     unit = w[0][0].shape[1]
-    parts = sem.shape[0]
-    step = rows // parts
-
-    def load(k):
-        at = pl.ds(k * step, step)
-        return pltpu.make_async_copy(x_ref.at[at, :], x.at[at, :], sem.at[k])
-
-    for k in range(parts):
-        load(k).start()
-    for k in range(parts):
-        load(k).wait()
-        at = slice(k * step, (k + 1) * step)
-        for b, (g, u, _) in enumerate(w):
-            both = jnp.dot(
-                x[at, :], jnp.concatenate([g[...], u[...]], axis=1), preferred_element_type=F32
-            )
-            hid[at, b * unit : (b + 1) * unit] = (
-                jax.nn.gelu(both[:, :unit], approximate=True) * both[:, unit:]
-            ).astype(BF)
+    for b, (g, u, _) in enumerate(w):
+        both = jnp.dot(
+            x_ref[...], jnp.concatenate([g[...], u[...]], axis=1), preferred_element_type=F32
+        )
+        hid[:, b * unit : (b + 1) * unit] = (
+            jax.nn.gelu(both[:, :unit], approximate=True) * both[:, unit:]
+        ).astype(BF)
     cols = 512
 
     @pl.loop(0, out_ref.shape[1] // cols)
@@ -361,35 +347,20 @@
     vmem = pl.BlockSpec(memory_space=pltpu.VMEM)
     return pl.pallas_call(
         ffn_kernel,
-        in_specs=[pl.BlockSpec(memory_space=pltpu.HBM)] + [vmem] * (3 * n),
+        in_specs=[vmem] * (1 + 3 * n),
         out_specs=vmem,
         out_shape=jax.ShapeDtypeStruct((rows, d), BF),
-        scratch_shapes=[
-            pltpu.VMEM((rows, d), BF),
-            pltpu.VMEM((rows, n * unit), BF),
-            pltpu.SemaphoreType.DMA((2,)),
-        ],
-        compiler_params=params(),
+        scratch_shapes=[pltpu.VMEM((rows, n * unit), BF)],
+        compiler_params=params(24),
         cost_estimate=cost(8),
         name="ffn",
     )(x, *[a for block in weights for a in block])
 
 
-def finish_kernel(parts_ref, stream_ref, out_ref, held, sems):
-    n = sems.shape[0]
-    step = held.shape[0] // n
-
-    def load(k):
-        at = pl.ds(k * step, step)
-        return pltpu.make_async_copy(parts_ref.at[at], held.at[at], sems.at[k])
-
-    for k in range(n):
-        load(k).start()
-    total = jnp.zeros(out_ref.shape, F32)
-    for k in range(n):
-        load(k).wait()
-        for j in range(k * step, (k + 1) * step):
-            total += held[j].astype(F32)
+def finish_kernel(parts_ref, stream_ref, out_ref):
+    total = parts_ref[0].astype(F32)
+    for k in range(1, parts_ref.shape[0]):
+        total += parts_ref[k].astype(F32)
     out_ref[...] = (stream_ref[...] + total).astype(BF)
 
 
@@ -397,11 +368,10 @@
     vmem = pl.BlockSpec(memory_space=pltpu.VMEM)
     return pl.pallas_call(
         finish_kernel,
-        in_specs=[pl.BlockSpec(memory_space=pltpu.HBM), vmem],
+        in_specs=[vmem, vmem],
         out_specs=vmem,
         out_shape=jax.ShapeDtypeStruct(stream.shape, BF),
-        scratch_shapes=[pltpu.VMEM(parts.shape, BF), pltpu.SemaphoreType.DMA((4,))],
-        compiler_params=params(),
+        compiler_params=params(4),
         cost_estimate=cost(2),
         name="finish",
     )(parts, stream)
@@ -426,7 +396,7 @@
             out_specs=pl.BlockSpec((block, 2 * rows, width), lambda i, *_: (i, 0, 0)),
         ),
         out_shape=jax.ShapeDtypeStruct((pages, 2 * rows, width), mine.dtype),
-        compiler_params=params(),
+        compiler_params=params(8),
         cost_estimate=cost(6),
         name="assemble",
     )(half, mine, peer)
@@ -444,18 +414,24 @@
     mine = lax.axis_index("mp").reshape(1)
     half = mine % 2
     swap = lambda bit: [(k, k ^ bit) for k in range(devices)]
-    core, side = swap(1), swap(2)
     send = lambda a, pairs: lax.ppermute(a, axes, pairs)
+    core, side, far = swap(1), swap(2), swap(6)
+    every = range(devices)
     groups = [
-        [k for k in range(devices) if k % 2 == c and ((k >> 1) ^ (k >> 2)) % 2 == w]
+        [k for k in every if k % 2 == c and ((k >> 1) ^ (k >> 2)) % 2 == w]
         for w in range(2)
         for c in range(2)
     ]
-    peers = len(groups[0])
-    exchange = lambda a: lax.all_to_all(a, axes, 0, 0, tiled=True, axis_index_groups=groups)
+    planes = [[k for k in every if k % 8 == z] for z in range(8)]
+    peers = len(planes[0])
+    exchange = lambda a, who: lax.all_to_all(
+        a, axes, 0, 0, tiled=True, axis_index_groups=who
+    )
 
     out_pages = outgoing_pages(half, send_slots.reshape(-1), move_count.reshape(-1), page_pool)
-    got = exchange(out_pages.reshape(n_dp, -1, page_len // 2, width)).reshape(out_pages.shape)
+    got = exchange(
+        out_pages.reshape(n_dp, -1, page_len // 2, width), groups
+    ).reshape(out_pages.shape)
 
     q_mine = (queries.transpose(1, 0, 2) * jnp.asarray(hd**-0.5, BF)).reshape(
         heads * games, hd
@@ -466,9 +442,17 @@
     lengths = jnp.tile(history_len[None, :], (1, copies))
 
     weights = (gate_proj, up_proj, down_proj)
-    w_side = tuple(send(a, side) for a in weights)
-    w_core = tuple(send(a, core) for a in weights)
-    w_last = tuple(send(a, core) for a in w_side)
+    each = lambda ws, pairs: tuple(send(a, pairs) for a in ws)
+    w_side = each(weights, side)
+    w_core = each(weights, core)
+    w_side_core = each(w_side, core)
+    w_far = each(weights, far)
+    w_diag = each(w_far, side)
+    w_far_core = each(w_far, core)
+    w_diag_core = each(w_diag, core)
+    blocks = [
+        weights, w_core, w_side, w_side_core, w_far, w_far_core, w_diag, w_diag_core
+    ]
 
     acc, stat, qt = resident(half, q_mine, q_peer, new_entry, table, lengths, page_pool)
     keep, give = moved(half, qt, table, lengths, acc, stat, got)
@@ -483,9 +467,9 @@
         mine, hold, hold_got, side_got, residual, ffn_gain.reshape(1, -1), peers
     )
     rows, d = stream.shape
-    x = exchange(spread)
-    parts = ffn(x.reshape(peers * rows, d), [weights, w_core, w_side, w_last])
-    back = exchange(parts.reshape(peers, rows, d))
+    x = exchange(spread, planes)
+    parts = ffn(x.reshape(peers * rows, d), blocks)
+    back = exchange(parts.reshape(peers, rows, d), planes)
     quarter = finish(back, stream)
     layer_out = lax.all_gather(quarter, "mp", axis=0, tiled=True)
     return arrived, layer_out
@@ -508,4 +492,6 @@
         P(("dp", "mp"), None),
     )
     out_specs = (P("dp", None, None), P("dp", None))
-    return jax.shard_map(step, mesh=mesh, in_specs=in_specs, out_specs=out_specs, check_vma=False)
+    return jax.shard_map(
+        step, mesh=mesh, in_specs=in_specs, out_specs=out_specs, check_vma=False
+    )

time: 213 us -> 228 us (1.070)
  blocking collectives: 7.59 us -> 27.5 us
  local copies, waits for them, and re-layouts: 8.85 us -> 24.9 us
  waiting for transfers between devices: 110 us -> 95.2 us
  Pallas kernels: 47.3 us -> 36.3 us
  starting transfers between devices: 36.4 us -> 41.3 us
    all_to_all x3 -> x2, waiting for transfers between devices: 71.6 us -> 16.1 us  [step(): lax.all_to_all(a, axes, 0, 0, tiled=True, axis_index_groups=who)]
    ppermute x14 -> x26, waiting for transfers between devices: 38.5 us -> 79.1 us  [step(): send = lambda a, pairs: lax.ppermute(a, axes, pairs)]
    all_to_all x0 -> x1, blocking collectives: none -> 20 us  [step(): lax.all_to_all(a, axes, 0, 0, tiled=True, axis_index_groups=who)]
    unnamed x42 -> x82, local copies, waits for them, and re-layouts: 6.87 us -> 22.9 us
    ppermute x14 -> x26, starting transfers between devices: 11.5 us -> 22.9 us  [step(): send = lambda a, pairs: lax.ppermute(a, axes, pairs)]
    all_to_all x3 -> x2, starting transfers between devices: 24.9 us -> 18.5 us  [step(): lax.all_to_all(a, axes, 0, 0, tiled=True, axis_index_groups=who)]
    pallas_call x2, Pallas kernels: 13 us -> 6.6 us  [the longest x1 6.45 us: ffn(): pl.pallas_call(ffn_kernel, in_specs=[vmem] * (1 + 3 * n), out_specs=vmem,...]
    pallas_call x1, Pallas kernels: 3.11 us -> 0.59 us  [project(): pl.pallas_call(project_kernel, grid_spec=pltpu.PrefetchScalarGridSpec(num...]
  transfers between devices with their start and end apart: 17 -> 28, of which waited for: 9 -> 10; matrix products, arithmetic and copies ran while one was open for 1% -> 1% of each run, Pallas kernels for 13% -> 10%
where the time goes in v3:
time: 228 us; the launch traced here: 226 us
  waiting for transfers between devices  95.2 us (42%)
  starting transfers between devices  41.3 us (18%)
  Pallas kernels  36.3 us (16%)
  blocking collectives  27.5 us (12%)
  local copies, waits for them, and re-layouts  24.9 us (11%)
    ppermute x26, waiting for transfers between devices, step(): send = lambda a, pairs: lax.ppermute(a, axes, pairs)  79.1 us
    unnamed x82, local copies, waits for them, and re-layouts  22.9 us
    ppermute x26, starting transfers between devices, step(): send = lambda a, pairs: lax.ppermute(a, axes, pairs)  22.9 us
    all_to_all x1, blocking collectives, step(): lax.all_to_all(a, axes, 0, 0, tiled=True, axis_index_groups=who)  20 us
    all_to_all x2, starting transfers between devices, step(): lax.all_to_all(a, axes, 0, 0, tiled=True, axis_index_groups=who)  18.5 us
    all_to_all x2, waiting for transfers between devices, step(): lax.all_to_all(a, axes, 0, 0, tiled=True, axis_index_groups=who)  16.1 us
    pallas_call x1, Pallas kernels, assemble(): pl.pallas_call(assemble_kernel, grid_spec=pltpu.PrefetchScalarGridSpec(nu...  8.87 us
    all_gather x1, blocking collectives, step(): layer_out = lax.all_gather(quarter, 'mp', axis=0, tiled=True)  7.47 us
  transfers between devices with their start and end apart: 28, of which 10 were waited for; matrix products, arithmetic and copies ran while one was open for 1% of the time, Pallas kernels for 10%

profile of v3, /device:TPU:1, one launch (start us, length us, event | category | flops | bytes accessed | tf_op | source)
XLA Modules:
  0.0 226.2 jit_solution(9395109042803177231)
XLA Ops:
  2.0 5.5 %outgoing.1 = bf16[64,64,512]{2,1,0:T(8,128)(2,1)} custom-call(s32[1]{0:T(128)S(6)} %select_n.7.half_ref, s32[64]{0:T(128)} %reshape.45.slot_ref, s32[32]{0:T(128)} %bitcast.20, bf16[64,128,512]{2,1,0:T(8,128)(2,1)} %pool_ref.3), custom_call_target="tpu_custom_call" | custom-call | flops 1200000000 | bytes 6000000 | tf_op jit(solution)/shard_map/outgoing/pallas_call | solution.py:45
  7.6 11.7 %all-to-all-start = ((bf16[32,2,64,512]{3,2,1,0:T(8,128)(2,1)}), bf16[32,2,64,512]{3,2,1,0:T(8,128)(2,1)}, u32[]{:S(2)}, u32[]{:S(2)}) async-start(bf16[32,2,64,512]{3,2,1,0:T(8,128)(2,1)} %bitcast.16), calls=%async_computation | async-start | bytes 8388608 | tf_op jit(solution)/shard_map/all_to_all | solution.py:427
  19.3 2.4 %collective-permute-start.14 = (bf16[2048,128]{1,0:T(8,128)(2,1)S(1)}, bf16[2048,128]{1,0:T(8,128)(2,1)S(1)}, u32[]{:S(2)}, u32[]{:S(2)}) collective-permute-start(bf16[2048,128]{1,0:T(8,128)(2,1)S(1)} %copy-done), channel_id=1, source_target_pairs={{0,6},{1,7},{2,4},{3,5},{4,2},{5,3},{6,0},{7,1},{8,14},{9,15},{10,... | collective-permute-start | bytes 1572872 | tf_op jit(solution)/shard_map/ppermute | solution.py:417
  22.2 1.7 collective-permute-start.1
  23.9 1.5 collective-permute-start.9
  26.6 2.7 %collective-permute-start.16 = (bf16[128,2048]{1,0:T(8,128)(2,1)S(1)}, bf16[128,2048]{1,0:T(8,128)(2,1)}, u32[]{:S(2)}, u32[]{:S(2)}) collective-permute-start(bf16[128,2048]{1,0:T(8,128)(2,1)S(1)} %copy-done.2), channel_id=1, source_target_pairs={{0,6},{1,7},{2,4},{3,5},{4,2},{5,3},{6,0},{7,1},{8,14},{9,15},{10,... | collective-permute-start | bytes 1572872 | tf_op jit(solution)/shard_map/ppermute | solution.py:417
  29.4 46.1 %collective-permute-done.14.refs_13_ = bf16[2048,128]{1,0:T(8,128)(2,1)S(1)} collective-permute-done((bf16[2048,128]{1,0:T(8,128)(2,1)S(1)}, bf16[2048,128]{1,0:T(8,128)(2,1)S(1)}, u32[]{:S(2)}, u32[]{:S(2)}) %collective-permute-start.14) | collective-permute-done | bytes 524320 | tf_op jit(solution)/shard_map/ppermute | solution.py:417
  75.4 4.3 %all-to-all-done = bf16[32,2,64,512]{3,2,1,0:T(8,128)(2,1)} async-done(((bf16[32,2,64,512]{3,2,1,0:T(8,128)(2,1)}), bf16[32,2,64,512]{3,2,1,0:T(8,128)(2,1)}, u32[]{:S(2)}, u32[]{:S(2)}) %all-to-all-start) | async-done | bytes 4194336 | tf_op jit(solution)/shard_map/all_to_all | solution.py:427
  79.7 2.3 %collective-permute-start = (bf16[64,64,512]{2,1,0:T(8,128)(2,1)}, bf16[64,64,512]{2,1,0:T(8,128)(2,1)}, u32[]{:S(2)}, u32[]{:S(2)}) collective-permute-start(bf16[64,64,512]{2,1,0:T(8,128)(2,1)} %bitcast.3.mine_ref.got_ref), channel_id=1, source_target_pairs={{0,1},{1,0},{2,3},{3,2},{4,5},{5,4},{6,7},{7,6},{8,9},{9,8},{10,11... | collective-permute-start | bytes 12582920 | tf_op jit(solution)/shard_map/ppermute | solution.py:417
  82.0 7.2 %resident.1 = (f32[256,256]{1,0:T(8,128)}, f32[8,256]{1,0:T(8,128)}, bf16[256,256]{1,0:T(8,128)(2,1)}) custom-call(s32[1]{0:T(128)S(6)} %select_n.7.half_ref, bf16[128,256]{1,0:T(8,128)(2,1)} %bitcast.18, bf16[128,256]{1,0:T(8,128)(2,1)} %copy-done.39, bf16[64,512]{1,0:T(8,128)(2,1)} %entry_ref.1, s32[16,256]{1,0:T(8,128)} %tile.18.tab_ref, ...), custom_call_target="tpu_custom_call" | custom-call | flops 3200000000 | bytes 16000000 | tf_op jit(solution)/shard_map/resident/pallas_call | solution.py:153
  92.2 6.4 %moved.1 = (f32[264,128]{1,0:T(8,128)S(1)}, f32[264,128]{1,0:T(8,128)S(1)}) custom-call(s32[1]{0:T(128)S(6)} %select_n.7.half_ref, bf16[256,256]{1,0:T(8,128)(2,1)S(1)} %copy-done.33, s32[16,256]{1,0:T(8,128)S(1)} %copy-done.27, s32[1,256]{1,0:T(1,128)S(1)} %copy-done.28, f32[256,256]{1,0:T(8,128)S(1)} %copy-done.32, f32[8,256]{1,0:T(8,128)S(1)} %copy-done.34, ...), custom_call_target="tpu_custom_call" | custom-call | flops 3200000000 | bytes 16000000 | tf_op jit(solution)/shard_map/moved/pallas_call | solution.py:209
  98.6 2.2 collective-permute-done.16.refs_15_
  100.9 1.3 collective-permute-start.2
  109.4 8.9 %collective-permute-done.20.refs_19_ = bf16[2048,128]{1,0:T(8,128)(2,1)S(1)} collective-permute-done((bf16[2048,128]{1,0:T(8,128)(2,1)S(1)}, bf16[2048,128]{1,0:T(8,128)(2,1)S(1)}, u32[]{:S(2)}, u32[]{:S(2)}) %collective-permute-start.20) | collective-permute-done | bytes 524320 | tf_op jit(solution)/shard_map/ppermute | solution.py:417
  118.8 10.7 %collective-permute-done.21.refs_20_ = bf16[2048,128]{1,0:T(8,128)(2,1)S(1)} collective-permute-done((bf16[2048,128]{1,0:T(8,128)(2,1)}, bf16[2048,128]{1,0:T(8,128)(2,1)S(1)}, u32[]{:S(2)}, u32[]{:S(2)}) %collective-permute-start.21) | collective-permute-done | bytes 524320 | tf_op jit(solution)/shard_map/ppermute | solution.py:417
  129.5 2.0 collective-permute-start.18
  131.6 9.2 %collective-permute-done.22.refs_21_ = bf16[128,2048]{1,0:T(8,128)(2,1)S(1)} collective-permute-done((bf16[128,2048]{1,0:T(8,128)(2,1)}, bf16[128,2048]{1,0:T(8,128)(2,1)S(1)}, u32[]{:S(2)}, u32[]{:S(2)}) %collective-permute-start.22) | collective-permute-done | bytes 524320 | tf_op jit(solution)/shard_map/ppermute | solution.py:417
  140.8 2.0 collective-permute-start.19
  146.0 6.8 %all-to-all-start.1 = ((bf16[16,16,2048]{2,1,0:T(8,128)(2,1)}), bf16[16,16,2048]{2,1,0:T(8,128)(2,1)S(1)}, u32[]{:S(2)}, u32[]{:S(2)}) async-start(bf16[16,16,2048]{2,1,0:T(8,128)(2,1)} %get-tuple-element.18), calls=%async_computation.1 | async-start | bytes 2097152 | tf_op jit(solution)/shard_map/all_to_all | solution.py:427
  158.2 11.8 %all-to-all-done.1 = bf16[16,16,2048]{2,1,0:T(8,128)(2,1)S(1)} async-done(((bf16[16,16,2048]{2,1,0:T(8,128)(2,1)}), bf16[16,16,2048]{2,1,0:T(8,128)(2,1)S(1)}, u32[]{:S(2)}, u32[]{:S(2)}) %all-to-all-start.1) | async-done | bytes 1048608 | tf_op jit(solution)/shard_map/all_to_all | solution.py:427
  182.5 6.5 %ffn.1 = bf16[256,2048]{1,0:T(8,128)(2,1)S(1)} custom-call(bf16[256,2048]{1,0:T(8,128)(2,1)S(1)} %bitcast.13, bf16[2048,128]{1,0:T(8,128)(2,1)S(1)} %copy-done, bf16[2048,128]{1,0:T(8,128)(2,1)S(1)} %copy-done.1, bf16[128,2048]{1,0:T(8,128)(2,1)S(1)} %copy-done.2, bf16[2048,128]{1,0:T(8,128)(2,1)S(1)} %copy-done.6, bf16[2048,128]{1,0:T(8,128)(2,1)S(1)} %copy-done.8, ...), custom_call_target="tpu_custom_call" | custom-call | flops 3200000000 | bytes 16000000 | tf_op jit(solution)/shard_map/ffn/pallas_call | solution.py:348
  189.0 20.0 %all_to_all.15.parts_ref = bf16[16,16,2048]{2,1,0:T(8,128)(2,1)S(1)} all-to-all(bf16[16,16,2048]{2,1,0:T(8,128)(2,1)S(1)} %bitcast.14), channel_id=1, replica_groups={{0,8,16,24,32,40,48,56,64,72,80,88,96,104,112,120},{1,9,17,25,33,41,49,..., dimensions={0} | all-to-all | bytes 2097152 | tf_op jit(solution)/shard_map/all_to_all | solution.py:427
  209.1 7.5 %all_gather.3 = bf16[64,2048]{1,0:T(8,128)(2,1)S(1)} all-gather(bf16[16,2048]{1,0:T(8,128)(2,1)S(1)} %finish.1), channel_id=1, replica_groups=mesh['dp'=32,'mp'=4] {'mp'}, dimensions={0}, use_global_device_ids=true | all-gather | bytes 327680 | tf_op jit(solution)/shard_map/all_gather | solution.py:474
  216.6 8.9 %assemble.1 = bf16[64,128,512]{2,1,0:T(8,128)(2,1)} custom-call(s32[1]{0:T(128)S(6)} %select_n.7.half_ref, bf16[64,64,512]{2,1,0:T(8,128)(2,1)} %bitcast.3.mine_ref.got_ref, bf16[64,64,512]{2,1,0:T(8,128)(2,1)} %collective-permute-done.peer_ref), custom_call_target="tpu_custom_call" | custom-call | flops 2400000000 | bytes 12000000 | tf_op jit(solution)/shard_map/assemble/pallas_call | solution.py:390
  (132 shorter events, 35.7 us)
Async XLA Ops:
  7.6 72.1 %all-to-all-start = ((bf16[32,2,64,512]{3,2,1,0:T(8,128)(2,1)}), bf16[32,2,64,512]{3,2,1,0:T(8,128)(2,1)}, u32[]{:S(2)}, u32[]{:S(2)}) async-start(bf16[32,2,64,512]{3,2,1,0:T(8,128)(2,1)} %bitcast.16), calls=%async_computation | async-start | bytes 8388608 | tf_op jit(solution)/shard_map/all_to_all | solution.py:427
  19.3 56.1 %collective-permute-start.14 = (bf16[2048,128]{1,0:T(8,128)(2,1)S(1)}, bf16[2048,128]{1,0:T(8,128)(2,1)S(1)}, u32[]{:S(2)}, u32[]{:S(2)}) collective-permute-start(bf16[2048,128]{1,0:T(8,128)(2,1)S(1)} %copy-done), channel_id=1, source_target_pairs={{0,6},{1,7},{2,4},{3,5},{4,2},{5,3},{6,0},{7,1},{8,14},{9,15},{10,... | collective-permute-start | bytes 1572872 | tf_op jit(solution)/shard_map/ppermute | solution.py:417
  21.7 67.9 %collective-permute-start.15 = (bf16[2048,128]{1,0:T(8,128)(2,1)S(1)}, bf16[2048,128]{1,0:T(8,128)(2,1)}, u32[]{:S(2)}, u32[]{:S(2)}) collective-permute-start(bf16[2048,128]{1,0:T(8,128)(2,1)S(1)} %copy-done.1), channel_id=1, source_target_pairs={{0,6},{1,7},{2,4},{3,5},{4,2},{5,3},{6,0},{7,1},{8,14},{9,15},{10,... | collective-permute-start | bytes 1572872 | tf_op jit(solution)/shard_map/ppermute | solution.py:417
  22.2 4.5 %collective-permute-start.1 = (bf16[128,256]{1,0:T(8,128)(2,1)S(1)}, bf16[128,256]{1,0:T(8,128)(2,1)S(1)}, u32[]{:S(2)}, u32[]{:S(2)}) collective-permute-start(bf16[128,256]{1,0:T(8,128)(2,1)S(1)} %bitcast.17), channel_id=1, source_target_pairs={{0,1},{1,0},{2,3},{3,2},{4,5},{5,4},{6,7},{7,6},{8,9},{9,8},{10,11... | collective-permute-start | bytes 196616 | tf_op jit(solution)/shard_map/ppermute | solution.py:417
  23.9 78.3 %collective-permute-start.8 = (bf16[2048,128]{1,0:T(8,128)(2,1)S(1)}, bf16[2048,128]{1,0:T(8,128)(2,1)}, u32[]{:S(2)}, u32[]{:S(2)}) collective-permute-start(bf16[2048,128]{1,0:T(8,128)(2,1)S(1)} %copy-done), channel_id=1, source_target_pairs={{0,2},{1,3},{2,0},{3,1},{4,6},{5,7},{6,4},{7,5},{8,10},{9,11},{10,... | collective-permute-start | bytes 1572872 | tf_op jit(solution)/shard_map/ppermute | solution.py:417
  23.9 78.3 %collective-permute-start.9 = (bf16[2048,128]{1,0:T(8,128)(2,1)S(1)}, bf16[2048,128]{1,0:T(8,128)(2,1)}, u32[]{:S(2)}, u32[]{:S(2)}) collective-permute-start(bf16[2048,128]{1,0:T(8,128)(2,1)S(1)} %copy-done.1), channel_id=1, source_target_pairs={{0,2},{1,3},{2,0},{3,1},{4,6},{5,7},{6,4},{7,5},{8,10},{9,11},{10,... | collective-permute-start | bytes 1572872 | tf_op jit(solution)/shard_map/ppermute | solution.py:417
  26.6 74.2 %collective-permute-start.16 = (bf16[128,2048]{1,0:T(8,128)(2,1)S(1)}, bf16[128,2048]{1,0:T(8,128)(2,1)}, u32[]{:S(2)}, u32[]{:S(2)}) collective-permute-start(bf16[128,2048]{1,0:T(8,128)(2,1)S(1)} %copy-done.2), channel_id=1, source_target_pairs={{0,6},{1,7},{2,4},{3,5},{4,2},{5,3},{6,0},{7,1},{8,14},{9,15},{10,... | collective-permute-start | bytes 1572872 | tf_op jit(solution)/shard_map/ppermute | solution.py:417
  79.7 136.9 %collective-permute-start = (bf16[64,64,512]{2,1,0:T(8,128)(2,1)}, bf16[64,64,512]{2,1,0:T(8,128)(2,1)}, u32[]{:S(2)}, u32[]{:S(2)}) collective-permute-start(bf16[64,64,512]{2,1,0:T(8,128)(2,1)} %bitcast.3.mine_ref.got_ref), channel_id=1, source_target_pairs={{0,1},{1,0},{2,3},{3,2},{4,5},{5,4},{6,7},{7,6},{8,9},{9,8},{10,11... | collective-permute-start | bytes 12582920 | tf_op jit(solution)/shard_map/ppermute | solution.py:417
  89.6 14.5 %collective-permute-start.10 = (bf16[128,2048]{1,0:T(8,128)(2,1)S(1)}, bf16[128,2048]{1,0:T(8,128)(2,1)S(1)}, u32[]{:S(2)}, u32[]{:S(2)}) collective-permute-start(bf16[128,2048]{1,0:T(8,128)(2,1)S(1)} %copy-done.2), channel_id=1, source_target_pairs={{0,2},{1,3},{2,0},{3,1},{4,6},{5,7},{6,4},{7,5},{8,10},{9,11},{10,... | collective-permute-start | bytes 1572872 | tf_op jit(solution)/shard_map/ppermute | solution.py:417
  102.2 3.5 %collective-permute-start.6 = (bf16[2048,128]{1,0:T(8,128)(2,1)S(1)}, bf16[2048,128]{1,0:T(8,128)(2,1)S(1)}, u32[]{:S(2)}, u32[]{:S(2)}) collective-permute-start(bf16[2048,128]{1,0:T(8,128)(2,1)S(1)} %copy-done.1), channel_id=1, source_target_pairs={{0,1},{1,0},{2,3},{3,2},{4,5},{5,4},{6,7},{7,6},{8,9},{9,8},{10,11... | collective-permute-start | bytes 1572872 | tf_op jit(solution)/shard_map/ppermute | solution.py:417
  103.2 4.0 %collective-permute-start.7 = (bf16[128,2048]{1,0:T(8,128)(2,1)S(1)}, bf16[128,2048]{1,0:T(8,128)(2,1)S(1)}, u32[]{:S(2)}, u32[]{:S(2)}) collective-permute-start(bf16[128,2048]{1,0:T(8,128)(2,1)S(1)} %copy-done.2), channel_id=1, source_target_pairs={{0,1},{1,0},{2,3},{3,2},{4,5},{5,4},{6,7},{7,6},{8,9},{9,8},{10,11... | collective-permute-start | bytes 1572872 | tf_op jit(solution)/shard_map/ppermute | solution.py:417
  104.2 4.7 %collective-permute-start.3 = (f32[2,16,2048]{2,1,0:T(8,128)S(1)}, f32[2,16,2048]{2,1,0:T(8,128)S(1)}, u32[]{:S(2)}, u32[]{:S(2)}) collective-permute-start(f32[2,16,2048]{2,1,0:T(8,128)S(1)} %get-tuple-element.17), channel_id=1, source_target_pairs={{0,1},{1,0},{2,3},{3,2},{4,5},{5,4},{6,7},{7,6},{8,9},{9,8},{10,11... | collective-permute-start | bytes 786440 | tf_op jit(solution)/shard_map/ppermute | solution.py:417
  105.2 13.1 %collective-permute-start.20 = (bf16[2048,128]{1,0:T(8,128)(2,1)S(1)}, bf16[2048,128]{1,0:T(8,128)(2,1)S(1)}, u32[]{:S(2)}, u32[]{:S(2)}) collective-permute-start(bf16[2048,128]{1,0:T(8,128)(2,1)S(1)} %collective-permute-done.14.refs_13_), channel_id=1, source_target_pairs={{0,2},{1,3},{2,0},{3,1},{4,6},{5,7},{6,4},{7,5},{8,10},{9,11},{10,... | collective-permute-start | bytes 1572872 | tf_op jit(solution)/shard_map/ppermute | solution.py:417
  106.5 36.3 %collective-permute-start.17 = (bf16[2048,128]{1,0:T(8,128)(2,1)S(1)}, bf16[2048,128]{1,0:T(8,128)(2,1)S(1)}, u32[]{:S(2)}, u32[]{:S(2)}) collective-permute-start(bf16[2048,128]{1,0:T(8,128)(2,1)S(1)} %collective-permute-done.14.refs_13_), channel_id=1, source_target_pairs={{0,1},{1,0},{2,3},{3,2},{4,5},{5,4},{6,7},{7,6},{8,9},{9,8},{10,11... | collective-permute-start | bytes 1572872 | tf_op jit(solution)/shard_map/ppermute | solution.py:417
  107.9 21.6 %collective-permute-start.21 = (bf16[2048,128]{1,0:T(8,128)(2,1)}, bf16[2048,128]{1,0:T(8,128)(2,1)S(1)}, u32[]{:S(2)}, u32[]{:S(2)}) collective-permute-start(bf16[2048,128]{1,0:T(8,128)(2,1)} %collective-permute-done.15.refs_14_), channel_id=1, source_target_pairs={{0,2},{1,3},{2,0},{3,1},{4,6},{5,7},{6,4},{7,5},{8,10},{9,11},{10,... | collective-permute-start | bytes 1572872 | tf_op jit(solution)/shard_map/ppermute | solution.py:417
  108.9 31.9 %collective-permute-start.22 = (bf16[128,2048]{1,0:T(8,128)(2,1)}, bf16[128,2048]{1,0:T(8,128)(2,1)S(1)}, u32[]{:S(2)}, u32[]{:S(2)}) collective-permute-start(bf16[128,2048]{1,0:T(8,128)(2,1)} %collective-permute-done.16.refs_15_), channel_id=1, source_target_pairs={{0,2},{1,3},{2,0},{3,1},{4,6},{5,7},{6,4},{7,5},{8,10},{9,11},{10,... | collective-permute-start | bytes 1572872 | tf_op jit(solution)/shard_map/ppermute | solution.py:417
  118.3 25.3 %collective-permute-start.4 = (f32[16,2048]{1,0:T(8,128)S(1)}, f32[16,2048]{1,0:T(8,128)S(1)}, u32[]{:S(2)}, u32[]{:S(2)}) collective-permute-start(f32[16,2048]{1,0:T(8,128)S(1)} %fusion), channel_id=1, source_target_pairs={{0,2},{1,3},{2,0},{3,1},{4,6},{5,7},{6,4},{7,5},{8,10},{9,11},{10,... | collective-permute-start | bytes 393224 | tf_op jit(solution)/shard_map/ppermute | solution.py:417
  129.5 23.2 %collective-permute-start.18 = (bf16[2048,128]{1,0:T(8,128)(2,1)}, bf16[2048,128]{1,0:T(8,128)(2,1)}, u32[]{:S(2)}, u32[]{:S(2)}) collective-permute-start(bf16[2048,128]{1,0:T(8,128)(2,1)} %collective-permute-done.15.refs_14_), channel_id=1, source_target_pairs={{0,1},{1,0},{2,3},{3,2},{4,5},{5,4},{6,7},{7,6},{8,9},{9,8},{10,11... | collective-permute-start | bytes 1572872 | tf_op jit(solution)/shard_map/ppermute | solution.py:417
  140.8 12.4 %collective-permute-start.19 = (bf16[128,2048]{1,0:T(8,128)(2,1)}, bf16[128,2048]{1,0:T(8,128)(2,1)}, u32[]{:S(2)}, u32[]{:S(2)}) collective-permute-start(bf16[128,2048]{1,0:T(8,128)(2,1)} %collective-permute-done.16.refs_15_), channel_id=1, source_target_pairs={{0,1},{1,0},{2,3},{3,2},{4,5},{5,4},{6,7},{7,6},{8,9},{9,8},{10,11... | collective-permute-start | bytes 1572872 | tf_op jit(solution)/shard_map/ppermute | solution.py:417
  143.6 9.8 %collective-permute-start.11 = (bf16[2048,128]{1,0:T(8,128)(2,1)}, bf16[2048,128]{1,0:T(8,128)(2,1)}, u32[]{:S(2)}, u32[]{:S(2)}) collective-permute-start(bf16[2048,128]{1,0:T(8,128)(2,1)} %collective-permute-done.8.refs_7_), channel_id=1, source_target_pairs={{0,1},{1,0},{2,3},{3,2},{4,5},{5,4},{6,7},{7,6},{8,9},{9,8},{10,11... | collective-permute-start | bytes 1572872 | tf_op jit(solution)/shard_map/ppermute | solution.py:417
  143.6 10.0 %collective-permute-start.12 = (bf16[2048,128]{1,0:T(8,128)(2,1)}, bf16[2048,128]{1,0:T(8,128)(2,1)}, u32[]{:S(2)}, u32[]{:S(2)}) collective-permute-start(bf16[2048,128]{1,0:T(8,128)(2,1)} %collective-permute-done.9.refs_8_), channel_id=1, source_target_pairs={{0,1},{1,0},{2,3},{3,2},{4,5},{5,4},{6,7},{7,6},{8,9},{9,8},{10,11... | collective-permute-start | bytes 1572872 | tf_op jit(solution)/shard_map/ppermute | solution.py:417
  146.0 24.1 %all-to-all-start.1 = ((bf16[16,16,2048]{2,1,0:T(8,128)(2,1)}), bf16[16,16,2048]{2,1,0:T(8,128)(2,1)S(1)}, u32[]{:S(2)}, u32[]{:S(2)}) async-start(bf16[16,16,2048]{2,1,0:T(8,128)(2,1)} %get-tuple-element.18), calls=%async_computation.1 | async-start | bytes 2097152 | tf_op jit(solution)/shard_map/all_to_all | solution.py:427
  153.4 3.2 %collective-permute-start.24 = (bf16[2048,128]{1,0:T(8,128)(2,1)}, bf16[2048,128]{1,0:T(8,128)(2,1)S(1)}, u32[]{:S(2)}, u32[]{:S(2)}) collective-permute-start(bf16[2048,128]{1,0:T(8,128)(2,1)} %copy-done.15), channel_id=1, source_target_pairs={{0,1},{1,0},{2,3},{3,2},{4,5},{5,4},{6,7},{7,6},{8,9},{9,8},{10,11... | collective-permute-start | bytes 1572872 | tf_op jit(solution)/shard_map/ppermute | solution.py:417
  153.7 3.7 %collective-permute-start.25 = (bf16[128,2048]{1,0:T(8,128)(2,1)}, bf16[128,2048]{1,0:T(8,128)(2,1)S(1)}, u32[]{:S(2)}, u32[]{:S(2)}) collective-permute-start(bf16[128,2048]{1,0:T(8,128)(2,1)} %copy-done.17), channel_id=1, source_target_pairs={{0,1},{1,0},{2,3},{3,2},{4,5},{5,4},{6,7},{7,6},{8,9},{9,8},{10,11... | collective-permute-start | bytes 1572872 | tf_op jit(solution)/shard_map/ppermute | solution.py:417
  (44 other events, 447.3 us)

commit v4 on v3

--- a/solution.py
+++ b/solution.py
@@ -25,7 +25,7 @@
     first = pl.multiple_of(half_ref[0] * rows, rows)
 
     def copy(i):
-        src = pool_ref.at[slot_ref[i], pl.ds(first, rows), :]
+        src = pool_ref.at[slot_ref[i // caps, i % caps], pl.ds(first, rows), :]
         return pltpu.make_async_copy(src, out_ref.at[i], sems.at[i])
 
     copies = [copy(i) for i in range(pages)]
@@ -40,14 +40,14 @@
 
 
 def outgoing_pages(half, slots, counts, pool):
-    pages = slots.shape[0]
+    pages = slots.size
     rows = pool.shape[1] // 2
     return pl.pallas_call(
         outgoing_kernel,
         grid_spec=pltpu.PrefetchScalarGridSpec(
             num_scalar_prefetch=3,
             grid=(1,),
-            in_specs=[pl.BlockSpec(memory_space=pl.ANY)],
+            in_specs=[pl.BlockSpec(memory_space=pltpu.HBM)],
             out_specs=pl.BlockSpec((pages, rows, pool.shape[2]), lambda i, *_: (0, 0, 0)),
             scratch_shapes=[pltpu.SemaphoreType.DMA((pages,))],
         ),
@@ -110,16 +110,28 @@
 
 def resident_kernel(
     half_ref, qa_ref, qb_ref, entry_ref, tab_ref, len_ref, pool_ref,
-    acc_ref, stat_ref, qt_ref, full, part,
+    acc_ref, stat_ref, qt_ref, full, part, held, sems,
 ):
     i = pl.program_id(0)
-    pages, rows, width = pool_ref.shape
+    steps = sems.shape[0]
+    slots, rows, width = held.shape
+    pages = slots // steps
     hd = width // 2
+    first = pl.multiple_of(half_ref[0] * rows, rows)
+
+    def load(k):
+        at = pl.ds(k * pages, pages)
+        return pltpu.make_async_copy(
+            pool_ref.at[at, pl.ds(first, rows), :], held.at[at], sems.at[k]
+        )
+
     mine = qa_ref.shape[0]
     games = entry_ref.shape[0]
 
     @pl.when(i == 0)
     def _():
+        for k in range(steps):
+            load(k).start()
         q = jnp.concatenate([qa_ref[...], qb_ref[...]], axis=0)
         qt_ref[...] = q.T
         tables(0, half_ref[0], rows, tab_ref, len_ref, full, part)
@@ -135,7 +147,9 @@
             entry_ref[:, hd:], p.astype(BF), (((0,), (0,)), ((), ())), preferred_element_type=F32
         )
 
-    chunk_step(pool_ref, i * pages, qt_ref, full, part, acc_ref, stat_ref)
+    load(i).wait()
+    at = pl.ds(pl.multiple_of(i * pages, pages), pages)
+    chunk_step(held.at[at], i * pages, qt_ref, full, part, acc_ref, stat_ref)
 
 
 def resident(half, q_mine, q_peer, entry, table, lengths, pool):
@@ -161,16 +175,18 @@
                 whole(entry.shape),
                 whole(table.shape),
                 whole(lengths.shape),
-                pl.BlockSpec((block, rows, width), lambda i, h: (i, h[0], 0)),
+                pl.BlockSpec(memory_space=pltpu.HBM),
             ],
             out_specs=[whole(o.shape) for o in outs],
             scratch_shapes=[
                 pltpu.VMEM((slots, lanes), F32),
                 pltpu.VMEM((slots, lanes), jnp.int32),
+                pltpu.VMEM((slots, rows, width), BF),
+                pltpu.SemaphoreType.DMA((slots // block,)),
             ],
         ),
         out_shape=outs,
-        compiler_params=params(60),
+        compiler_params=params(57),
         cost_estimate=cost(8),
         name="resident",
     )(half, q_mine, q_peer, entry, table, lengths, pool)
@@ -228,7 +244,7 @@
             ],
         ),
         out_shape=[out, out],
-        compiler_params=params(20),
+        compiler_params=params(60),
         cost_estimate=cost(8),
         name="moved",
     )(half, qt, table, lengths, acc, stat, got)
@@ -319,25 +335,47 @@
 
 
 def ffn_kernel(*refs):
-    n = (len(refs) - 3) // 3
+    n = (len(refs) - 6) // 3
     x_ref = refs[0]
     w = [refs[1 + 3 * b : 4 + 3 * b] for b in range(n)]
-    out_ref, hid = refs[1 + 3 * n :]
-    unit = w[0][0].shape[1]
-    for b, (g, u, _) in enumerate(w):
-        both = jnp.dot(
-            x_ref[...], jnp.concatenate([g[...], u[...]], axis=1), preferred_element_type=F32
+    out_ref, gu, down, hid, sems = refs[1 + 3 * n :]
+    unit = gu.shape[2] // 2
+
+    def loads(b):
+        g, u, d = w[b]
+        return (
+            pltpu.make_async_copy(g, gu.at[b, :, pl.ds(0, unit)], sems.at[3 * b]),
+            pltpu.make_async_copy(u, gu.at[b, :, pl.ds(unit, unit)], sems.at[3 * b + 1]),
+            pltpu.make_async_copy(d, down.at[pl.ds(b * unit, unit), :], sems.at[3 * b + 2]),
         )
+
+    copies = [loads(b) for b in range(n)]
+    gates = [c for block in copies for c in block[:2]]
+    downs = [block[2] for block in copies]
+    queue = gates + downs
+    ahead = 4
+    for c in queue[:ahead]:
+        c.start()
+    for b in range(n):
+        for k in (2 * b, 2 * b + 1):
+            queue[k].wait()
+            queue[k + ahead].start()
+        both = jnp.dot(x_ref[...], gu[b], preferred_element_type=F32)
         hid[:, b * unit : (b + 1) * unit] = (
             jax.nn.gelu(both[:, :unit], approximate=True) * both[:, unit:]
         ).astype(BF)
+    for c in queue[2 * n + ahead :]:
+        c.start()
+    for c in downs:
+        c.wait()
     cols = 512
 
     @pl.loop(0, out_ref.shape[1] // cols)
     def _(k):
         at = pl.ds(pl.multiple_of(k * cols, cols), cols)
-        down = jnp.concatenate([d[:, at] for _, _, d in w], axis=0)
-        out_ref[:, at] = jnp.dot(hid[...], down, preferred_element_type=F32).astype(BF)
+        out_ref[:, at] = jnp.dot(
+            hid[...], down[:, at], preferred_element_type=F32
+        ).astype(BF)
 
 
 def ffn(x, weights):
@@ -347,11 +385,16 @@
     vmem = pl.BlockSpec(memory_space=pltpu.VMEM)
     return pl.pallas_call(
         ffn_kernel,
-        in_specs=[vmem] * (1 + 3 * n),
+        in_specs=[vmem] + [pl.BlockSpec(memory_space=pl.ANY)] * (3 * n),
         out_specs=vmem,
         out_shape=jax.ShapeDtypeStruct((rows, d), BF),
-        scratch_shapes=[pltpu.VMEM((rows, n * unit), BF)],
-        compiler_params=params(24),
+        scratch_shapes=[
+            pltpu.VMEM((n, d, 2 * unit), BF),
+            pltpu.VMEM((n * unit, d), BF),
+            pltpu.VMEM((rows, n * unit), BF),
+            pltpu.SemaphoreType.DMA((3 * n,)),
+        ],
+        compiler_params=params(60),
         cost_estimate=cost(8),
         name="ffn",
     )(x, *[a for block in weights for a in block])
@@ -428,7 +471,7 @@
         a, axes, 0, 0, tiled=True, axis_index_groups=who
     )
 
-    out_pages = outgoing_pages(half, send_slots.reshape(-1), move_count.reshape(-1), page_pool)
+    out_pages = outgoing_pages(half, send_slots, move_count.reshape(-1), page_pool)
     got = exchange(
         out_pages.reshape(n_dp, -1, page_len // 2, width), groups
     ).reshape(out_pages.shape)
@@ -446,8 +489,12 @@
     w_side = each(weights, side)
     w_core = each(weights, core)
     w_side_core = each(w_side, core)
-    w_far = each(weights, far)
-    w_diag = each(w_far, side)
+    far_up, far_down, far_gate = (send(weights[k], far) for k in (1, 2, 0))
+    w_far = (far_gate, far_up, far_down)
+    diag_gate = send(w_side[0], far)
+    diag_up = send(far_up, side)
+    diag_down = send(far_down, side)
+    w_diag = (diag_gate, diag_up, diag_down)
     w_far_core = each(w_far, core)
     w_diag_core = each(w_diag, core)
     blocks = [

time: 228 us -> 209 us (0.917)
  local copies, waits for them, and re-layouts: 24.9 us -> 6.21 us
  starting transfers between devices: 41.3 us -> 31.4 us
  Pallas kernels: 36.3 us -> 43.6 us
  waiting for transfers between devices: 95.2 us -> 98.4 us
    all_to_all x2, waiting for transfers between devices: 16.1 us -> 61.5 us  [step(): lax.all_to_all(a, axes, 0, 0, tiled=True, axis_index_groups=who)]
    ppermute x26, waiting for transfers between devices: 79.1 us -> 36.9 us  [step(): send = lambda a, pairs: lax.ppermute(a, axes, pairs)]
    unnamed x82 -> x52, local copies, waits for them, and re-layouts: 22.9 us -> 4.87 us
    ppermute x26, starting transfers between devices: 22.9 us -> 16.1 us  [step(): send = lambda a, pairs: lax.ppermute(a, axes, pairs)]
    pallas_call x1, Pallas kernels: 6.45 us -> 12.2 us  [ffn(): pl.pallas_call(ffn_kernel, in_specs=[vmem] + [pl.BlockSpec(memory_space=p...]
    all_to_all x2, starting transfers between devices: 18.5 us -> 15.3 us  [step(): lax.all_to_all(a, axes, 0, 0, tiled=True, axis_index_groups=who)]
  transfers between devices with their start and end apart: 28 -> 28, of which waited for: 10 -> 12; matrix products, arithmetic and copies ran while one was open for 1% -> 1% of each run, Pallas kernels for 10% -> 14%
where the time goes in v4:
time: 209 us; the launch traced here: 208 us
  waiting for transfers between devices  98.4 us (47%)
  Pallas kernels  43.6 us (21%)
  starting transfers between devices  31.4 us (15%)
  blocking collectives  27.3 us (13%)
  local copies, waits for them, and re-layouts  6.21 us (3%)
    all_to_all x2, waiting for transfers between devices, step(): lax.all_to_all(a, axes, 0, 0, tiled=True, axis_index_groups=who)  61.5 us
    ppermute x26, waiting for transfers between devices, step(): send = lambda a, pairs: lax.ppermute(a, axes, pairs)  36.9 us
    all_to_all x1, blocking collectives, step(): lax.all_to_all(a, axes, 0, 0, tiled=True, axis_index_groups=who)  19.6 us
    ppermute x26, starting transfers between devices, step(): send = lambda a, pairs: lax.ppermute(a, axes, pairs)  16.1 us
    all_to_all x2, starting transfers between devices, step(): lax.all_to_all(a, axes, 0, 0, tiled=True, axis_index_groups=who)  15.3 us
    pallas_call x1, Pallas kernels, ffn(): pl.pallas_call(ffn_kernel, in_specs=[vmem] + [pl.BlockSpec(memory_space=p...  12.2 us
    pallas_call x1, Pallas kernels, assemble(): pl.pallas_call(assemble_kernel, grid_spec=pltpu.PrefetchScalarGridSpec(nu...  8.87 us
    all_gather x1, blocking collectives, step(): layer_out = lax.all_gather(quarter, 'mp', axis=0, tiled=True)  7.71 us
  transfers between devices with their start and end apart: 28, of which 12 were waited for; matrix products, arithmetic and copies ran while one was open for 1% of the time, Pallas kernels for 14%

profile of v4, /device:TPU:1, one launch (start us, length us, event | category | flops | bytes accessed | tf_op | source)
XLA Modules:
  0.0 208.0 jit_solution(10319126880235852250)
XLA Ops:
  0.6 1.4 copy.15.slot_ref
  2.0 5.8 %outgoing.1 = bf16[64,64,512]{2,1,0:T(8,128)(2,1)} custom-call(s32[1]{0:T(128)S(6)} %select_n.7.half_ref, s32[32,2]{1,0:T(8,128)} %copy.15.slot_ref, s32[32]{0:T(128)} %bitcast.20, bf16[64,128,512]{2,1,0:T(8,128)(2,1)} %pool_ref.3), custom_call_target="tpu_custom_call" | custom-call | flops 1200000000 | bytes 6000000 | tf_op jit(solution)/shard_map/outgoing/pallas_call | solution.py:45
  7.9 11.7 %all-to-all-start = ((bf16[32,2,64,512]{3,2,1,0:T(8,128)(2,1)}), bf16[32,2,64,512]{3,2,1,0:T(8,128)(2,1)}, u32[]{:S(2)}, u32[]{:S(2)}) async-start(bf16[32,2,64,512]{3,2,1,0:T(8,128)(2,1)} %bitcast.14), calls=%async_computation | async-start | bytes 8388608 | tf_op jit(solution)/shard_map/all_to_all | solution.py:470
  19.6 2.4 %collective-permute-start.15 = (bf16[2048,128]{1,0:T(8,128)(2,1)S(1)}, bf16[2048,128]{1,0:T(8,128)(2,1)}, u32[]{:S(2)}, u32[]{:S(2)}) collective-permute-start(bf16[2048,128]{1,0:T(8,128)(2,1)S(1)} %copy-done.6), channel_id=1, source_target_pairs={{0,6},{1,7},{2,4},{3,5},{4,2},{5,3},{6,0},{7,1},{8,14},{9,15},{10,... | collective-permute-start | bytes 1572872 | tf_op jit(solution)/shard_map/ppermute | solution.py:460
  22.2 1.7 collective-permute-start.1
  23.9 1.0 collective-permute-start.9
  26.7 5.4 %collective-permute-done.8.refs_7_ = bf16[2048,128]{1,0:T(8,128)(2,1)S(1)} collective-permute-done((bf16[2048,128]{1,0:T(8,128)(2,1)S(1)}, bf16[2048,128]{1,0:T(8,128)(2,1)S(1)}, u32[]{:S(2)}, u32[]{:S(2)}) %collective-permute-start.8) | collective-permute-done | bytes 524320 | tf_op jit(solution)/shard_map/ppermute | solution.py:460
  32.2 47.8 %all-to-all-done = bf16[32,2,64,512]{3,2,1,0:T(8,128)(2,1)} async-done(((bf16[32,2,64,512]{3,2,1,0:T(8,128)(2,1)}), bf16[32,2,64,512]{3,2,1,0:T(8,128)(2,1)}, u32[]{:S(2)}, u32[]{:S(2)}) %all-to-all-start) | async-done | bytes 4194336 | tf_op jit(solution)/shard_map/all_to_all | solution.py:470
  80.0 2.3 %collective-permute-start = (bf16[64,64,512]{2,1,0:T(8,128)(2,1)}, bf16[64,64,512]{2,1,0:T(8,128)(2,1)}, u32[]{:S(2)}, u32[]{:S(2)}) collective-permute-start(bf16[64,64,512]{2,1,0:T(8,128)(2,1)} %bitcast.3.mine_ref.got_ref), channel_id=1, source_target_pairs={{0,1},{1,0},{2,3},{3,2},{4,5},{5,4},{6,7},{7,6},{8,9},{9,8},{10,11... | collective-permute-start | bytes 12582920 | tf_op jit(solution)/shard_map/ppermute | solution.py:460
  82.3 7.6 %resident.1 = (f32[256,256]{1,0:T(8,128)}, f32[8,256]{1,0:T(8,128)}, bf16[256,256]{1,0:T(8,128)(2,1)}) custom-call(s32[1]{0:T(128)S(6)} %select_n.7.half_ref, bf16[128,256]{1,0:T(8,128)(2,1)} %bitcast.18, bf16[128,256]{1,0:T(8,128)(2,1)} %copy-done.24, bf16[64,512]{1,0:T(8,128)(2,1)} %entry_ref.1, s32[16,256]{1,0:T(8,128)} %tile.18.tab_ref, ...), custom_call_target="tpu_custom_call" | custom-call | flops 3200000000 | bytes 16000000 | tf_op jit(solution)/shard_map/resident/pallas_call | solution.py:167
  90.0 7.2 %moved.1 = (f32[264,128]{1,0:T(8,128)}, f32[264,128]{1,0:T(8,128)}) custom-call(s32[1]{0:T(128)S(6)} %select_n.7.half_ref, bf16[256,256]{1,0:T(8,128)(2,1)} %get-tuple-element.11.qt_ref, s32[16,256]{1,0:T(8,128)} %tile.18.tab_ref, s32[1,256]{1,0:T(1,128)} %tile.20.len_ref, f32[256,256]{1,0:T(8,128)} %get-tuple-element.12.acc_in, ...), custom_call_target="tpu_custom_call" | custom-call | flops 3200000000 | bytes 16000000 | tf_op jit(solution)/shard_map/moved/pallas_call | solution.py:225
  100.5 4.2 %collective-permute-done.14.refs_13_ = bf16[2048,128]{1,0:T(8,128)(2,1)} collective-permute-done((bf16[2048,128]{1,0:T(8,128)(2,1)S(1)}, bf16[2048,128]{1,0:T(8,128)(2,1)}, u32[]{:S(2)}, u32[]{:S(2)}) %collective-permute-start.14) | collective-permute-done | bytes 524320 | tf_op jit(solution)/shard_map/ppermute | solution.py:460
  107.5 12.9 %collective-permute-done.20.refs_19_ = bf16[2048,128]{1,0:T(8,128)(2,1)S(1)} collective-permute-done((bf16[2048,128]{1,0:T(8,128)(2,1)S(1)}, bf16[2048,128]{1,0:T(8,128)(2,1)S(1)}, u32[]{:S(2)}, u32[]{:S(2)}) %collective-permute-start.20) | collective-permute-done | bytes 524320 | tf_op jit(solution)/shard_map/ppermute | solution.py:460
  121.4 9.3 %collective-permute-done.22.refs_21_ = bf16[128,2048]{1,0:T(8,128)(2,1)S(1)} collective-permute-done((bf16[128,2048]{1,0:T(8,128)(2,1)}, bf16[128,2048]{1,0:T(8,128)(2,1)S(1)}, u32[]{:S(2)}, u32[]{:S(2)}) %collective-permute-start.22) | collective-permute-done | bytes 524320 | tf_op jit(solution)/shard_map/ppermute | solution.py:460
  130.7 1.9 collective-permute-start.19
  133.5 1.2 collective-permute-start.13
  134.6 1.2 norm.1
  135.8 3.7 %all-to-all-start.1 = ((bf16[16,16,2048]{2,1,0:T(8,128)(2,1)}), bf16[16,16,2048]{2,1,0:T(8,128)(2,1)S(1)}, u32[]{:S(2)}, u32[]{:S(2)}) async-start(bf16[16,16,2048]{2,1,0:T(8,128)(2,1)} %get-tuple-element.18), calls=%async_computation.1 | async-start | bytes 2097152 | tf_op jit(solution)/shard_map/all_to_all | solution.py:470
  140.6 1.1 collective-permute-done.17.refs_16_
  144.1 13.7 %all-to-all-done.1 = bf16[16,16,2048]{2,1,0:T(8,128)(2,1)S(1)} async-done(((bf16[16,16,2048]{2,1,0:T(8,128)(2,1)}), bf16[16,16,2048]{2,1,0:T(8,128)(2,1)S(1)}, u32[]{:S(2)}, u32[]{:S(2)}) %all-to-all-start.1) | async-done | bytes 1048608 | tf_op jit(solution)/shard_map/all_to_all | solution.py:470
  158.7 12.2 %ffn.1 = bf16[256,2048]{1,0:T(8,128)(2,1)} custom-call(bf16[256,2048]{1,0:T(8,128)(2,1)} %bitcast.15, bf16[2048,128]{1,0:T(8,128)(2,1)} %refs_1_.1, bf16[2048,128]{1,0:T(8,128)(2,1)} %refs_2_.1, bf16[128,2048]{1,0:T(8,128)(2,1)} %refs_3_.1, bf16[2048,128]{1,0:T(8,128)(2,1)} %copy-done.10, bf16[2048,128]{1,0:T(8,128)(2,1)} %copy-done.11, ...), custom_call_target="tpu_custom_call" | custom-call | flops 3200000000 | bytes 16000000 | tf_op jit(solution)/shard_map/ffn/pallas_call | solution.py:386
  171.0 19.6 %all_to_all.15.parts_ref = bf16[16,16,2048]{2,1,0:T(8,128)(2,1)S(1)} all-to-all(bf16[16,16,2048]{2,1,0:T(8,128)(2,1)} %bitcast.16), channel_id=1, replica_groups={{0,8,16,24,32,40,48,56,64,72,80,88,96,104,112,120},{1,9,17,25,33,41,49,..., dimensions={0} | all-to-all | bytes 2097152 | tf_op jit(solution)/shard_map/all_to_all | solution.py:470
  190.8 7.7 %all_gather.3 = bf16[64,2048]{1,0:T(8,128)(2,1)S(1)} all-gather(bf16[16,2048]{1,0:T(8,128)(2,1)S(1)} %finish.1), channel_id=1, replica_groups=mesh['dp'=32,'mp'=4] {'mp'}, dimensions={0}, use_global_device_ids=true | all-gather | bytes 327680 | tf_op jit(solution)/shard_map/all_gather | solution.py:521
  198.5 8.9 %assemble.1 = bf16[64,128,512]{2,1,0:T(8,128)(2,1)} custom-call(s32[1]{0:T(128)S(6)} %select_n.7.half_ref, bf16[64,64,512]{2,1,0:T(8,128)(2,1)} %bitcast.3.mine_ref.got_ref, bf16[64,64,512]{2,1,0:T(8,128)(2,1)} %collective-permute-done.peer_ref), custom_call_target="tpu_custom_call" | custom-call | flops 2400000000 | bytes 12000000 | tf_op jit(solution)/shard_map/assemble/pallas_call | solution.py:433
  (101 shorter events, 15.2 us)
Async XLA Ops:
  7.9 72.1 %all-to-all-start = ((bf16[32,2,64,512]{3,2,1,0:T(8,128)(2,1)}), bf16[32,2,64,512]{3,2,1,0:T(8,128)(2,1)}, u32[]{:S(2)}, u32[]{:S(2)}) async-start(bf16[32,2,64,512]{3,2,1,0:T(8,128)(2,1)} %bitcast.14), calls=%async_computation | async-start | bytes 8388608 | tf_op jit(solution)/shard_map/all_to_all | solution.py:470
  19.5 12.6 %collective-permute-start.8 = (bf16[2048,128]{1,0:T(8,128)(2,1)S(1)}, bf16[2048,128]{1,0:T(8,128)(2,1)S(1)}, u32[]{:S(2)}, u32[]{:S(2)}) collective-permute-start(bf16[2048,128]{1,0:T(8,128)(2,1)S(1)} %copy-done.5), channel_id=1, source_target_pairs={{0,2},{1,3},{2,0},{3,1},{4,6},{5,7},{6,4},{7,5},{8,10},{9,11},{10,... | collective-permute-start | bytes 1572872 | tf_op jit(solution)/shard_map/ppermute | solution.py:460
  19.6 70.2 %collective-permute-start.15 = (bf16[2048,128]{1,0:T(8,128)(2,1)S(1)}, bf16[2048,128]{1,0:T(8,128)(2,1)}, u32[]{:S(2)}, u32[]{:S(2)}) collective-permute-start(bf16[2048,128]{1,0:T(8,128)(2,1)S(1)} %copy-done.6), channel_id=1, source_target_pairs={{0,6},{1,7},{2,4},{3,5},{4,2},{5,3},{6,0},{7,1},{8,14},{9,15},{10,... | collective-permute-start | bytes 1572872 | tf_op jit(solution)/shard_map/ppermute | solution.py:460
  22.2 4.4 %collective-permute-start.1 = (bf16[128,256]{1,0:T(8,128)(2,1)S(1)}, bf16[128,256]{1,0:T(8,128)(2,1)S(1)}, u32[]{:S(2)}, u32[]{:S(2)}) collective-permute-start(bf16[128,256]{1,0:T(8,128)(2,1)S(1)} %bitcast.17), channel_id=1, source_target_pairs={{0,1},{1,0},{2,3},{3,2},{4,5},{5,4},{6,7},{7,6},{8,9},{9,8},{10,11... | collective-permute-start | bytes 196616 | tf_op jit(solution)/shard_map/ppermute | solution.py:460
  23.9 73.5 %collective-permute-start.9 = (bf16[2048,128]{1,0:T(8,128)(2,1)S(1)}, bf16[2048,128]{1,0:T(8,128)(2,1)}, u32[]{:S(2)}, u32[]{:S(2)}) collective-permute-start(bf16[2048,128]{1,0:T(8,128)(2,1)S(1)} %copy-done.6), channel_id=1, source_target_pairs={{0,2},{1,3},{2,0},{3,1},{4,6},{5,7},{6,4},{7,5},{8,10},{9,11},{10,... | collective-permute-start | bytes 1572872 | tf_op jit(solution)/shard_map/ppermute | solution.py:460
  24.9 72.3 %collective-permute-start.16 = (bf16[128,2048]{1,0:T(8,128)(2,1)S(1)}, bf16[128,2048]{1,0:T(8,128)(2,1)}, u32[]{:S(2)}, u32[]{:S(2)}) collective-permute-start(bf16[128,2048]{1,0:T(8,128)(2,1)S(1)} %copy-done.7), channel_id=1, source_target_pairs={{0,6},{1,7},{2,4},{3,5},{4,2},{5,3},{6,0},{7,1},{8,14},{9,15},{10,... | collective-permute-start | bytes 1572872 | tf_op jit(solution)/shard_map/ppermute | solution.py:460
  26.6 71.2 %collective-permute-start.10 = (bf16[128,2048]{1,0:T(8,128)(2,1)S(1)}, bf16[128,2048]{1,0:T(8,128)(2,1)}, u32[]{:S(2)}, u32[]{:S(2)}) collective-permute-start(bf16[128,2048]{1,0:T(8,128)(2,1)S(1)} %copy-done.7), channel_id=1, source_target_pairs={{0,2},{1,3},{2,0},{3,1},{4,6},{5,7},{6,4},{7,5},{8,10},{9,11},{10,... | collective-permute-start | bytes 1572872 | tf_op jit(solution)/shard_map/ppermute | solution.py:460
  80.0 118.5 %collective-permute-start = (bf16[64,64,512]{2,1,0:T(8,128)(2,1)}, bf16[64,64,512]{2,1,0:T(8,128)(2,1)}, u32[]{:S(2)}, u32[]{:S(2)}) collective-permute-start(bf16[64,64,512]{2,1,0:T(8,128)(2,1)} %bitcast.3.mine_ref.got_ref), channel_id=1, source_target_pairs={{0,1},{1,0},{2,3},{3,2},{4,5},{5,4},{6,7},{7,6},{8,9},{9,8},{10,11... | collective-permute-start | bytes 12582920 | tf_op jit(solution)/shard_map/ppermute | solution.py:460
  89.9 14.9 %collective-permute-start.14 = (bf16[2048,128]{1,0:T(8,128)(2,1)S(1)}, bf16[2048,128]{1,0:T(8,128)(2,1)}, u32[]{:S(2)}, u32[]{:S(2)}) collective-permute-start(bf16[2048,128]{1,0:T(8,128)(2,1)S(1)} %copy-done.5), channel_id=1, source_target_pairs={{0,6},{1,7},{2,4},{3,5},{4,2},{5,3},{6,0},{7,1},{8,14},{9,15},{10,... | collective-permute-start | bytes 1572872 | tf_op jit(solution)/shard_map/ppermute | solution.py:460
  97.3 8.3 %collective-permute-start.5 = (bf16[2048,128]{1,0:T(8,128)(2,1)S(1)}, bf16[2048,128]{1,0:T(8,128)(2,1)S(1)}, u32[]{:S(2)}, u32[]{:S(2)}) collective-permute-start(bf16[2048,128]{1,0:T(8,128)(2,1)S(1)} %copy-done.5), channel_id=1, source_target_pairs={{0,1},{1,0},{2,3},{3,2},{4,5},{5,4},{6,7},{7,6},{8,9},{9,8},{10,11... | collective-permute-start | bytes 1572872 | tf_op jit(solution)/shard_map/ppermute | solution.py:460
  97.8 7.9 %collective-permute-start.6 = (bf16[2048,128]{1,0:T(8,128)(2,1)S(1)}, bf16[2048,128]{1,0:T(8,128)(2,1)S(1)}, u32[]{:S(2)}, u32[]{:S(2)}) collective-permute-start(bf16[2048,128]{1,0:T(8,128)(2,1)S(1)} %copy-done.6), channel_id=1, source_target_pairs={{0,1},{1,0},{2,3},{3,2},{4,5},{5,4},{6,7},{7,6},{8,9},{9,8},{10,11... | collective-permute-start | bytes 1572872 | tf_op jit(solution)/shard_map/ppermute | solution.py:460
  98.9 7.1 %collective-permute-start.7 = (bf16[128,2048]{1,0:T(8,128)(2,1)S(1)}, bf16[128,2048]{1,0:T(8,128)(2,1)S(1)}, u32[]{:S(2)}, u32[]{:S(2)}) collective-permute-start(bf16[128,2048]{1,0:T(8,128)(2,1)S(1)} %copy-done.7), channel_id=1, source_target_pairs={{0,1},{1,0},{2,3},{3,2},{4,5},{5,4},{6,7},{7,6},{8,9},{9,8},{10,11... | collective-permute-start | bytes 1572872 | tf_op jit(solution)/shard_map/ppermute | solution.py:460
  105.6 14.7 %collective-permute-start.20 = (bf16[2048,128]{1,0:T(8,128)(2,1)S(1)}, bf16[2048,128]{1,0:T(8,128)(2,1)S(1)}, u32[]{:S(2)}, u32[]{:S(2)}) collective-permute-start(bf16[2048,128]{1,0:T(8,128)(2,1)S(1)} %copy-done.9), channel_id=1, source_target_pairs={{0,6},{1,7},{2,4},{3,5},{4,2},{5,3},{6,0},{7,1},{8,14},{9,15},{10,... | collective-permute-start | bytes 1572872 | tf_op jit(solution)/shard_map/ppermute | solution.py:460
  105.8 26.8 %collective-permute-start.11 = (bf16[2048,128]{1,0:T(8,128)(2,1)S(1)}, bf16[2048,128]{1,0:T(8,128)(2,1)S(1)}, u32[]{:S(2)}, u32[]{:S(2)}) collective-permute-start(bf16[2048,128]{1,0:T(8,128)(2,1)S(1)} %copy-done.9), channel_id=1, source_target_pairs={{0,1},{1,0},{2,3},{3,2},{4,5},{5,4},{6,7},{7,6},{8,9},{9,8},{10,11... | collective-permute-start | bytes 1572872 | tf_op jit(solution)/shard_map/ppermute | solution.py:460
  106.0 14.4 %collective-permute-start.21 = (bf16[2048,128]{1,0:T(8,128)(2,1)}, bf16[2048,128]{1,0:T(8,128)(2,1)S(1)}, u32[]{:S(2)}, u32[]{:S(2)}) collective-permute-start(bf16[2048,128]{1,0:T(8,128)(2,1)} %collective-permute-done.15.refs_14_), channel_id=1, source_target_pairs={{0,2},{1,3},{2,0},{3,1},{4,6},{5,7},{6,4},{7,5},{8,10},{9,11},{10,... | collective-permute-start | bytes 1572872 | tf_op jit(solution)/shard_map/ppermute | solution.py:460
  106.8 23.9 %collective-permute-start.22 = (bf16[128,2048]{1,0:T(8,128)(2,1)}, bf16[128,2048]{1,0:T(8,128)(2,1)S(1)}, u32[]{:S(2)}, u32[]{:S(2)}) collective-permute-start(bf16[128,2048]{1,0:T(8,128)(2,1)} %collective-permute-done.16.refs_15_), channel_id=1, source_target_pairs={{0,2},{1,3},{2,0},{3,1},{4,6},{5,7},{6,4},{7,5},{8,10},{9,11},{10,... | collective-permute-start | bytes 1572872 | tf_op jit(solution)/shard_map/ppermute | solution.py:460
  120.4 13.1 %collective-permute-start.4 = (f32[16,2048]{1,0:T(8,128)S(1)}, f32[16,2048]{1,0:T(8,128)S(1)}, u32[]{:S(2)}, u32[]{:S(2)}) collective-permute-start(f32[16,2048]{1,0:T(8,128)S(1)} %fusion), channel_id=1, source_target_pairs={{0,2},{1,3},{2,0},{3,1},{4,6},{5,7},{6,4},{7,5},{8,10},{9,11},{10,... | collective-permute-start | bytes 393224 | tf_op jit(solution)/shard_map/ppermute | solution.py:460
  120.4 19.1 %collective-permute-start.18 = (bf16[2048,128]{1,0:T(8,128)(2,1)}, bf16[2048,128]{1,0:T(8,128)(2,1)}, u32[]{:S(2)}, u32[]{:S(2)}) collective-permute-start(bf16[2048,128]{1,0:T(8,128)(2,1)} %collective-permute-done.15.refs_14_), channel_id=1, source_target_pairs={{0,1},{1,0},{2,3},{3,2},{4,5},{5,4},{6,7},{7,6},{8,9},{9,8},{10,11... | collective-permute-start | bytes 1572872 | tf_op jit(solution)/shard_map/ppermute | solution.py:460
  130.7 9.0 %collective-permute-start.19 = (bf16[128,2048]{1,0:T(8,128)(2,1)}, bf16[128,2048]{1,0:T(8,128)(2,1)}, u32[]{:S(2)}, u32[]{:S(2)}) collective-permute-start(bf16[128,2048]{1,0:T(8,128)(2,1)} %collective-permute-done.16.refs_15_), channel_id=1, source_target_pairs={{0,1},{1,0},{2,3},{3,2},{4,5},{5,4},{6,7},{7,6},{8,9},{9,8},{10,11... | collective-permute-start | bytes 1572872 | tf_op jit(solution)/shard_map/ppermute | solution.py:460
  132.6 7.5 %collective-permute-start.12 = (bf16[2048,128]{1,0:T(8,128)(2,1)}, bf16[2048,128]{1,0:T(8,128)(2,1)}, u32[]{:S(2)}, u32[]{:S(2)}) collective-permute-start(bf16[2048,128]{1,0:T(8,128)(2,1)} %collective-permute-done.9.refs_8_), channel_id=1, source_target_pairs={{0,1},{1,0},{2,3},{3,2},{4,5},{5,4},{6,7},{7,6},{8,9},{9,8},{10,11... | collective-permute-start | bytes 1572872 | tf_op jit(solution)/shard_map/ppermute | solution.py:460
  133.5 6.9 %collective-permute-start.13 = (bf16[128,2048]{1,0:T(8,128)(2,1)}, bf16[128,2048]{1,0:T(8,128)(2,1)}, u32[]{:S(2)}, u32[]{:S(2)}) collective-permute-start(bf16[128,2048]{1,0:T(8,128)(2,1)} %collective-permute-done.10.refs_9_), channel_id=1, source_target_pairs={{0,1},{1,0},{2,3},{3,2},{4,5},{5,4},{6,7},{7,6},{8,9},{9,8},{10,11... | collective-permute-start | bytes 1572872 | tf_op jit(solution)/shard_map/ppermute | solution.py:460
  135.8 22.0 %all-to-all-start.1 = ((bf16[16,16,2048]{2,1,0:T(8,128)(2,1)}), bf16[16,16,2048]{2,1,0:T(8,128)(2,1)S(1)}, u32[]{:S(2)}, u32[]{:S(2)}) async-start(bf16[16,16,2048]{2,1,0:T(8,128)(2,1)} %get-tuple-element.18), calls=%async_computation.1 | async-start | bytes 2097152 | tf_op jit(solution)/shard_map/all_to_all | solution.py:470
  140.1 3.1 %collective-permute-start.24 = (bf16[2048,128]{1,0:T(8,128)(2,1)S(1)}, bf16[2048,128]{1,0:T(8,128)(2,1)S(1)}, u32[]{:S(2)}, u32[]{:S(2)}) collective-permute-start(bf16[2048,128]{1,0:T(8,128)(2,1)S(1)} %collective-permute-done.21.refs_20_), channel_id=1, source_target_pairs={{0,1},{1,0},{2,3},{3,2},{4,5},{5,4},{6,7},{7,6},{8,9},{9,8},{10,11... | collective-permute-start | bytes 1572872 | tf_op jit(solution)/shard_map/ppermute | solution.py:460
  140.4 3.7 %collective-permute-start.25 = (bf16[128,2048]{1,0:T(8,128)(2,1)S(1)}, bf16[128,2048]{1,0:T(8,128)(2,1)}, u32[]{:S(2)}, u32[]{:S(2)}) collective-permute-start(bf16[128,2048]{1,0:T(8,128)(2,1)S(1)} %collective-permute-done.22.refs_21_), channel_id=1, source_target_pairs={{0,1},{1,0},{2,3},{3,2},{4,5},{5,4},{6,7},{7,6},{8,9},{9,8},{10,11... | collective-permute-start | bytes 1572872 | tf_op jit(solution)/shard_map/ppermute | solution.py:460
  (29 other events, 584.3 us)

commit v5 on v3

--- a/solution.py
+++ b/solution.py
@@ -25,7 +25,7 @@
     first = pl.multiple_of(half_ref[0] * rows, rows)
 
     def copy(i):
-        src = pool_ref.at[slot_ref[i], pl.ds(first, rows), :]
+        src = pool_ref.at[slot_ref[i // caps, i % caps], pl.ds(first, rows), :]
         return pltpu.make_async_copy(src, out_ref.at[i], sems.at[i])
 
     copies = [copy(i) for i in range(pages)]
@@ -40,14 +40,14 @@
 
 
 def outgoing_pages(half, slots, counts, pool):
-    pages = slots.shape[0]
+    pages = slots.size
     rows = pool.shape[1] // 2
     return pl.pallas_call(
         outgoing_kernel,
         grid_spec=pltpu.PrefetchScalarGridSpec(
             num_scalar_prefetch=3,
             grid=(1,),
-            in_specs=[pl.BlockSpec(memory_space=pl.ANY)],
+            in_specs=[pl.BlockSpec(memory_space=pltpu.HBM)],
             out_specs=pl.BlockSpec((pages, rows, pool.shape[2]), lambda i, *_: (0, 0, 0)),
             scratch_shapes=[pltpu.SemaphoreType.DMA((pages,))],
         ),
@@ -110,16 +110,28 @@
 
 def resident_kernel(
     half_ref, qa_ref, qb_ref, entry_ref, tab_ref, len_ref, pool_ref,
-    acc_ref, stat_ref, qt_ref, full, part,
+    acc_ref, stat_ref, qt_ref, full, part, held, sems,
 ):
     i = pl.program_id(0)
-    pages, rows, width = pool_ref.shape
+    steps = sems.shape[0]
+    slots, rows, width = held.shape
+    pages = slots // steps
     hd = width // 2
+    first = pl.multiple_of(half_ref[0] * rows, rows)
+
+    def load(k):
+        at = pl.ds(k * pages, pages)
+        return pltpu.make_async_copy(
+            pool_ref.at[at, pl.ds(first, rows), :], held.at[at], sems.at[k]
+        )
+
     mine = qa_ref.shape[0]
     games = entry_ref.shape[0]
 
     @pl.when(i == 0)
     def _():
+        for k in range(steps):
+            load(k).start()
         q = jnp.concatenate([qa_ref[...], qb_ref[...]], axis=0)
         qt_ref[...] = q.T
         tables(0, half_ref[0], rows, tab_ref, len_ref, full, part)
@@ -135,7 +147,9 @@
             entry_ref[:, hd:], p.astype(BF), (((0,), (0,)), ((), ())), preferred_element_type=F32
         )
 
-    chunk_step(pool_ref, i * pages, qt_ref, full, part, acc_ref, stat_ref)
+    load(i).wait()
+    at = pl.ds(pl.multiple_of(i * pages, pages), pages)
+    chunk_step(held.at[at], i * pages, qt_ref, full, part, acc_ref, stat_ref)
 
 
 def resident(half, q_mine, q_peer, entry, table, lengths, pool):
@@ -161,16 +175,18 @@
                 whole(entry.shape),
                 whole(table.shape),
                 whole(lengths.shape),
-                pl.BlockSpec((block, rows, width), lambda i, h: (i, h[0], 0)),
+                pl.BlockSpec(memory_space=pltpu.HBM),
             ],
             out_specs=[whole(o.shape) for o in outs],
             scratch_shapes=[
                 pltpu.VMEM((slots, lanes), F32),
                 pltpu.VMEM((slots, lanes), jnp.int32),
+                pltpu.VMEM((slots, rows, width), BF),
+                pltpu.SemaphoreType.DMA((slots // block,)),
             ],
         ),
         out_shape=outs,
-        compiler_params=params(60),
+        compiler_params=params(48),
         cost_estimate=cost(8),
         name="resident",
     )(half, q_mine, q_peer, entry, table, lengths, pool)
@@ -228,7 +244,7 @@
             ],
         ),
         out_shape=[out, out],
-        compiler_params=params(20),
+        compiler_params=params(40),
         cost_estimate=cost(8),
         name="moved",
     )(half, qt, table, lengths, acc, stat, got)
@@ -428,7 +444,7 @@
         a, axes, 0, 0, tiled=True, axis_index_groups=who
     )
 
-    out_pages = outgoing_pages(half, send_slots.reshape(-1), move_count.reshape(-1), page_pool)
+    out_pages = outgoing_pages(half, send_slots, move_count.reshape(-1), page_pool)
     got = exchange(
         out_pages.reshape(n_dp, -1, page_len // 2, width), groups
     ).reshape(out_pages.shape)
@@ -446,8 +462,12 @@
     w_side = each(weights, side)
     w_core = each(weights, core)
     w_side_core = each(w_side, core)
-    w_far = each(weights, far)
-    w_diag = each(w_far, side)
+    far_up, far_down, far_gate = (send(weights[k], far) for k in (1, 2, 0))
+    w_far = (far_gate, far_up, far_down)
+    diag_gate = send(w_side[0], far)
+    diag_up = send(far_up, side)
+    diag_down = send(far_down, side)
+    w_diag = (diag_gate, diag_up, diag_down)
     w_far_core = each(w_far, core)
     w_diag_core = each(w_diag, core)
     blocks = [

time: 228 us -> 216 us (0.947)
  starting transfers between devices: 41.3 us -> 34.3 us
  local copies, waits for them, and re-layouts: 24.9 us -> 21.2 us
    all_to_all x2, waiting for transfers between devices: 16.1 us -> 59.7 us  [step(): lax.all_to_all(a, axes, 0, 0, tiled=True, axis_index_groups=who)]
    ppermute x26, waiting for transfers between devices: 79.1 us -> 36 us  [step(): send = lambda a, pairs: lax.ppermute(a, axes, pairs)]
    ppermute x26, starting transfers between devices: 22.9 us -> 17.4 us  [step(): send = lambda a, pairs: lax.ppermute(a, axes, pairs)]
    unnamed x82 -> x70, local copies, waits for them, and re-layouts: 22.9 us -> 21 us
  transfers between devices with their start and end apart: 28 -> 28, of which waited for: 10 -> 10; matrix products, arithmetic and copies ran while one was open for 1% -> 0% of each run, Pallas kernels for 10% -> 10%
where the time goes in v5:
time: 216 us; the launch traced here: 215 us
  waiting for transfers between devices  95.7 us (44%)
  Pallas kernels  35.2 us (16%)
  starting transfers between devices  34.3 us (16%)
  blocking collectives  27.5 us (13%)
  local copies, waits for them, and re-layouts  21.2 us (10%)
    all_to_all x2, waiting for transfers between devices, step(): lax.all_to_all(a, axes, 0, 0, tiled=True, axis_index_groups=who)  59.7 us
    ppermute x26, waiting for transfers between devices, step(): send = lambda a, pairs: lax.ppermute(a, axes, pairs)  36 us
    unnamed x70, local copies, waits for them, and re-layouts  21 us
    all_to_all x1, blocking collectives, step(): lax.all_to_all(a, axes, 0, 0, tiled=True, axis_index_groups=who)  20 us
    ppermute x26, starting transfers between devices, step(): send = lambda a, pairs: lax.ppermute(a, axes, pairs)  17.4 us
    all_to_all x2, starting transfers between devices, step(): lax.all_to_all(a, axes, 0, 0, tiled=True, axis_index_groups=who)  16.9 us
    pallas_call x1, Pallas kernels, assemble(): pl.pallas_call(assemble_kernel, grid_spec=pltpu.PrefetchScalarGridSpec(nu...  8.87 us
    all_gather x1, blocking collectives, step(): layer_out = lax.all_gather(quarter, 'mp', axis=0, tiled=True)  7.47 us
  transfers between devices with their start and end apart: 28, of which 10 were waited for; matrix products, arithmetic and copies ran while one was open for 0% of the time, Pallas kernels for 10%

profile of v5, /device:TPU:1, one launch (start us, length us, event | category | flops | bytes accessed | tf_op | source)
XLA Modules:
  0.0 215.0 jit_solution(8883074540463318743)
XLA Ops:
  0.6 1.4 copy.15.slot_ref
  2.0 5.8 %outgoing.1 = bf16[64,64,512]{2,1,0:T(8,128)(2,1)} custom-call(s32[1]{0:T(128)S(6)} %select_n.7.half_ref, s32[32,2]{1,0:T(8,128)} %copy.15.slot_ref, s32[32]{0:T(128)} %bitcast.20, bf16[64,128,512]{2,1,0:T(8,128)(2,1)} %pool_ref.3), custom_call_target="tpu_custom_call" | custom-call | flops 1200000000 | bytes 6000000 | tf_op jit(solution)/shard_map/outgoing/pallas_call | solution.py:45
  7.9 11.7 %all-to-all-start = ((bf16[32,2,64,512]{3,2,1,0:T(8,128)(2,1)}), bf16[32,2,64,512]{3,2,1,0:T(8,128)(2,1)}, u32[]{:S(2)}, u32[]{:S(2)}) async-start(bf16[32,2,64,512]{3,2,1,0:T(8,128)(2,1)} %bitcast.18), calls=%async_computation | async-start | bytes 8388608 | tf_op jit(solution)/shard_map/all_to_all | solution.py:443
  19.7 2.4 %collective-permute-start.15 = (bf16[2048,128]{1,0:T(8,128)(2,1)S(1)}, bf16[2048,128]{1,0:T(8,128)(2,1)}, u32[]{:S(2)}, u32[]{:S(2)}) collective-permute-start(bf16[2048,128]{1,0:T(8,128)(2,1)S(1)} %copy-done.1), channel_id=1, source_target_pairs={{0,6},{1,7},{2,4},{3,5},{4,2},{5,3},{6,0},{7,1},{8,14},{9,15},{10,... | collective-permute-start | bytes 1572872 | tf_op jit(solution)/shard_map/ppermute | solution.py:433
  22.2 1.7 collective-permute-start.1
  23.9 1.0 collective-permute-start.9
  25.8 6.3 %collective-permute-done.8.refs_7_ = bf16[2048,128]{1,0:T(8,128)(2,1)S(1)} collective-permute-done((bf16[2048,128]{1,0:T(8,128)(2,1)S(1)}, bf16[2048,128]{1,0:T(8,128)(2,1)S(1)}, u32[]{:S(2)}, u32[]{:S(2)}) %collective-permute-start.8) | collective-permute-done | bytes 524320 | tf_op jit(solution)/shard_map/ppermute | solution.py:433
  32.2 47.8 %all-to-all-done = bf16[32,2,64,512]{3,2,1,0:T(8,128)(2,1)} async-done(((bf16[32,2,64,512]{3,2,1,0:T(8,128)(2,1)}), bf16[32,2,64,512]{3,2,1,0:T(8,128)(2,1)}, u32[]{:S(2)}, u32[]{:S(2)}) %all-to-all-start) | async-done | bytes 4194336 | tf_op jit(solution)/shard_map/all_to_all | solution.py:443
  80.0 2.3 %collective-permute-start = (bf16[64,64,512]{2,1,0:T(8,128)(2,1)}, bf16[64,64,512]{2,1,0:T(8,128)(2,1)}, u32[]{:S(2)}, u32[]{:S(2)}) collective-permute-start(bf16[64,64,512]{2,1,0:T(8,128)(2,1)} %bitcast.3.mine_ref.got_ref), channel_id=1, source_target_pairs={{0,1},{1,0},{2,3},{3,2},{4,5},{5,4},{6,7},{7,6},{8,9},{9,8},{10,11... | collective-permute-start | bytes 12582920 | tf_op jit(solution)/shard_map/ppermute | solution.py:433
  82.3 5.8 %resident.1 = (f32[256,256]{1,0:T(8,128)S(1)}, f32[8,256]{1,0:T(8,128)S(1)}, bf16[256,256]{1,0:T(8,128)(2,1)S(1)}) custom-call(s32[1]{0:T(128)S(6)} %select_n.7.half_ref, bf16[128,256]{1,0:T(8,128)(2,1)S(1)} %bitcast.16, bf16[128,256]{1,0:T(8,128)(2,1)S(1)} %collective-permute-done.1.qb_ref, bf16[64,512]{1,0:T(8,128)(2,1)S(1)} %copy-done.29, ...), custom_call_target="tpu_custom_call" | custom-call | flops 3200000000 | bytes 16000000 | tf_op jit(solution)/shard_map/resident/pallas_call | solution.py:167
  88.2 6.4 %moved.1 = (f32[264,128]{1,0:T(8,128)S(1)}, f32[264,128]{1,0:T(8,128)S(1)}) custom-call(s32[1]{0:T(128)S(6)} %select_n.7.half_ref, bf16[256,256]{1,0:T(8,128)(2,1)S(1)} %get-tuple-element.11.qt_ref, s32[16,256]{1,0:T(8,128)S(1)} %tile.18.tab_ref, s32[1,256]{1,0:T(1,128)S(1)} %tile.20.len_ref, f32[256,256]{1,0:T(8,128)S(1)} %get-tuple-element.12.acc_in, ...), custom_call_target="tpu_custom_call" | custom-call | flops 3200000000 | bytes 16000000 | tf_op jit(solution)/shard_map/moved/pallas_call | solution.py:225
  96.9 6.0 %collective-permute-done.14.refs_13_ = bf16[2048,128]{1,0:T(8,128)(2,1)S(1)} collective-permute-done((bf16[2048,128]{1,0:T(8,128)(2,1)S(1)}, bf16[2048,128]{1,0:T(8,128)(2,1)S(1)}, u32[]{:S(2)}, u32[]{:S(2)}) %collective-permute-start.14) | collective-permute-done | bytes 524320 | tf_op jit(solution)/shard_map/ppermute | solution.py:433
  106.5 1.5 collective-permute-start.22
  108.0 11.2 %collective-permute-done.20.refs_19_ = bf16[2048,128]{1,0:T(8,128)(2,1)S(1)} collective-permute-done((bf16[2048,128]{1,0:T(8,128)(2,1)S(1)}, bf16[2048,128]{1,0:T(8,128)(2,1)S(1)}, u32[]{:S(2)}, u32[]{:S(2)}) %collective-permute-start.20) | collective-permute-done | bytes 524320 | tf_op jit(solution)/shard_map/ppermute | solution.py:433
  120.0 1.7 collective-permute-start.18
  121.7 9.6 %collective-permute-done.22.refs_21_ = bf16[128,2048]{1,0:T(8,128)(2,1)S(1)} collective-permute-done((bf16[128,2048]{1,0:T(8,128)(2,1)}, bf16[128,2048]{1,0:T(8,128)(2,1)S(1)}, u32[]{:S(2)}, u32[]{:S(2)}) %collective-permute-start.22) | collective-permute-done | bytes 524320 | tf_op jit(solution)/shard_map/ppermute | solution.py:433
  131.3 1.7 collective-permute-start.19
  135.1 1.2 norm.1
  136.3 5.3 %all-to-all-start.1 = ((bf16[16,16,2048]{2,1,0:T(8,128)(2,1)}), bf16[16,16,2048]{2,1,0:T(8,128)(2,1)S(1)}, u32[]{:S(2)}, u32[]{:S(2)}) async-start(bf16[16,16,2048]{2,1,0:T(8,128)(2,1)} %get-tuple-element.18), calls=%async_computation.1 | async-start | bytes 2097152 | tf_op jit(solution)/shard_map/all_to_all | solution.py:443
  147.0 11.8 %all-to-all-done.1 = bf16[16,16,2048]{2,1,0:T(8,128)(2,1)S(1)} async-done(((bf16[16,16,2048]{2,1,0:T(8,128)(2,1)}), bf16[16,16,2048]{2,1,0:T(8,128)(2,1)S(1)}, u32[]{:S(2)}, u32[]{:S(2)}) %all-to-all-start.1) | async-done | bytes 1048608 | tf_op jit(solution)/shard_map/all_to_all | solution.py:443
  171.3 6.5 %ffn.1 = bf16[256,2048]{1,0:T(8,128)(2,1)S(1)} custom-call(bf16[256,2048]{1,0:T(8,128)(2,1)S(1)} %bitcast.13, bf16[2048,128]{1,0:T(8,128)(2,1)S(1)} %copy-done, bf16[2048,128]{1,0:T(8,128)(2,1)S(1)} %copy-done.1, bf16[128,2048]{1,0:T(8,128)(2,1)S(1)} %copy-done.2, bf16[2048,128]{1,0:T(8,128)(2,1)S(1)} %copy-done.6, bf16[2048,128]{1,0:T(8,128)(2,1)S(1)} %copy-done.8, ...), custom_call_target="tpu_custom_call" | custom-call | flops 3200000000 | bytes 16000000 | tf_op jit(solution)/shard_map/ffn/pallas_call | solution.py:364
  177.8 20.0 %all_to_all.15.parts_ref = bf16[16,16,2048]{2,1,0:T(8,128)(2,1)S(1)} all-to-all(bf16[16,16,2048]{2,1,0:T(8,128)(2,1)S(1)} %bitcast.14), channel_id=1, replica_groups={{0,8,16,24,32,40,48,56,64,72,80,88,96,104,112,120},{1,9,17,25,33,41,49,..., dimensions={0} | all-to-all | bytes 2097152 | tf_op jit(solution)/shard_map/all_to_all | solution.py:443
  197.9 7.5 %all_gather.3 = bf16[64,2048]{1,0:T(8,128)(2,1)S(1)} all-gather(bf16[16,2048]{1,0:T(8,128)(2,1)S(1)} %finish.1), channel_id=1, replica_groups=mesh['dp'=32,'mp'=4] {'mp'}, dimensions={0}, use_global_device_ids=true | all-gather | bytes 327680 | tf_op jit(solution)/shard_map/all_gather | solution.py:494
  205.4 8.9 %assemble.1 = bf16[64,128,512]{2,1,0:T(8,128)(2,1)} custom-call(s32[1]{0:T(128)S(6)} %select_n.7.half_ref, bf16[64,64,512]{2,1,0:T(8,128)(2,1)} %bitcast.3.mine_ref.got_ref, bf16[64,64,512]{2,1,0:T(8,128)(2,1)} %collective-permute-done.peer_ref), custom_call_target="tpu_custom_call" | custom-call | flops 2400000000 | bytes 12000000 | tf_op jit(solution)/shard_map/assemble/pallas_call | solution.py:406
  (119 shorter events, 28.8 us)
Async XLA Ops:
  7.9 72.1 %all-to-all-start = ((bf16[32,2,64,512]{3,2,1,0:T(8,128)(2,1)}), bf16[32,2,64,512]{3,2,1,0:T(8,128)(2,1)}, u32[]{:S(2)}, u32[]{:S(2)}) async-start(bf16[32,2,64,512]{3,2,1,0:T(8,128)(2,1)} %bitcast.18), calls=%async_computation | async-start | bytes 8388608 | tf_op jit(solution)/shard_map/all_to_all | solution.py:443
  19.6 12.6 %collective-permute-start.8 = (bf16[2048,128]{1,0:T(8,128)(2,1)S(1)}, bf16[2048,128]{1,0:T(8,128)(2,1)S(1)}, u32[]{:S(2)}, u32[]{:S(2)}) collective-permute-start(bf16[2048,128]{1,0:T(8,128)(2,1)S(1)} %copy-done), channel_id=1, source_target_pairs={{0,2},{1,3},{2,0},{3,1},{4,6},{5,7},{6,4},{7,5},{8,10},{9,11},{10,... | collective-permute-start | bytes 1572872 | tf_op jit(solution)/shard_map/ppermute | solution.py:433
  19.7 68.5 %collective-permute-start.15 = (bf16[2048,128]{1,0:T(8,128)(2,1)S(1)}, bf16[2048,128]{1,0:T(8,128)(2,1)}, u32[]{:S(2)}, u32[]{:S(2)}) collective-permute-start(bf16[2048,128]{1,0:T(8,128)(2,1)S(1)} %copy-done.1), channel_id=1, source_target_pairs={{0,6},{1,7},{2,4},{3,5},{4,2},{5,3},{6,0},{7,1},{8,14},{9,15},{10,... | collective-permute-start | bytes 1572872 | tf_op jit(solution)/shard_map/ppermute | solution.py:433
  22.2 3.3 %collective-permute-start.1 = (bf16[128,256]{1,0:T(8,128)(2,1)S(1)}, bf16[128,256]{1,0:T(8,128)(2,1)S(1)}, u32[]{:S(2)}, u32[]{:S(2)}) collective-permute-start(bf16[128,256]{1,0:T(8,128)(2,1)S(1)} %bitcast.15), channel_id=1, source_target_pairs={{0,1},{1,0},{2,3},{3,2},{4,5},{5,4},{6,7},{7,6},{8,9},{9,8},{10,11... | collective-permute-start | bytes 196616 | tf_op jit(solution)/shard_map/ppermute | solution.py:433
  23.9 70.9 %collective-permute-start.9 = (bf16[2048,128]{1,0:T(8,128)(2,1)S(1)}, bf16[2048,128]{1,0:T(8,128)(2,1)}, u32[]{:S(2)}, u32[]{:S(2)}) collective-permute-start(bf16[2048,128]{1,0:T(8,128)(2,1)S(1)} %copy-done.1), channel_id=1, source_target_pairs={{0,2},{1,3},{2,0},{3,1},{4,6},{5,7},{6,4},{7,5},{8,10},{9,11},{10,... | collective-permute-start | bytes 1572872 | tf_op jit(solution)/shard_map/ppermute | solution.py:433
  24.9 69.7 %collective-permute-start.16 = (bf16[128,2048]{1,0:T(8,128)(2,1)S(1)}, bf16[128,2048]{1,0:T(8,128)(2,1)}, u32[]{:S(2)}, u32[]{:S(2)}) collective-permute-start(bf16[128,2048]{1,0:T(8,128)(2,1)S(1)} %copy-done.2), channel_id=1, source_target_pairs={{0,6},{1,7},{2,4},{3,5},{4,2},{5,3},{6,0},{7,1},{8,14},{9,15},{10,... | collective-permute-start | bytes 1572872 | tf_op jit(solution)/shard_map/ppermute | solution.py:433
  25.5 69.8 %collective-permute-start.10 = (bf16[128,2048]{1,0:T(8,128)(2,1)S(1)}, bf16[128,2048]{1,0:T(8,128)(2,1)}, u32[]{:S(2)}, u32[]{:S(2)}) collective-permute-start(bf16[128,2048]{1,0:T(8,128)(2,1)S(1)} %copy-done.2), channel_id=1, source_target_pairs={{0,2},{1,3},{2,0},{3,1},{4,6},{5,7},{6,4},{7,5},{8,10},{9,11},{10,... | collective-permute-start | bytes 1572872 | tf_op jit(solution)/shard_map/ppermute | solution.py:433
  80.0 125.4 %collective-permute-start = (bf16[64,64,512]{2,1,0:T(8,128)(2,1)}, bf16[64,64,512]{2,1,0:T(8,128)(2,1)}, u32[]{:S(2)}, u32[]{:S(2)}) collective-permute-start(bf16[64,64,512]{2,1,0:T(8,128)(2,1)} %bitcast.3.mine_ref.got_ref), channel_id=1, source_target_pairs={{0,1},{1,0},{2,3},{3,2},{4,5},{5,4},{6,7},{7,6},{8,9},{9,8},{10,11... | collective-permute-start | bytes 12582920 | tf_op jit(solution)/shard_map/ppermute | solution.py:433
  88.1 14.8 %collective-permute-start.14 = (bf16[2048,128]{1,0:T(8,128)(2,1)S(1)}, bf16[2048,128]{1,0:T(8,128)(2,1)S(1)}, u32[]{:S(2)}, u32[]{:S(2)}) collective-permute-start(bf16[2048,128]{1,0:T(8,128)(2,1)S(1)} %copy-done), channel_id=1, source_target_pairs={{0,6},{1,7},{2,4},{3,5},{4,2},{5,3},{6,0},{7,1},{8,14},{9,15},{10,... | collective-permute-start | bytes 1572872 | tf_op jit(solution)/shard_map/ppermute | solution.py:433
  94.8 9.0 %collective-permute-start.5 = (bf16[2048,128]{1,0:T(8,128)(2,1)S(1)}, bf16[2048,128]{1,0:T(8,128)(2,1)S(1)}, u32[]{:S(2)}, u32[]{:S(2)}) collective-permute-start(bf16[2048,128]{1,0:T(8,128)(2,1)S(1)} %copy-done), channel_id=1, source_target_pairs={{0,1},{1,0},{2,3},{3,2},{4,5},{5,4},{6,7},{7,6},{8,9},{9,8},{10,11... | collective-permute-start | bytes 1572872 | tf_op jit(solution)/shard_map/ppermute | solution.py:433
  95.3 9.3 %collective-permute-start.6 = (bf16[2048,128]{1,0:T(8,128)(2,1)S(1)}, bf16[2048,128]{1,0:T(8,128)(2,1)S(1)}, u32[]{:S(2)}, u32[]{:S(2)}) collective-permute-start(bf16[2048,128]{1,0:T(8,128)(2,1)S(1)} %copy-done.1), channel_id=1, source_target_pairs={{0,1},{1,0},{2,3},{3,2},{4,5},{5,4},{6,7},{7,6},{8,9},{9,8},{10,11... | collective-permute-start | bytes 1572872 | tf_op jit(solution)/shard_map/ppermute | solution.py:433
  96.1 9.6 %collective-permute-start.7 = (bf16[128,2048]{1,0:T(8,128)(2,1)S(1)}, bf16[128,2048]{1,0:T(8,128)(2,1)S(1)}, u32[]{:S(2)}, u32[]{:S(2)}) collective-permute-start(bf16[128,2048]{1,0:T(8,128)(2,1)S(1)} %copy-done.2), channel_id=1, source_target_pairs={{0,1},{1,0},{2,3},{3,2},{4,5},{5,4},{6,7},{7,6},{8,9},{9,8},{10,11... | collective-permute-start | bytes 1572872 | tf_op jit(solution)/shard_map/ppermute | solution.py:433
  102.9 3.6 %collective-permute-start.3 = (f32[2,16,2048]{2,1,0:T(8,128)S(1)}, f32[2,16,2048]{2,1,0:T(8,128)S(1)}, u32[]{:S(2)}, u32[]{:S(2)}) collective-permute-start(f32[2,16,2048]{2,1,0:T(8,128)S(1)} %get-tuple-element.17), channel_id=1, source_target_pairs={{0,1},{1,0},{2,3},{3,2},{4,5},{5,4},{6,7},{7,6},{8,9},{9,8},{10,11... | collective-permute-start | bytes 786440 | tf_op jit(solution)/shard_map/ppermute | solution.py:433
  104.5 14.6 %collective-permute-start.20 = (bf16[2048,128]{1,0:T(8,128)(2,1)S(1)}, bf16[2048,128]{1,0:T(8,128)(2,1)S(1)}, u32[]{:S(2)}, u32[]{:S(2)}) collective-permute-start(bf16[2048,128]{1,0:T(8,128)(2,1)S(1)} %collective-permute-done.8.refs_7_), channel_id=1, source_target_pairs={{0,6},{1,7},{2,4},{3,5},{4,2},{5,3},{6,0},{7,1},{8,14},{9,15},{10,... | collective-permute-start | bytes 1572872 | tf_op jit(solution)/shard_map/ppermute | solution.py:433
  105.4 27.6 %collective-permute-start.11 = (bf16[2048,128]{1,0:T(8,128)(2,1)S(1)}, bf16[2048,128]{1,0:T(8,128)(2,1)S(1)}, u32[]{:S(2)}, u32[]{:S(2)}) collective-permute-start(bf16[2048,128]{1,0:T(8,128)(2,1)S(1)} %collective-permute-done.8.refs_7_), channel_id=1, source_target_pairs={{0,1},{1,0},{2,3},{3,2},{4,5},{5,4},{6,7},{7,6},{8,9},{9,8},{10,11... | collective-permute-start | bytes 1572872 | tf_op jit(solution)/shard_map/ppermute | solution.py:433
  106.5 13.5 %collective-permute-start.21 = (bf16[2048,128]{1,0:T(8,128)(2,1)}, bf16[2048,128]{1,0:T(8,128)(2,1)S(1)}, u32[]{:S(2)}, u32[]{:S(2)}) collective-permute-start(bf16[2048,128]{1,0:T(8,128)(2,1)} %collective-permute-done.15.refs_14_), channel_id=1, source_target_pairs={{0,2},{1,3},{2,0},{3,1},{4,6},{5,7},{6,4},{7,5},{8,10},{9,11},{10,... | collective-permute-start | bytes 1572872 | tf_op jit(solution)/shard_map/ppermute | solution.py:433
  106.5 24.7 %collective-permute-start.22 = (bf16[128,2048]{1,0:T(8,128)(2,1)}, bf16[128,2048]{1,0:T(8,128)(2,1)S(1)}, u32[]{:S(2)}, u32[]{:S(2)}) collective-permute-start(bf16[128,2048]{1,0:T(8,128)(2,1)} %collective-permute-done.16.refs_15_), channel_id=1, source_target_pairs={{0,2},{1,3},{2,0},{3,1},{4,6},{5,7},{6,4},{7,5},{8,10},{9,11},{10,... | collective-permute-start | bytes 1572872 | tf_op jit(solution)/shard_map/ppermute | solution.py:433
  119.2 14.9 %collective-permute-start.4 = (f32[16,2048]{1,0:T(8,128)S(1)}, f32[16,2048]{1,0:T(8,128)S(1)}, u32[]{:S(2)}, u32[]{:S(2)}) collective-permute-start(f32[16,2048]{1,0:T(8,128)S(1)} %fusion), channel_id=1, source_target_pairs={{0,2},{1,3},{2,0},{3,1},{4,6},{5,7},{6,4},{7,5},{8,10},{9,11},{10,... | collective-permute-start | bytes 393224 | tf_op jit(solution)/shard_map/ppermute | solution.py:433
  120.0 21.5 %collective-permute-start.18 = (bf16[2048,128]{1,0:T(8,128)(2,1)}, bf16[2048,128]{1,0:T(8,128)(2,1)}, u32[]{:S(2)}, u32[]{:S(2)}) collective-permute-start(bf16[2048,128]{1,0:T(8,128)(2,1)} %collective-permute-done.15.refs_14_), channel_id=1, source_target_pairs={{0,1},{1,0},{2,3},{3,2},{4,5},{5,4},{6,7},{7,6},{8,9},{9,8},{10,11... | collective-permute-start | bytes 1572872 | tf_op jit(solution)/shard_map/ppermute | solution.py:433
  131.3 10.7 %collective-permute-start.19 = (bf16[128,2048]{1,0:T(8,128)(2,1)}, bf16[128,2048]{1,0:T(8,128)(2,1)}, u32[]{:S(2)}, u32[]{:S(2)}) collective-permute-start(bf16[128,2048]{1,0:T(8,128)(2,1)} %collective-permute-done.16.refs_15_), channel_id=1, source_target_pairs={{0,1},{1,0},{2,3},{3,2},{4,5},{5,4},{6,7},{7,6},{8,9},{9,8},{10,11... | collective-permute-start | bytes 1572872 | tf_op jit(solution)/shard_map/ppermute | solution.py:433
  133.7 8.4 %collective-permute-start.12 = (bf16[2048,128]{1,0:T(8,128)(2,1)}, bf16[2048,128]{1,0:T(8,128)(2,1)}, u32[]{:S(2)}, u32[]{:S(2)}) collective-permute-start(bf16[2048,128]{1,0:T(8,128)(2,1)} %collective-permute-done.9.refs_8_), channel_id=1, source_target_pairs={{0,1},{1,0},{2,3},{3,2},{4,5},{5,4},{6,7},{7,6},{8,9},{9,8},{10,11... | collective-permute-start | bytes 1572872 | tf_op jit(solution)/shard_map/ppermute | solution.py:433
  134.1 8.4 %collective-permute-start.13 = (bf16[128,2048]{1,0:T(8,128)(2,1)}, bf16[128,2048]{1,0:T(8,128)(2,1)}, u32[]{:S(2)}, u32[]{:S(2)}) collective-permute-start(bf16[128,2048]{1,0:T(8,128)(2,1)} %collective-permute-done.10.refs_9_), channel_id=1, source_target_pairs={{0,1},{1,0},{2,3},{3,2},{4,5},{5,4},{6,7},{7,6},{8,9},{9,8},{10,11... | collective-permute-start | bytes 1572872 | tf_op jit(solution)/shard_map/ppermute | solution.py:433
  136.3 22.5 %all-to-all-start.1 = ((bf16[16,16,2048]{2,1,0:T(8,128)(2,1)}), bf16[16,16,2048]{2,1,0:T(8,128)(2,1)S(1)}, u32[]{:S(2)}, u32[]{:S(2)}) async-start(bf16[16,16,2048]{2,1,0:T(8,128)(2,1)} %get-tuple-element.18), calls=%async_computation.1 | async-start | bytes 2097152 | tf_op jit(solution)/shard_map/all_to_all | solution.py:443
  142.5 3.7 %collective-permute-start.25 = (bf16[128,2048]{1,0:T(8,128)(2,1)}, bf16[128,2048]{1,0:T(8,128)(2,1)S(1)}, u32[]{:S(2)}, u32[]{:S(2)}) collective-permute-start(bf16[128,2048]{1,0:T(8,128)(2,1)} %copy-done.17), channel_id=1, source_target_pairs={{0,1},{1,0},{2,3},{3,2},{4,5},{5,4},{6,7},{7,6},{8,9},{9,8},{10,11... | collective-permute-start | bytes 1572872 | tf_op jit(solution)/shard_map/ppermute | solution.py:433
  (38 other events, 344.3 us)

commit v6 on v5

--- a/solution.py
+++ b/solution.py
@@ -469,7 +469,10 @@
     diag_down = send(far_down, side)
     w_diag = (diag_gate, diag_up, diag_down)
     w_far_core = each(w_far, core)
-    w_diag_core = each(w_diag, core)
+    diag_core_gate = send(diag_gate, core)
+    diag_core_up = send(diag_up, core)
+    diag_core_down = send(diag_down, core)
+    w_diag_core = (diag_core_gate, diag_core_up, diag_core_down)
     blocks = [
         weights, w_core, w_side, w_side_core, w_far, w_far_core, w_diag, w_diag_core
     ]

time: 216 us -> 216 us (level)
  no operation moved by 1% of the time
where the time goes in v6:
time: 216 us; the launch traced here: 215 us
  waiting for transfers between devices  95.7 us (44%)
  Pallas kernels  35.2 us (16%)
  starting transfers between devices  34.3 us (16%)
  blocking collectives  27.5 us (13%)
  local copies, waits for them, and re-layouts  21.2 us (10%)
    all_to_all x2, waiting for transfers between devices, step(): lax.all_to_all(a, axes, 0, 0, tiled=True, axis_index_groups=who)  59.7 us
    ppermute x26, waiting for transfers between devices, step(): send = lambda a, pairs: lax.ppermute(a, axes, pairs)  36 us
    unnamed x70, local copies, waits for them, and re-layouts  21 us
    all_to_all x1, blocking collectives, step(): lax.all_to_all(a, axes, 0, 0, tiled=True, axis_index_groups=who)  20 us
    ppermute x26, starting transfers between devices, step(): send = lambda a, pairs: lax.ppermute(a, axes, pairs)  17.4 us
    all_to_all x2, starting transfers between devices, step(): lax.all_to_all(a, axes, 0, 0, tiled=True, axis_index_groups=who)  16.9 us
    pallas_call x1, Pallas kernels, assemble(): pl.pallas_call(assemble_kernel, grid_spec=pltpu.PrefetchScalarGridSpec(nu...  8.87 us
    all_gather x1, blocking collectives, step(): layer_out = lax.all_gather(quarter, 'mp', axis=0, tiled=True)  7.47 us
  transfers between devices with their start and end apart: 28, of which 10 were waited for; matrix products, arithmetic and copies ran while one was open for 0% of the time, Pallas kernels for 10%

profile of v6, /device:TPU:1, one launch (start us, length us, event | category | flops | bytes accessed | tf_op | source)
XLA Modules:
  0.0 215.0 jit_solution(8883074540463318743)
XLA Ops:
  0.6 1.4 copy.15.slot_ref
  2.0 5.8 %outgoing.1 = bf16[64,64,512]{2,1,0:T(8,128)(2,1)} custom-call(s32[1]{0:T(128)S(6)} %select_n.7.half_ref, s32[32,2]{1,0:T(8,128)} %copy.15.slot_ref, s32[32]{0:T(128)} %bitcast.20, bf16[64,128,512]{2,1,0:T(8,128)(2,1)} %pool_ref.3), custom_call_target="tpu_custom_call" | custom-call | flops 1200000000 | bytes 6000000 | tf_op jit(solution)/shard_map/outgoing/pallas_call | solution.py:45
  7.9 11.7 %all-to-all-start = ((bf16[32,2,64,512]{3,2,1,0:T(8,128)(2,1)}), bf16[32,2,64,512]{3,2,1,0:T(8,128)(2,1)}, u32[]{:S(2)}, u32[]{:S(2)}) async-start(bf16[32,2,64,512]{3,2,1,0:T(8,128)(2,1)} %bitcast.18), calls=%async_computation | async-start | bytes 8388608 | tf_op jit(solution)/shard_map/all_to_all | solution.py:443
  19.7 2.4 %collective-permute-start.15 = (bf16[2048,128]{1,0:T(8,128)(2,1)S(1)}, bf16[2048,128]{1,0:T(8,128)(2,1)}, u32[]{:S(2)}, u32[]{:S(2)}) collective-permute-start(bf16[2048,128]{1,0:T(8,128)(2,1)S(1)} %copy-done.1), channel_id=1, source_target_pairs={{0,6},{1,7},{2,4},{3,5},{4,2},{5,3},{6,0},{7,1},{8,14},{9,15},{10,... | collective-permute-start | bytes 1572872 | tf_op jit(solution)/shard_map/ppermute | solution.py:433
  22.2 1.7 collective-permute-start.1
  23.9 1.0 collective-permute-start.9
  25.8 6.3 %collective-permute-done.8.refs_7_ = bf16[2048,128]{1,0:T(8,128)(2,1)S(1)} collective-permute-done((bf16[2048,128]{1,0:T(8,128)(2,1)S(1)}, bf16[2048,128]{1,0:T(8,128)(2,1)S(1)}, u32[]{:S(2)}, u32[]{:S(2)}) %collective-permute-start.8) | collective-permute-done | bytes 524320 | tf_op jit(solution)/shard_map/ppermute | solution.py:433
  32.2 47.8 %all-to-all-done = bf16[32,2,64,512]{3,2,1,0:T(8,128)(2,1)} async-done(((bf16[32,2,64,512]{3,2,1,0:T(8,128)(2,1)}), bf16[32,2,64,512]{3,2,1,0:T(8,128)(2,1)}, u32[]{:S(2)}, u32[]{:S(2)}) %all-to-all-start) | async-done | bytes 4194336 | tf_op jit(solution)/shard_map/all_to_all | solution.py:443
  80.0 2.3 %collective-permute-start = (bf16[64,64,512]{2,1,0:T(8,128)(2,1)}, bf16[64,64,512]{2,1,0:T(8,128)(2,1)}, u32[]{:S(2)}, u32[]{:S(2)}) collective-permute-start(bf16[64,64,512]{2,1,0:T(8,128)(2,1)} %bitcast.3.mine_ref.got_ref), channel_id=1, source_target_pairs={{0,1},{1,0},{2,3},{3,2},{4,5},{5,4},{6,7},{7,6},{8,9},{9,8},{10,11... | collective-permute-start | bytes 12582920 | tf_op jit(solution)/shard_map/ppermute | solution.py:433
  82.3 5.8 %resident.1 = (f32[256,256]{1,0:T(8,128)S(1)}, f32[8,256]{1,0:T(8,128)S(1)}, bf16[256,256]{1,0:T(8,128)(2,1)S(1)}) custom-call(s32[1]{0:T(128)S(6)} %select_n.7.half_ref, bf16[128,256]{1,0:T(8,128)(2,1)S(1)} %bitcast.16, bf16[128,256]{1,0:T(8,128)(2,1)S(1)} %collective-permute-done.1.qb_ref, bf16[64,512]{1,0:T(8,128)(2,1)S(1)} %copy-done.29, ...), custom_call_target="tpu_custom_call" | custom-call | flops 3200000000 | bytes 16000000 | tf_op jit(solution)/shard_map/resident/pallas_call | solution.py:167
  88.2 6.4 %moved.1 = (f32[264,128]{1,0:T(8,128)S(1)}, f32[264,128]{1,0:T(8,128)S(1)}) custom-call(s32[1]{0:T(128)S(6)} %select_n.7.half_ref, bf16[256,256]{1,0:T(8,128)(2,1)S(1)} %get-tuple-element.11.qt_ref, s32[16,256]{1,0:T(8,128)S(1)} %tile.18.tab_ref, s32[1,256]{1,0:T(1,128)S(1)} %tile.20.len_ref, f32[256,256]{1,0:T(8,128)S(1)} %get-tuple-element.12.acc_in, ...), custom_call_target="tpu_custom_call" | custom-call | flops 3200000000 | bytes 16000000 | tf_op jit(solution)/shard_map/moved/pallas_call | solution.py:225
  96.9 6.0 %collective-permute-done.14.refs_13_ = bf16[2048,128]{1,0:T(8,128)(2,1)S(1)} collective-permute-done((bf16[2048,128]{1,0:T(8,128)(2,1)S(1)}, bf16[2048,128]{1,0:T(8,128)(2,1)S(1)}, u32[]{:S(2)}, u32[]{:S(2)}) %collective-permute-start.14) | collective-permute-done | bytes 524320 | tf_op jit(solution)/shard_map/ppermute | solution.py:433
  106.5 1.5 collective-permute-start.22
  108.0 11.2 %collective-permute-done.20.refs_19_ = bf16[2048,128]{1,0:T(8,128)(2,1)S(1)} collective-permute-done((bf16[2048,128]{1,0:T(8,128)(2,1)S(1)}, bf16[2048,128]{1,0:T(8,128)(2,1)S(1)}, u32[]{:S(2)}, u32[]{:S(2)}) %collective-permute-start.20) | collective-permute-done | bytes 524320 | tf_op jit(solution)/shard_map/ppermute | solution.py:433
  120.0 1.7 collective-permute-start.18
  121.7 9.6 %collective-permute-done.22.refs_21_ = bf16[128,2048]{1,0:T(8,128)(2,1)S(1)} collective-permute-done((bf16[128,2048]{1,0:T(8,128)(2,1)}, bf16[128,2048]{1,0:T(8,128)(2,1)S(1)}, u32[]{:S(2)}, u32[]{:S(2)}) %collective-permute-start.22) | collective-permute-done | bytes 524320 | tf_op jit(solution)/shard_map/ppermute | solution.py:433
  131.3 1.7 collective-permute-start.19
  135.1 1.2 norm.1
  136.3 5.3 %all-to-all-start.1 = ((bf16[16,16,2048]{2,1,0:T(8,128)(2,1)}), bf16[16,16,2048]{2,1,0:T(8,128)(2,1)S(1)}, u32[]{:S(2)}, u32[]{:S(2)}) async-start(bf16[16,16,2048]{2,1,0:T(8,128)(2,1)} %get-tuple-element.18), calls=%async_computation.1 | async-start | bytes 2097152 | tf_op jit(solution)/shard_map/all_to_all | solution.py:443
  147.0 11.8 %all-to-all-done.1 = bf16[16,16,2048]{2,1,0:T(8,128)(2,1)S(1)} async-done(((bf16[16,16,2048]{2,1,0:T(8,128)(2,1)}), bf16[16,16,2048]{2,1,0:T(8,128)(2,1)S(1)}, u32[]{:S(2)}, u32[]{:S(2)}) %all-to-all-start.1) | async-done | bytes 1048608 | tf_op jit(solution)/shard_map/all_to_all | solution.py:443
  171.3 6.5 %ffn.1 = bf16[256,2048]{1,0:T(8,128)(2,1)S(1)} custom-call(bf16[256,2048]{1,0:T(8,128)(2,1)S(1)} %bitcast.13, bf16[2048,128]{1,0:T(8,128)(2,1)S(1)} %copy-done, bf16[2048,128]{1,0:T(8,128)(2,1)S(1)} %copy-done.1, bf16[128,2048]{1,0:T(8,128)(2,1)S(1)} %copy-done.2, bf16[2048,128]{1,0:T(8,128)(2,1)S(1)} %copy-done.6, bf16[2048,128]{1,0:T(8,128)(2,1)S(1)} %copy-done.8, ...), custom_call_target="tpu_custom_call" | custom-call | flops 3200000000 | bytes 16000000 | tf_op jit(solution)/shard_map/ffn/pallas_call | solution.py:364
  177.8 20.0 %all_to_all.15.parts_ref = bf16[16,16,2048]{2,1,0:T(8,128)(2,1)S(1)} all-to-all(bf16[16,16,2048]{2,1,0:T(8,128)(2,1)S(1)} %bitcast.14), channel_id=1, replica_groups={{0,8,16,24,32,40,48,56,64,72,80,88,96,104,112,120},{1,9,17,25,33,41,49,..., dimensions={0} | all-to-all | bytes 2097152 | tf_op jit(solution)/shard_map/all_to_all | solution.py:443
  197.9 7.5 %all_gather.3 = bf16[64,2048]{1,0:T(8,128)(2,1)S(1)} all-gather(bf16[16,2048]{1,0:T(8,128)(2,1)S(1)} %finish.1), channel_id=1, replica_groups=mesh['dp'=32,'mp'=4] {'mp'}, dimensions={0}, use_global_device_ids=true | all-gather | bytes 327680 | tf_op jit(solution)/shard_map/all_gather | solution.py:497
  205.4 8.9 %assemble.1 = bf16[64,128,512]{2,1,0:T(8,128)(2,1)} custom-call(s32[1]{0:T(128)S(6)} %select_n.7.half_ref, bf16[64,64,512]{2,1,0:T(8,128)(2,1)} %bitcast.3.mine_ref.got_ref, bf16[64,64,512]{2,1,0:T(8,128)(2,1)} %collective-permute-done.peer_ref), custom_call_target="tpu_custom_call" | custom-call | flops 2400000000 | bytes 12000000 | tf_op jit(solution)/shard_map/assemble/pallas_call | solution.py:406
  (119 shorter events, 28.8 us)
Async XLA Ops:
  7.9 72.1 %all-to-all-start = ((bf16[32,2,64,512]{3,2,1,0:T(8,128)(2,1)}), bf16[32,2,64,512]{3,2,1,0:T(8,128)(2,1)}, u32[]{:S(2)}, u32[]{:S(2)}) async-start(bf16[32,2,64,512]{3,2,1,0:T(8,128)(2,1)} %bitcast.18), calls=%async_computation | async-start | bytes 8388608 | tf_op jit(solution)/shard_map/all_to_all | solution.py:443
  19.6 12.6 %collective-permute-start.8 = (bf16[2048,128]{1,0:T(8,128)(2,1)S(1)}, bf16[2048,128]{1,0:T(8,128)(2,1)S(1)}, u32[]{:S(2)}, u32[]{:S(2)}) collective-permute-start(bf16[2048,128]{1,0:T(8,128)(2,1)S(1)} %copy-done), channel_id=1, source_target_pairs={{0,2},{1,3},{2,0},{3,1},{4,6},{5,7},{6,4},{7,5},{8,10},{9,11},{10,... | collective-permute-start | bytes 1572872 | tf_op jit(solution)/shard_map/ppermute | solution.py:433
  19.7 68.5 %collective-permute-start.15 = (bf16[2048,128]{1,0:T(8,128)(2,1)S(1)}, bf16[2048,128]{1,0:T(8,128)(2,1)}, u32[]{:S(2)}, u32[]{:S(2)}) collective-permute-start(bf16[2048,128]{1,0:T(8,128)(2,1)S(1)} %copy-done.1), channel_id=1, source_target_pairs={{0,6},{1,7},{2,4},{3,5},{4,2},{5,3},{6,0},{7,1},{8,14},{9,15},{10,... | collective-permute-start | bytes 1572872 | tf_op jit(solution)/shard_map/ppermute | solution.py:433
  22.2 3.3 %collective-permute-start.1 = (bf16[128,256]{1,0:T(8,128)(2,1)S(1)}, bf16[128,256]{1,0:T(8,128)(2,1)S(1)}, u32[]{:S(2)}, u32[]{:S(2)}) collective-permute-start(bf16[128,256]{1,0:T(8,128)(2,1)S(1)} %bitcast.15), channel_id=1, source_target_pairs={{0,1},{1,0},{2,3},{3,2},{4,5},{5,4},{6,7},{7,6},{8,9},{9,8},{10,11... | collective-permute-start | bytes 196616 | tf_op jit(solution)/shard_map/ppermute | solution.py:433
  23.9 70.9 %collective-permute-start.9 = (bf16[2048,128]{1,0:T(8,128)(2,1)S(1)}, bf16[2048,128]{1,0:T(8,128)(2,1)}, u32[]{:S(2)}, u32[]{:S(2)}) collective-permute-start(bf16[2048,128]{1,0:T(8,128)(2,1)S(1)} %copy-done.1), channel_id=1, source_target_pairs={{0,2},{1,3},{2,0},{3,1},{4,6},{5,7},{6,4},{7,5},{8,10},{9,11},{10,... | collective-permute-start | bytes 1572872 | tf_op jit(solution)/shard_map/ppermute | solution.py:433
  24.9 69.7 %collective-permute-start.16 = (bf16[128,2048]{1,0:T(8,128)(2,1)S(1)}, bf16[128,2048]{1,0:T(8,128)(2,1)}, u32[]{:S(2)}, u32[]{:S(2)}) collective-permute-start(bf16[128,2048]{1,0:T(8,128)(2,1)S(1)} %copy-done.2), channel_id=1, source_target_pairs={{0,6},{1,7},{2,4},{3,5},{4,2},{5,3},{6,0},{7,1},{8,14},{9,15},{10,... | collective-permute-start | bytes 1572872 | tf_op jit(solution)/shard_map/ppermute | solution.py:433
  25.5 69.8 %collective-permute-start.10 = (bf16[128,2048]{1,0:T(8,128)(2,1)S(1)}, bf16[128,2048]{1,0:T(8,128)(2,1)}, u32[]{:S(2)}, u32[]{:S(2)}) collective-permute-start(bf16[128,2048]{1,0:T(8,128)(2,1)S(1)} %copy-done.2), channel_id=1, source_target_pairs={{0,2},{1,3},{2,0},{3,1},{4,6},{5,7},{6,4},{7,5},{8,10},{9,11},{10,... | collective-permute-start | bytes 1572872 | tf_op jit(solution)/shard_map/ppermute | solution.py:433
  80.0 125.4 %collective-permute-start = (bf16[64,64,512]{2,1,0:T(8,128)(2,1)}, bf16[64,64,512]{2,1,0:T(8,128)(2,1)}, u32[]{:S(2)}, u32[]{:S(2)}) collective-permute-start(bf16[64,64,512]{2,1,0:T(8,128)(2,1)} %bitcast.3.mine_ref.got_ref), channel_id=1, source_target_pairs={{0,1},{1,0},{2,3},{3,2},{4,5},{5,4},{6,7},{7,6},{8,9},{9,8},{10,11... | collective-permute-start | bytes 12582920 | tf_op jit(solution)/shard_map/ppermute | solution.py:433
  88.1 14.8 %collective-permute-start.14 = (bf16[2048,128]{1,0:T(8,128)(2,1)S(1)}, bf16[2048,128]{1,0:T(8,128)(2,1)S(1)}, u32[]{:S(2)}, u32[]{:S(2)}) collective-permute-start(bf16[2048,128]{1,0:T(8,128)(2,1)S(1)} %copy-done), channel_id=1, source_target_pairs={{0,6},{1,7},{2,4},{3,5},{4,2},{5,3},{6,0},{7,1},{8,14},{9,15},{10,... | collective-permute-start | bytes 1572872 | tf_op jit(solution)/shard_map/ppermute | solution.py:433
  94.8 9.0 %collective-permute-start.5 = (bf16[2048,128]{1,0:T(8,128)(2,1)S(1)}, bf16[2048,128]{1,0:T(8,128)(2,1)S(1)}, u32[]{:S(2)}, u32[]{:S(2)}) collective-permute-start(bf16[2048,128]{1,0:T(8,128)(2,1)S(1)} %copy-done), channel_id=1, source_target_pairs={{0,1},{1,0},{2,3},{3,2},{4,5},{5,4},{6,7},{7,6},{8,9},{9,8},{10,11... | collective-permute-start | bytes 1572872 | tf_op jit(solution)/shard_map/ppermute | solution.py:433
  95.3 9.3 %collective-permute-start.6 = (bf16[2048,128]{1,0:T(8,128)(2,1)S(1)}, bf16[2048,128]{1,0:T(8,128)(2,1)S(1)}, u32[]{:S(2)}, u32[]{:S(2)}) collective-permute-start(bf16[2048,128]{1,0:T(8,128)(2,1)S(1)} %copy-done.1), channel_id=1, source_target_pairs={{0,1},{1,0},{2,3},{3,2},{4,5},{5,4},{6,7},{7,6},{8,9},{9,8},{10,11... | collective-permute-start | bytes 1572872 | tf_op jit(solution)/shard_map/ppermute | solution.py:433
  96.1 9.6 %collective-permute-start.7 = (bf16[128,2048]{1,0:T(8,128)(2,1)S(1)}, bf16[128,2048]{1,0:T(8,128)(2,1)S(1)}, u32[]{:S(2)}, u32[]{:S(2)}) collective-permute-start(bf16[128,2048]{1,0:T(8,128)(2,1)S(1)} %copy-done.2), channel_id=1, source_target_pairs={{0,1},{1,0},{2,3},{3,2},{4,5},{5,4},{6,7},{7,6},{8,9},{9,8},{10,11... | collective-permute-start | bytes 1572872 | tf_op jit(solution)/shard_map/ppermute | solution.py:433
  102.9 3.6 %collective-permute-start.3 = (f32[2,16,2048]{2,1,0:T(8,128)S(1)}, f32[2,16,2048]{2,1,0:T(8,128)S(1)}, u32[]{:S(2)}, u32[]{:S(2)}) collective-permute-start(f32[2,16,2048]{2,1,0:T(8,128)S(1)} %get-tuple-element.17), channel_id=1, source_target_pairs={{0,1},{1,0},{2,3},{3,2},{4,5},{5,4},{6,7},{7,6},{8,9},{9,8},{10,11... | collective-permute-start | bytes 786440 | tf_op jit(solution)/shard_map/ppermute | solution.py:433
  104.5 14.6 %collective-permute-start.20 = (bf16[2048,128]{1,0:T(8,128)(2,1)S(1)}, bf16[2048,128]{1,0:T(8,128)(2,1)S(1)}, u32[]{:S(2)}, u32[]{:S(2)}) collective-permute-start(bf16[2048,128]{1,0:T(8,128)(2,1)S(1)} %collective-permute-done.8.refs_7_), channel_id=1, source_target_pairs={{0,6},{1,7},{2,4},{3,5},{4,2},{5,3},{6,0},{7,1},{8,14},{9,15},{10,... | collective-permute-start | bytes 1572872 | tf_op jit(solution)/shard_map/ppermute | solution.py:433
  105.4 27.6 %collective-permute-start.11 = (bf16[2048,128]{1,0:T(8,128)(2,1)S(1)}, bf16[2048,128]{1,0:T(8,128)(2,1)S(1)}, u32[]{:S(2)}, u32[]{:S(2)}) collective-permute-start(bf16[2048,128]{1,0:T(8,128)(2,1)S(1)} %collective-permute-done.8.refs_7_), channel_id=1, source_target_pairs={{0,1},{1,0},{2,3},{3,2},{4,5},{5,4},{6,7},{7,6},{8,9},{9,8},{10,11... | collective-permute-start | bytes 1572872 | tf_op jit(solution)/shard_map/ppermute | solution.py:433
  106.5 13.5 %collective-permute-start.21 = (bf16[2048,128]{1,0:T(8,128)(2,1)}, bf16[2048,128]{1,0:T(8,128)(2,1)S(1)}, u32[]{:S(2)}, u32[]{:S(2)}) collective-permute-start(bf16[2048,128]{1,0:T(8,128)(2,1)} %collective-permute-done.15.refs_14_), channel_id=1, source_target_pairs={{0,2},{1,3},{2,0},{3,1},{4,6},{5,7},{6,4},{7,5},{8,10},{9,11},{10,... | collective-permute-start | bytes 1572872 | tf_op jit(solution)/shard_map/ppermute | solution.py:433
  106.5 24.7 %collective-permute-start.22 = (bf16[128,2048]{1,0:T(8,128)(2,1)}, bf16[128,2048]{1,0:T(8,128)(2,1)S(1)}, u32[]{:S(2)}, u32[]{:S(2)}) collective-permute-start(bf16[128,2048]{1,0:T(8,128)(2,1)} %collective-permute-done.16.refs_15_), channel_id=1, source_target_pairs={{0,2},{1,3},{2,0},{3,1},{4,6},{5,7},{6,4},{7,5},{8,10},{9,11},{10,... | collective-permute-start | bytes 1572872 | tf_op jit(solution)/shard_map/ppermute | solution.py:433
  119.2 14.9 %collective-permute-start.4 = (f32[16,2048]{1,0:T(8,128)S(1)}, f32[16,2048]{1,0:T(8,128)S(1)}, u32[]{:S(2)}, u32[]{:S(2)}) collective-permute-start(f32[16,2048]{1,0:T(8,128)S(1)} %fusion), channel_id=1, source_target_pairs={{0,2},{1,3},{2,0},{3,1},{4,6},{5,7},{6,4},{7,5},{8,10},{9,11},{10,... | collective-permute-start | bytes 393224 | tf_op jit(solution)/shard_map/ppermute | solution.py:433
  120.0 21.5 %collective-permute-start.18 = (bf16[2048,128]{1,0:T(8,128)(2,1)}, bf16[2048,128]{1,0:T(8,128)(2,1)}, u32[]{:S(2)}, u32[]{:S(2)}) collective-permute-start(bf16[2048,128]{1,0:T(8,128)(2,1)} %collective-permute-done.15.refs_14_), channel_id=1, source_target_pairs={{0,1},{1,0},{2,3},{3,2},{4,5},{5,4},{6,7},{7,6},{8,9},{9,8},{10,11... | collective-permute-start | bytes 1572872 | tf_op jit(solution)/shard_map/ppermute | solution.py:433
  131.3 10.7 %collective-permute-start.19 = (bf16[128,2048]{1,0:T(8,128)(2,1)}, bf16[128,2048]{1,0:T(8,128)(2,1)}, u32[]{:S(2)}, u32[]{:S(2)}) collective-permute-start(bf16[128,2048]{1,0:T(8,128)(2,1)} %collective-permute-done.16.refs_15_), channel_id=1, source_target_pairs={{0,1},{1,0},{2,3},{3,2},{4,5},{5,4},{6,7},{7,6},{8,9},{9,8},{10,11... | collective-permute-start | bytes 1572872 | tf_op jit(solution)/shard_map/ppermute | solution.py:433
  133.7 8.4 %collective-permute-start.12 = (bf16[2048,128]{1,0:T(8,128)(2,1)}, bf16[2048,128]{1,0:T(8,128)(2,1)}, u32[]{:S(2)}, u32[]{:S(2)}) collective-permute-start(bf16[2048,128]{1,0:T(8,128)(2,1)} %collective-permute-done.9.refs_8_), channel_id=1, source_target_pairs={{0,1},{1,0},{2,3},{3,2},{4,5},{5,4},{6,7},{7,6},{8,9},{9,8},{10,11... | collective-permute-start | bytes 1572872 | tf_op jit(solution)/shard_map/ppermute | solution.py:433
  134.1 8.4 %collective-permute-start.13 = (bf16[128,2048]{1,0:T(8,128)(2,1)}, bf16[128,2048]{1,0:T(8,128)(2,1)}, u32[]{:S(2)}, u32[]{:S(2)}) collective-permute-start(bf16[128,2048]{1,0:T(8,128)(2,1)} %collective-permute-done.10.refs_9_), channel_id=1, source_target_pairs={{0,1},{1,0},{2,3},{3,2},{4,5},{5,4},{6,7},{7,6},{8,9},{9,8},{10,11... | collective-permute-start | bytes 1572872 | tf_op jit(solution)/shard_map/ppermute | solution.py:433
  136.3 22.5 %all-to-all-start.1 = ((bf16[16,16,2048]{2,1,0:T(8,128)(2,1)}), bf16[16,16,2048]{2,1,0:T(8,128)(2,1)S(1)}, u32[]{:S(2)}, u32[]{:S(2)}) async-start(bf16[16,16,2048]{2,1,0:T(8,128)(2,1)} %get-tuple-element.18), calls=%async_computation.1 | async-start | bytes 2097152 | tf_op jit(solution)/shard_map/all_to_all | solution.py:443
  142.5 3.7 %collective-permute-start.25 = (bf16[128,2048]{1,0:T(8,128)(2,1)}, bf16[128,2048]{1,0:T(8,128)(2,1)S(1)}, u32[]{:S(2)}, u32[]{:S(2)}) collective-permute-start(bf16[128,2048]{1,0:T(8,128)(2,1)} %copy-done.17), channel_id=1, source_target_pairs={{0,1},{1,0},{2,3},{3,2},{4,5},{5,4},{6,7},{7,6},{8,9},{9,8},{10,11... | collective-permute-start | bytes 1572872 | tf_op jit(solution)/shard_map/ppermute | solution.py:433
  (38 other events, 344.3 us)

commit v7 on v5

--- a/solution.py
+++ b/solution.py
@@ -19,53 +19,70 @@
     return pl.CostEstimate(flops=int(us * 4e8), bytes_accessed=int(us * 2e6), transcendentals=0)
 
 
-def outgoing_kernel(half_ref, slot_ref, count_ref, pool_ref, out_ref, sems):
-    pages, rows, _ = out_ref.shape
+def outgoing_kernel(
+    mine_ref, twist_ref, slot_ref, count_ref, pool_ref, a_ref, b_ref, sems
+):
+    pages, quarter, _ = a_ref.shape
+    rest = b_ref.shape[1]
     caps = pages // count_ref.shape[0]
-    first = pl.multiple_of(half_ref[0] * rows, rows)
-
-    def copy(i):
-        src = pool_ref.at[slot_ref[i // caps, i % caps], pl.ds(first, rows), :]
-        return pltpu.make_async_copy(src, out_ref.at[i], sems.at[i])
-
-    copies = [copy(i) for i in range(pages)]
-    for c in copies:
-        c.start()
-    for i, c in enumerate(copies):
-        c.wait()
+    core = lax.rem(mine_ref[0], 2)
+    low = pl.multiple_of(4 * quarter + core * rest, rest)
+
+    def copies(i):
+        page = slot_ref[i // caps, i % caps]
+        side = lax.rem(twist_ref[0] + (i // caps) % 2, 2)
+        first = pl.multiple_of((2 * side + core) * quarter, quarter)
+        return (
+            pltpu.make_async_copy(
+                pool_ref.at[page, pl.ds(first, quarter), :], a_ref.at[i], sems.at[2 * i]
+            ),
+            pltpu.make_async_copy(
+                pool_ref.at[page, pl.ds(low, rest), :], b_ref.at[i], sems.at[2 * i + 1]
+            ),
+        )
+
+    pending = [copies(i) for i in range(pages)]
+    for pair in pending:
+        for c in pair:
+            c.start()
+    for i, pair in enumerate(pending):
+        for c in pair:
+            c.wait()
 
         @pl.when(i % caps >= count_ref[i // caps])
         def _():
-            out_ref[i] = jnp.zeros(out_ref.shape[1:], out_ref.dtype)
-
-
-def outgoing_pages(half, slots, counts, pool):
+            a_ref[i] = jnp.zeros(a_ref.shape[1:], a_ref.dtype)
+            b_ref[i] = jnp.zeros(b_ref.shape[1:], b_ref.dtype)
+
+
+def outgoing_pages(mine, twist, slots, counts, pool):
     pages = slots.size
-    rows = pool.shape[1] // 2
+    page_len, width = pool.shape[1:]
+    shapes = [(pages, page_len // 8, width), (pages, page_len // 4, width)]
     return pl.pallas_call(
         outgoing_kernel,
         grid_spec=pltpu.PrefetchScalarGridSpec(
-            num_scalar_prefetch=3,
+            num_scalar_prefetch=4,
             grid=(1,),
             in_specs=[pl.BlockSpec(memory_space=pltpu.HBM)],
-            out_specs=pl.BlockSpec((pages, rows, pool.shape[2]), lambda i, *_: (0, 0, 0)),
-            scratch_shapes=[pltpu.SemaphoreType.DMA((pages,))],
+            out_specs=[pl.BlockSpec(x, lambda i, *_: (0, 0, 0)) for x in shapes],
+            scratch_shapes=[pltpu.SemaphoreType.DMA((2 * pages,))],
         ),
-        out_shape=jax.ShapeDtypeStruct((pages, rows, pool.shape[2]), pool.dtype),
+        out_shape=[jax.ShapeDtypeStruct(x, pool.dtype) for x in shapes],
         compiler_params=params(60),
         cost_estimate=cost(3),
         name="outgoing",
-    )(half, slots, counts, pool)
-
-
-def chunk_step(block, base, qt, full, part, acc, stat):
+    )(mine, twist, slots, counts, pool)
+
+
+def chunk_step(block, base, first, qt, full, part, acc, stat):
     pages, rows, width = block.shape
     hd = width // 2
     lanes = qt.shape[1]
     keys = block[:, :, :hd].reshape(pages * rows, hd)
     values = block[:, :, hd:].reshape(pages * rows, hd)
     s = jnp.dot(keys, qt[...], preferred_element_type=F32)
-    spot = lax.broadcasted_iota(jnp.int32, (rows, lanes), 0)
+    spot = lax.broadcasted_iota(jnp.int32, (rows, lanes), 0) + first
     old = stat[0:1, :]
     tops = jnp.full((8, lanes), NEG, F32)
     counts = []
@@ -94,18 +111,18 @@
     )
 
 
-def tables(first, half, rows, tab_ref, len_ref, full, part):
+def tables(first, page_len, tab_ref, len_ref, full, part):
     entries, lanes = full.shape
     page_id = lax.broadcasted_iota(jnp.int32, (entries, lanes), 0) + first
     whole = jnp.zeros((entries, lanes), F32)
     rest = jnp.zeros((entries, lanes), jnp.int32)
     for j in range(tab_ref.shape[0]):
         hit = page_id == tab_ref[j : j + 1, :]
-        kept = len_ref[...] - j * 2 * rows
-        whole += jnp.where(hit & (kept >= 2 * rows), 1.0, 0.0)
-        rest += jnp.where(hit & (kept > 0) & (kept < 2 * rows), kept, 0)
+        kept = len_ref[...] - j * page_len
+        whole += jnp.where(hit & (kept >= page_len), 1.0, 0.0)
+        rest += jnp.where(hit & (kept > 0) & (kept < page_len), kept, 0)
     full[...] = whole
-    part[...] = rest - half * rows
+    part[...] = rest
 
 
 def resident_kernel(
@@ -134,7 +151,7 @@
             load(k).start()
         q = jnp.concatenate([qa_ref[...], qb_ref[...]], axis=0)
         qt_ref[...] = q.T
-        tables(0, half_ref[0], rows, tab_ref, len_ref, full, part)
+        tables(0, 2 * rows, tab_ref, len_ref, full, part)
         s = jnp.dot(entry_ref[:, :hd], qt_ref[...], preferred_element_type=F32)
         game = lax.broadcasted_iota(jnp.int32, s.shape, 0)
         lane = lax.broadcasted_iota(jnp.int32, s.shape, 1)
@@ -149,7 +166,7 @@
 
     load(i).wait()
     at = pl.ds(pl.multiple_of(i * pages, pages), pages)
-    chunk_step(held.at[at], i * pages, qt_ref, full, part, acc_ref, stat_ref)
+    chunk_step(held.at[at], i * pages, first, qt_ref, full, part, acc_ref, stat_ref)
 
 
 def resident(half, q_mine, q_peer, entry, table, lengths, pool):
@@ -193,47 +210,60 @@
 
 
 def moved_kernel(
-    half_ref, qt_ref, tab_ref, len_ref, acc_in, stat_in, got_ref,
+    mine_ref, qt_ref, tab_ref, len_ref, acc_in, stat_in, a_ref, z_ref, b_ref,
     keep_ref, send_ref, acc, stat, full, part,
 ):
     i = pl.program_id(0)
-    pages, rows, width = got_ref.shape
+    quarter = a_ref.shape[1]
+    pages, rest, width = b_ref.shape
     hd = width // 2
-    mine = qt_ref.shape[1] // 2
+    half = qt_ref.shape[1] // 2
+    m = mine_ref[0]
+    core = lax.rem(m, 2)
+    state = (qt_ref, full, part, acc, stat)
 
     @pl.when(i == 0)
     def _():
-        tables(full.shape[0], half_ref[0], rows, tab_ref, len_ref, full, part)
+        tables(full.shape[0], 8 * quarter, tab_ref, len_ref, full, part)
         acc[...] = acc_in[...]
         stat[...] = stat_in[...]
-
-    chunk_step(got_ref, i * pages, qt_ref, full, part, acc, stat)
+        chunk_step(a_ref, 0, m * quarter, *state)
+
+    @pl.when(i == 1)
+    def _():
+        chunk_step(z_ref, 0, lax.rem(m + 2, 4) * quarter, *state)
+
+    @pl.when(i >= 2)
+    def _():
+        chunk_step(b_ref, (i - 2) * pages, 4 * quarter + core * rest, *state)
 
     @pl.when(i == pl.num_programs(0) - 1)
     def _():
         for k, out in enumerate((keep_ref, send_ref)):
-            out[:hd, :] = acc[:, k * mine : (k + 1) * mine]
-            out[hd : hd + 8, :] = stat[:, k * mine : (k + 1) * mine]
-
-
-def moved(half, qt, table, lengths, acc, stat, got):
-    slots, rows, width = got.shape
+            out[:hd, :] = acc[:, k * half : (k + 1) * half]
+            out[hd : hd + 8, :] = stat[:, k * half : (k + 1) * half]
+
+
+def moved(mine, qt, table, lengths, acc, stat, got_a, got_z, got_b):
+    slots, rest, width = got_b.shape
     hd, lanes = qt.shape
-    block = 16
+    block = slots // 2
     whole = lambda shape: pl.BlockSpec(shape, lambda i, *_: (0,) * len(shape))
     out = jax.ShapeDtypeStruct((hd + 8, lanes // 2), F32)
     return pl.pallas_call(
         moved_kernel,
         grid_spec=pltpu.PrefetchScalarGridSpec(
             num_scalar_prefetch=1,
-            grid=(slots // block,),
+            grid=(4,),
             in_specs=[
                 whole(qt.shape),
                 whole(table.shape),
                 whole(lengths.shape),
                 whole(acc.shape),
                 whole(stat.shape),
-                pl.BlockSpec((block, rows, width), lambda i, *_: (i, 0, 0)),
+                whole(got_a.shape),
+                whole(got_z.shape),
+                pl.BlockSpec((block, rest, width), lambda i, *_: (jnp.maximum(i - 2, 0), 0, 0)),
             ],
             out_specs=[whole(out.shape), whole(out.shape)],
             scratch_shapes=[
@@ -247,7 +277,7 @@
         compiler_params=params(40),
         cost_estimate=cost(8),
         name="moved",
-    )(half, qt, table, lengths, acc, stat, got)
+    )(mine, qt, table, lengths, acc, stat, got_a, got_z, got_b)
 
 
 def project_kernel(mine_ref, a_ref, b_ref, w_ref, keep_ref, send_ref, scratch):
@@ -393,29 +423,40 @@
     )(parts, stream)
 
 
-def assemble_kernel(half_ref, mine_ref, peer_ref, out_ref):
-    rows = mine_ref.shape[1]
-    for ref, h in ((mine_ref, half_ref[0]), (peer_ref, 1 - half_ref[0])):
-        out_ref[:, pl.ds(pl.multiple_of(h * rows, rows), rows), :] = ref[...]
-
-
-def assemble(half, mine, peer):
-    pages, rows, width = mine.shape
+def assemble_kernel(mine_ref, *refs):
+    out_ref = refs[6]
+    m = mine_ref[0]
+    core, side = lax.rem(m, 2), m // 2
+    for c, (a, z, b) in ((core, refs[:3]), (1 - core, refs[3:6])):
+        quarter, rest = a.shape[1], b.shape[1]
+        for ref, first in (
+            (a, (2 * side + c) * quarter),
+            (z, (2 * (1 - side) + c) * quarter),
+            (b, 4 * quarter + c * rest),
+        ):
+            rows = ref.shape[1]
+            out_ref[:, pl.ds(pl.multiple_of(first, rows), rows), :] = ref[...]
+
+
+def assemble(mine, parts):
+    pages, quarter, width = parts[0].shape
     block = 8
-    spec = pl.BlockSpec((block, rows, width), lambda i, *_: (i, 0, 0))
+    page_len = 8 * quarter
     return pl.pallas_call(
         assemble_kernel,
         grid_spec=pltpu.PrefetchScalarGridSpec(
             num_scalar_prefetch=1,
             grid=(pages // block,),
-            in_specs=[spec, spec],
-            out_specs=pl.BlockSpec((block, 2 * rows, width), lambda i, *_: (i, 0, 0)),
+            in_specs=[
+                pl.BlockSpec((block, p.shape[1], width), lambda i, *_: (i, 0, 0)) for p in parts
+            ],
+            out_specs=pl.BlockSpec((block, page_len, width), lambda i, *_: (i, 0, 0)),
         ),
-        out_shape=jax.ShapeDtypeStruct((pages, 2 * rows, width), mine.dtype),
+        out_shape=jax.ShapeDtypeStruct((pages, page_len, width), parts[0].dtype),
         compiler_params=params(8),
         cost_estimate=cost(6),
         name="assemble",
-    )(half, mine, peer)
+    )(mine, *parts)
 
 
 def step(
@@ -426,7 +467,6 @@
     n_dp, n_mp = lax.axis_size("dp"), lax.axis_size("mp")
     devices = n_dp * n_mp
     games, heads, hd = queries.shape
-    page_len, width = page_pool.shape[1:]
     mine = lax.axis_index("mp").reshape(1)
     half = mine % 2
     swap = lambda bit: [(k, k ^ bit) for k in range(devices)]
@@ -444,10 +484,12 @@
         a, axes, 0, 0, tiled=True, axis_index_groups=who
     )
 
-    out_pages = outgoing_pages(half, send_slots, move_count.reshape(-1), page_pool)
-    got = exchange(
-        out_pages.reshape(n_dp, -1, page_len // 2, width), groups
-    ).reshape(out_pages.shape)
+    twist = (mine // 2 + lax.axis_index("dp")) % 2
+    out_a, out_b = outgoing_pages(mine, twist, send_slots, move_count.reshape(-1), page_pool)
+    spread_out = lambda a: exchange(a.reshape(n_dp, -1, *a.shape[1:]), groups).reshape(a.shape)
+    got_a = spread_out(out_a)
+    got_b = spread_out(out_b)
+    got_z = send(got_a, side)
 
     q_mine = (queries.transpose(1, 0, 2) * jnp.asarray(hd**-0.5, BF)).reshape(
         heads * games, hd
@@ -459,9 +501,13 @@
 
     weights = (gate_proj, up_proj, down_proj)
     each = lambda ws, pairs: tuple(send(a, pairs) for a in ws)
-    w_side = each(weights, side)
+    side_gate, side_up = send(weights[0], side), send(weights[1], side)
+    side_down = send(weights[2], side)
+    w_side = (side_gate, side_up, side_down)
     w_core = each(weights, core)
-    w_side_core = each(w_side, core)
+    side_core_gate, side_core_up = send(side_gate, core), send(side_up, core)
+    side_core_down = send(side_down, core)
+    w_side_core = (side_core_gate, side_core_up, side_core_down)
     far_up, far_down, far_gate = (send(weights[k], far) for k in (1, 2, 0))
     w_far = (far_gate, far_up, far_down)
     diag_gate = send(w_side[0], far)
@@ -475,13 +521,13 @@
     ]
 
     acc, stat, qt = resident(half, q_mine, q_peer, new_entry, table, lengths, page_pool)
-    keep, give = moved(half, qt, table, lengths, acc, stat, got)
+    keep, give = moved(mine, qt, table, lengths, acc, stat, got_a, got_z, got_b)
     other = send(give, core)
-    got_peer = send(got, core)
+    got_peer = each((got_a, got_z, got_b), core)
     hold, pass_on = project(mine, keep, other, out_proj, games)
     hold_got = send(pass_on, core)
     side_got = send(hold[1] + hold_got[1], side)
-    arrived = assemble(half, got, got_peer)
+    arrived = assemble(mine, (got_a, got_z, got_b, *got_peer))
 
     spread, stream = norm(
         mine, hold, hold_got, side_got, residual, ffn_gain.reshape(1, -1), peers

time: 216 us -> 214 us (level)
  waiting for transfers between devices: 95.7 us -> 67.8 us
  starting transfers between devices: 34.3 us -> 46.6 us
  blocking collectives: 27.5 us -> 38 us
  local copies, waits for them, and re-layouts: 21.2 us -> 24.9 us
    all_to_all x2 -> x3, waiting for transfers between devices: 59.7 us -> 34.5 us  [step(): lax.all_to_all(a, axes, 0, 0, tiled=True, axis_index_groups=who)]
    ppermute x26 -> x29, starting transfers between devices: 17.4 us -> 31.4 us  [step(): send = lambda a, pairs: lax.ppermute(a, axes, pairs)]
    all_to_all x1, blocking collectives: 20 us -> 29.4 us  [step(): lax.all_to_all(a, axes, 0, 0, tiled=True, axis_index_groups=who)]
    unnamed x70 -> x88, local copies, waits for them, and re-layouts: 21 us -> 24.7 us
    ppermute x26 -> x29, waiting for transfers between devices: 36 us -> 33.3 us  [step(): send = lambda a, pairs: lax.ppermute(a, axes, pairs)]
    all_to_all x2 -> x3, starting transfers between devices: 16.9 us -> 15.2 us  [step(): lax.all_to_all(a, axes, 0, 0, tiled=True, axis_index_groups=who)]
  transfers between devices with their start and end apart: 28 -> 32, of which waited for: 10 -> 11; matrix products, arithmetic and copies ran while one was open for 0% -> 0% of each run, Pallas kernels for 10% -> 13%
where the time goes in v7:
time: 214 us; the launch traced here: 213 us
  waiting for transfers between devices  67.8 us (32%)
  starting transfers between devices  46.6 us (22%)
  blocking collectives  38 us (18%)
  Pallas kernels  34.4 us (16%)
  local copies, waits for them, and re-layouts  24.9 us (12%)
    all_to_all x3, waiting for transfers between devices, step(): lax.all_to_all(a, axes, 0, 0, tiled=True, axis_index_groups=who)  34.5 us
    ppermute x29, waiting for transfers between devices, step(): send = lambda a, pairs: lax.ppermute(a, axes, pairs)  33.3 us
    ppermute x29, starting transfers between devices, step(): send = lambda a, pairs: lax.ppermute(a, axes, pairs)  31.4 us
    all_to_all x1, blocking collectives, step(): lax.all_to_all(a, axes, 0, 0, tiled=True, axis_index_groups=who)  29.4 us
    unnamed x88, local copies, waits for them, and re-layouts  24.7 us
    all_to_all x3, starting transfers between devices, step(): lax.all_to_all(a, axes, 0, 0, tiled=True, axis_index_groups=who)  15.2 us
    all_gather x1, blocking collectives, step(): layer_out = lax.all_gather(quarter, 'mp', axis=0, tiled=True)  8.63 us
    pallas_call x1, Pallas kernels, assemble(): pl.pallas_call(assemble_kernel, grid_spec=pltpu.PrefetchScalarGridSpec(nu...  7.87 us
  transfers between devices with their start and end apart: 32, of which 11 were waited for; matrix products, arithmetic and copies ran while one was open for 0% of the time, Pallas kernels for 13%

profile of v7, /device:TPU:1, one launch (start us, length us, event | category | flops | bytes accessed | tf_op | source)
XLA Modules:
  0.0 212.7 jit_solution(5611300024987514933)
XLA Ops:
  2.0 5.7 %outgoing.1 = (bf16[64,16,512]{2,1,0:T(8,128)(2,1)}, bf16[64,32,512]{2,1,0:T(8,128)(2,1)}) custom-call(s32[1]{0:T(128)} %bitcast.mine_ref, s32[1]{0:T(128)S(6)} %select_n.17.twist_ref, s32[32,2]{1,0:T(8,128)} %copy.15.slot_ref, s32[32]{0:T(128)} %bitcast.31, bf16[64,128,512]{2,1,0:T(8,128)(2,1)} %pool_ref.3), custom_call_target="tpu_custom_call" | custom-call | flops 1200000000 | bytes 6000000 | tf_op jit(solution)/shard_map/outgoing/pallas_call | solution.py:62
  7.8 29.4 %all_to_all.20 = bf16[32,2,16,512]{3,2,1,0:T(8,128)(2,1)S(1)} all-to-all(bf16[32,2,16,512]{3,2,1,0:T(8,128)(2,1)} %bitcast.29), channel_id=1, replica_groups={{0,6,8,14,16,22,24,30,32,38,40,46,48,54,56,62,64,70,72,78,80,86,88,94,9..., dimensions={0} | all-to-all | bytes 2097152 | tf_op jit(solution)/shard_map/all_to_all | solution.py:483
  37.2 4.2 %all-to-all-start.1 = ((bf16[32,2,32,512]{3,2,1,0:T(8,128)(2,1)}), bf16[32,2,32,512]{3,2,1,0:T(8,128)(2,1)S(1)}, u32[]{:S(2)}, u32[]{:S(2)}) async-start(bf16[32,2,32,512]{3,2,1,0:T(8,128)(2,1)} %bitcast.28), calls=%async_computation.1 | async-start | bytes 4194304 | tf_op jit(solution)/shard_map/all_to_all | solution.py:483
  43.5 2.6 %collective-permute-start.18 = (bf16[2048,128]{1,0:T(8,128)(2,1)}, bf16[2048,128]{1,0:T(8,128)(2,1)}, u32[]{:S(2)}, u32[]{:S(2)}) collective-permute-start(bf16[2048,128]{1,0:T(8,128)(2,1)} %refs_2_.1), channel_id=1, source_target_pairs={{0,6},{1,7},{2,4},{3,5},{4,2},{5,3},{6,0},{7,1},{8,14},{9,15},{10,... | collective-permute-start | bytes 1572872 | tf_op jit(solution)/shard_map/ppermute | solution.py:473
  48.1 5.8 %resident.1 = (f32[256,256]{1,0:T(8,128)S(1)}, f32[8,256]{1,0:T(8,128)S(1)}, bf16[256,256]{1,0:T(8,128)(2,1)S(1)}) custom-call(s32[1]{0:T(128)S(6)} %select_n.18.half_ref, bf16[128,256]{1,0:T(8,128)(2,1)S(1)} %bitcast.26, bf16[128,256]{1,0:T(8,128)(2,1)S(1)} %collective-permute-done.4.qb_ref, bf16[64,512]{1,0:T(8,128)(2,1)S(1)} %copy-done.36, ...), custom_call_target="tpu_custom_call" | custom-call | flops 3200000000 | bytes 16000000 | tf_op jit(solution)/shard_map/resident/pallas_call | solution.py:184
  54.6 15.6 %all-to-all-done.1 = bf16[32,2,32,512]{3,2,1,0:T(8,128)(2,1)S(1)} async-done(((bf16[32,2,32,512]{3,2,1,0:T(8,128)(2,1)}), bf16[32,2,32,512]{3,2,1,0:T(8,128)(2,1)S(1)}, u32[]{:S(2)}, u32[]{:S(2)}) %all-to-all-start.1) | async-done | bytes 2097184 | tf_op jit(solution)/shard_map/all_to_all | solution.py:483
  71.2 6.2 %moved.1 = (f32[264,128]{1,0:T(8,128)S(1)}, f32[264,128]{1,0:T(8,128)S(1)}) custom-call(s32[1]{0:T(128)} %bitcast.mine_ref, bf16[256,256]{1,0:T(8,128)(2,1)S(1)} %get-tuple-element.15.qt_ref, s32[16,256]{1,0:T(8,128)S(1)} %tile.18.tab_ref, s32[1,256]{1,0:T(1,128)S(1)} %tile.20.len_ref, f32[256,256]{1,0:T(8,128)S(1)} %copy-done.39, ...), custom_call_target="tpu_custom_call" | custom-call | flops 3200000000 | bytes 16000000 | tf_op jit(solution)/shard_map/moved/pallas_call | solution.py:253
  77.4 2.6 %collective-permute-start.5 = (f32[264,128]{1,0:T(8,128)S(1)}, f32[264,128]{1,0:T(8,128)S(1)}, u32[]{:S(2)}, u32[]{:S(2)}) collective-permute-start(f32[264,128]{1,0:T(8,128)S(1)} %get-tuple-element.19), channel_id=1, source_target_pairs={{0,1},{1,0},{2,3},{3,2},{4,5},{5,4},{6,7},{7,6},{8,9},{9,8},{10,11... | collective-permute-start | bytes 405512 | tf_op jit(solution)/shard_map/ppermute | solution.py:473
  80.0 6.8 %collective-permute-done.11.refs_7_ = bf16[2048,128]{1,0:T(8,128)(2,1)} collective-permute-done((bf16[2048,128]{1,0:T(8,128)(2,1)}, bf16[2048,128]{1,0:T(8,128)(2,1)}, u32[]{:S(2)}, u32[]{:S(2)}) %collective-permute-start.11) | collective-permute-done | bytes 524320 | tf_op jit(solution)/shard_map/ppermute | solution.py:473
  87.1 2.0 collective-permute-start.17
  90.2 2.2 %collective-permute-start.10 = (bf16[128,2048]{1,0:T(8,128)(2,1)S(1)}, bf16[128,2048]{1,0:T(8,128)(2,1)S(1)}, u32[]{:S(2)}, u32[]{:S(2)}) collective-permute-start(bf16[128,2048]{1,0:T(8,128)(2,1)S(1)} %copy-done.8), channel_id=1, source_target_pairs={{0,1},{1,0},{2,3},{3,2},{4,5},{5,4},{6,7},{7,6},{8,9},{9,8},{10,11... | collective-permute-start | bytes 1572872 | tf_op jit(solution)/shard_map/ppermute | solution.py:473
  93.7 3.9 %collective-permute-done.13.refs_9_ = bf16[128,2048]{1,0:T(8,128)(2,1)} collective-permute-done((bf16[128,2048]{1,0:T(8,128)(2,1)S(1)}, bf16[128,2048]{1,0:T(8,128)(2,1)}, u32[]{:S(2)}, u32[]{:S(2)}) %collective-permute-start.13) | collective-permute-done | bytes 524320 | tf_op jit(solution)/shard_map/ppermute | solution.py:473
  97.6 3.7 %collective-permute-start.9 = (bf16[2048,128]{1,0:T(8,128)(2,1)S(1)}, bf16[2048,128]{1,0:T(8,128)(2,1)S(1)}, u32[]{:S(2)}, u32[]{:S(2)}) collective-permute-start(bf16[2048,128]{1,0:T(8,128)(2,1)S(1)} %copy-done.6), channel_id=1, source_target_pairs={{0,1},{1,0},{2,3},{3,2},{4,5},{5,4},{6,7},{7,6},{8,9},{9,8},{10,11... | collective-permute-start | bytes 1572872 | tf_op jit(solution)/shard_map/ppermute | solution.py:473
  101.2 2.0 collective-permute-start.23
  106.8 7.9 %collective-permute-done.23.refs_19_ = bf16[2048,128]{1,0:T(8,128)(2,1)S(1)} collective-permute-done((bf16[2048,128]{1,0:T(8,128)(2,1)}, bf16[2048,128]{1,0:T(8,128)(2,1)S(1)}, u32[]{:S(2)}, u32[]{:S(2)}) %collective-permute-start.23) | collective-permute-done | bytes 524320 | tf_op jit(solution)/shard_map/ppermute | solution.py:473
  114.7 2.2 %collective-permute-start.21 = (bf16[2048,128]{1,0:T(8,128)(2,1)}, bf16[2048,128]{1,0:T(8,128)(2,1)}, u32[]{:S(2)}, u32[]{:S(2)}) collective-permute-start(bf16[2048,128]{1,0:T(8,128)(2,1)} %collective-permute-done.18.refs_14_), channel_id=1, source_target_pairs={{0,1},{1,0},{2,3},{3,2},{4,5},{5,4},{6,7},{7,6},{8,9},{9,8},{10,11... | collective-permute-start | bytes 1572872 | tf_op jit(solution)/shard_map/ppermute | solution.py:473
  120.1 9.7 %collective-permute-done.25.refs_21_ = bf16[128,2048]{1,0:T(8,128)(2,1)S(1)} collective-permute-done((bf16[128,2048]{1,0:T(8,128)(2,1)}, bf16[128,2048]{1,0:T(8,128)(2,1)S(1)}, u32[]{:S(2)}, u32[]{:S(2)}) %collective-permute-start.25) | collective-permute-done | bytes 524320 | tf_op jit(solution)/shard_map/ppermute | solution.py:473
  134.8 6.6 %all-to-all-start.2 = ((bf16[16,16,2048]{2,1,0:T(8,128)(2,1)}), bf16[16,16,2048]{2,1,0:T(8,128)(2,1)S(1)}, u32[]{:S(2)}, u32[]{:S(2)}) async-start(bf16[16,16,2048]{2,1,0:T(8,128)(2,1)} %copy-done.3), calls=%async_computation.2 | async-start | bytes 2097152 | tf_op jit(solution)/shard_map/all_to_all | solution.py:483
  147.4 11.4 %all-to-all-done.2 = bf16[16,16,2048]{2,1,0:T(8,128)(2,1)S(1)} async-done(((bf16[16,16,2048]{2,1,0:T(8,128)(2,1)}), bf16[16,16,2048]{2,1,0:T(8,128)(2,1)S(1)}, u32[]{:S(2)}, u32[]{:S(2)}) %all-to-all-start.2) | async-done | bytes 1048608 | tf_op jit(solution)/shard_map/all_to_all | solution.py:483
  174.4 6.6 %ffn.1 = bf16[256,2048]{1,0:T(8,128)(2,1)S(1)} custom-call(bf16[256,2048]{1,0:T(8,128)(2,1)S(1)} %bitcast.19, bf16[2048,128]{1,0:T(8,128)(2,1)S(1)} %copy-done.5, bf16[2048,128]{1,0:T(8,128)(2,1)S(1)} %copy-done.7, bf16[128,2048]{1,0:T(8,128)(2,1)S(1)} %copy-done.9, bf16[2048,128]{1,0:T(8,128)(2,1)S(1)} %copy-done.15, bf16[2048,128]{1,0:T(8,128)(2,1)S(1)} %copy-done.17, ...), custom_call_target="tpu_custom_call" | custom-call | flops 3200000000 | bytes 16000000 | tf_op jit(solution)/shard_map/ffn/pallas_call | solution.py:394
  182.1 4.5 %all-to-all-start.3 = ((bf16[16,16,2048]{2,1,0:T(8,128)(2,1)}), bf16[16,16,2048]{2,1,0:T(8,128)(2,1)}, u32[]{:S(2)}, u32[]{:S(2)}) async-start(bf16[16,16,2048]{2,1,0:T(8,128)(2,1)} %bitcast.20), calls=%async_computation.3 | async-start | bytes 2097152 | tf_op jit(solution)/shard_map/all_to_all | solution.py:483
  186.6 7.9 %assemble.1 = bf16[64,128,512]{2,1,0:T(8,128)(2,1)} custom-call(s32[1]{0:T(128)} %bitcast.mine_ref, bf16[64,16,512]{2,1,0:T(8,128)(2,1)S(1)} %bitcast.24, bf16[64,16,512]{2,1,0:T(8,128)(2,1)} %collective-permute-done.refs_1_.z_ref, bf16[64,32,512]{2,1,0:T(8,128)(2,1)S(1)} %bitcast.18, bf16[64,16,512]{2,1,0:T(8,128)(2,1)} %collective-permute-done.1.refs_3_, ...), custom_call_target="tpu_custom_call" | custom-call | flops 2400000000 | bytes 12000000 | tf_op jit(solution)/shard_map/assemble/pallas_call | solution.py:445
  194.5 7.6 %all-to-all-done.3.parts_ref = bf16[16,16,2048]{2,1,0:T(8,128)(2,1)} async-done(((bf16[16,16,2048]{2,1,0:T(8,128)(2,1)}), bf16[16,16,2048]{2,1,0:T(8,128)(2,1)}, u32[]{:S(2)}, u32[]{:S(2)}) %all-to-all-start.3) | async-done | bytes 1048608 | tf_op jit(solution)/shard_map/all_to_all | solution.py:483
  203.4 8.6 %all_gather.3 = bf16[64,2048]{1,0:T(8,128)(2,1)S(1)} all-gather(bf16[16,2048]{1,0:T(8,128)(2,1)S(1)} %finish.1), channel_id=1, replica_groups=mesh['dp'=32,'mp'=4] {'mp'}, dimensions={0}, use_global_device_ids=true | all-gather | bytes 327680 | tf_op jit(solution)/shard_map/all_gather | solution.py:540
  (145 shorter events, 46.0 us)
Async XLA Ops:
  37.2 33.1 %all-to-all-start.1 = ((bf16[32,2,32,512]{3,2,1,0:T(8,128)(2,1)}), bf16[32,2,32,512]{3,2,1,0:T(8,128)(2,1)S(1)}, u32[]{:S(2)}, u32[]{:S(2)}) async-start(bf16[32,2,32,512]{3,2,1,0:T(8,128)(2,1)} %bitcast.28), calls=%async_computation.1 | async-start | bytes 4194304 | tf_op jit(solution)/shard_map/all_to_all | solution.py:483
  41.3 28.9 %collective-permute-start = (bf16[64,16,512]{2,1,0:T(8,128)(2,1)S(1)}, bf16[64,16,512]{2,1,0:T(8,128)(2,1)}, u32[]{:S(2)}, u32[]{:S(2)}) collective-permute-start(bf16[64,16,512]{2,1,0:T(8,128)(2,1)S(1)} %bitcast.21), channel_id=1, source_target_pairs={{0,2},{1,3},{2,0},{3,1},{4,6},{5,7},{6,4},{7,5},{8,10},{9,11},{10,... | collective-permute-start | bytes 3145736 | tf_op jit(solution)/shard_map/ppermute | solution.py:473
  43.5 43.5 %collective-permute-start.18 = (bf16[2048,128]{1,0:T(8,128)(2,1)}, bf16[2048,128]{1,0:T(8,128)(2,1)}, u32[]{:S(2)}, u32[]{:S(2)}) collective-permute-start(bf16[2048,128]{1,0:T(8,128)(2,1)} %refs_2_.1), channel_id=1, source_target_pairs={{0,6},{1,7},{2,4},{3,5},{4,2},{5,3},{6,0},{7,1},{8,14},{9,15},{10,... | collective-permute-start | bytes 1572872 | tf_op jit(solution)/shard_map/ppermute | solution.py:473
  46.2 47.0 %collective-permute-start.12 = (bf16[2048,128]{1,0:T(8,128)(2,1)}, bf16[2048,128]{1,0:T(8,128)(2,1)}, u32[]{:S(2)}, u32[]{:S(2)}) collective-permute-start(bf16[2048,128]{1,0:T(8,128)(2,1)} %refs_2_.1), channel_id=1, source_target_pairs={{0,2},{1,3},{2,0},{3,1},{4,6},{5,7},{6,4},{7,5},{8,10},{9,11},{10,... | collective-permute-start | bytes 1572872 | tf_op jit(solution)/shard_map/ppermute | solution.py:473
  47.3 39.5 %collective-permute-start.11 = (bf16[2048,128]{1,0:T(8,128)(2,1)}, bf16[2048,128]{1,0:T(8,128)(2,1)}, u32[]{:S(2)}, u32[]{:S(2)}) collective-permute-start(bf16[2048,128]{1,0:T(8,128)(2,1)} %refs_1_.1), channel_id=1, source_target_pairs={{0,2},{1,3},{2,0},{3,1},{4,6},{5,7},{6,4},{7,5},{8,10},{9,11},{10,... | collective-permute-start | bytes 1572872 | tf_op jit(solution)/shard_map/ppermute | solution.py:473
  47.8 42.4 %collective-permute-start.19 = (bf16[128,2048]{1,0:T(8,128)(2,1)}, bf16[128,2048]{1,0:T(8,128)(2,1)}, u32[]{:S(2)}, u32[]{:S(2)}) collective-permute-start(bf16[128,2048]{1,0:T(8,128)(2,1)} %refs_3_.1), channel_id=1, source_target_pairs={{0,6},{1,7},{2,4},{3,5},{4,2},{5,3},{6,0},{7,1},{8,14},{9,15},{10,... | collective-permute-start | bytes 1572872 | tf_op jit(solution)/shard_map/ppermute | solution.py:473
  77.4 15.1 %collective-permute-start.5 = (f32[264,128]{1,0:T(8,128)S(1)}, f32[264,128]{1,0:T(8,128)S(1)}, u32[]{:S(2)}, u32[]{:S(2)}) collective-permute-start(f32[264,128]{1,0:T(8,128)S(1)} %get-tuple-element.19), channel_id=1, source_target_pairs={{0,1},{1,0},{2,3},{3,2},{4,5},{5,4},{6,7},{7,6},{8,9},{9,8},{10,11... | collective-permute-start | bytes 405512 | tf_op jit(solution)/shard_map/ppermute | solution.py:473
  87.1 14.2 %collective-permute-start.17 = (bf16[2048,128]{1,0:T(8,128)(2,1)S(1)}, bf16[2048,128]{1,0:T(8,128)(2,1)S(1)}, u32[]{:S(2)}, u32[]{:S(2)}) collective-permute-start(bf16[2048,128]{1,0:T(8,128)(2,1)S(1)} %copy-done.4), channel_id=1, source_target_pairs={{0,6},{1,7},{2,4},{3,5},{4,2},{5,3},{6,0},{7,1},{8,14},{9,15},{10,... | collective-permute-start | bytes 1572872 | tf_op jit(solution)/shard_map/ppermute | solution.py:473
  90.2 13.0 %collective-permute-start.10 = (bf16[128,2048]{1,0:T(8,128)(2,1)S(1)}, bf16[128,2048]{1,0:T(8,128)(2,1)S(1)}, u32[]{:S(2)}, u32[]{:S(2)}) collective-permute-start(bf16[128,2048]{1,0:T(8,128)(2,1)S(1)} %copy-done.8), channel_id=1, source_target_pairs={{0,1},{1,0},{2,3},{3,2},{4,5},{5,4},{6,7},{7,6},{8,9},{9,8},{10,11... | collective-permute-start | bytes 1572872 | tf_op jit(solution)/shard_map/ppermute | solution.py:473
  92.5 12.5 %collective-permute-start.8 = (bf16[2048,128]{1,0:T(8,128)(2,1)S(1)}, bf16[2048,128]{1,0:T(8,128)(2,1)S(1)}, u32[]{:S(2)}, u32[]{:S(2)}) collective-permute-start(bf16[2048,128]{1,0:T(8,128)(2,1)S(1)} %copy-done.4), channel_id=1, source_target_pairs={{0,1},{1,0},{2,3},{3,2},{4,5},{5,4},{6,7},{7,6},{8,9},{9,8},{10,11... | collective-permute-start | bytes 1572872 | tf_op jit(solution)/shard_map/ppermute | solution.py:473
  93.2 11.8 %collective-permute-start.6 = (f32[2,16,2048]{2,1,0:T(8,128)S(1)}, f32[2,16,2048]{2,1,0:T(8,128)S(1)}, u32[]{:S(2)}, u32[]{:S(2)}) collective-permute-start(f32[2,16,2048]{2,1,0:T(8,128)S(1)} %get-tuple-element.21), channel_id=1, source_target_pairs={{0,1},{1,0},{2,3},{3,2},{4,5},{5,4},{6,7},{7,6},{8,9},{9,8},{10,11... | collective-permute-start | bytes 786440 | tf_op jit(solution)/shard_map/ppermute | solution.py:473
  101.2 13.5 %collective-permute-start.23 = (bf16[2048,128]{1,0:T(8,128)(2,1)}, bf16[2048,128]{1,0:T(8,128)(2,1)S(1)}, u32[]{:S(2)}, u32[]{:S(2)}) collective-permute-start(bf16[2048,128]{1,0:T(8,128)(2,1)} %collective-permute-done.11.refs_7_), channel_id=1, source_target_pairs={{0,6},{1,7},{2,4},{3,5},{4,2},{5,3},{6,0},{7,1},{8,14},{9,15},{10,... | collective-permute-start | bytes 1572872 | tf_op jit(solution)/shard_map/ppermute | solution.py:473
  103.3 28.0 %collective-permute-start.14 = (bf16[2048,128]{1,0:T(8,128)(2,1)}, bf16[2048,128]{1,0:T(8,128)(2,1)S(1)}, u32[]{:S(2)}, u32[]{:S(2)}) collective-permute-start(bf16[2048,128]{1,0:T(8,128)(2,1)} %collective-permute-done.11.refs_7_), channel_id=1, source_target_pairs={{0,1},{1,0},{2,3},{3,2},{4,5},{5,4},{6,7},{7,6},{8,9},{9,8},{10,11... | collective-permute-start | bytes 1572872 | tf_op jit(solution)/shard_map/ppermute | solution.py:473
  105.0 13.6 %collective-permute-start.24 = (bf16[2048,128]{1,0:T(8,128)(2,1)}, bf16[2048,128]{1,0:T(8,128)(2,1)S(1)}, u32[]{:S(2)}, u32[]{:S(2)}) collective-permute-start(bf16[2048,128]{1,0:T(8,128)(2,1)} %collective-permute-done.18.refs_14_), channel_id=1, source_target_pairs={{0,2},{1,3},{2,0},{3,1},{4,6},{5,7},{6,4},{7,5},{8,10},{9,11},{10,... | collective-permute-start | bytes 1572872 | tf_op jit(solution)/shard_map/ppermute | solution.py:473
  105.0 24.8 %collective-permute-start.25 = (bf16[128,2048]{1,0:T(8,128)(2,1)}, bf16[128,2048]{1,0:T(8,128)(2,1)S(1)}, u32[]{:S(2)}, u32[]{:S(2)}) collective-permute-start(bf16[128,2048]{1,0:T(8,128)(2,1)} %collective-permute-done.19.refs_15_), channel_id=1, source_target_pairs={{0,2},{1,3},{2,0},{3,1},{4,6},{5,7},{6,4},{7,5},{8,10},{9,11},{10,... | collective-permute-start | bytes 1572872 | tf_op jit(solution)/shard_map/ppermute | solution.py:473
  106.5 26.1 %collective-permute-start.7 = (f32[16,2048]{1,0:T(8,128)S(1)}, f32[16,2048]{1,0:T(8,128)S(1)}, u32[]{:S(2)}, u32[]{:S(2)}) collective-permute-start(f32[16,2048]{1,0:T(8,128)S(1)} %fusion), channel_id=1, source_target_pairs={{0,2},{1,3},{2,0},{3,1},{4,6},{5,7},{6,4},{7,5},{8,10},{9,11},{10,... | collective-permute-start | bytes 393224 | tf_op jit(solution)/shard_map/ppermute | solution.py:473
  114.7 26.7 %collective-permute-start.21 = (bf16[2048,128]{1,0:T(8,128)(2,1)}, bf16[2048,128]{1,0:T(8,128)(2,1)}, u32[]{:S(2)}, u32[]{:S(2)}) collective-permute-start(bf16[2048,128]{1,0:T(8,128)(2,1)} %collective-permute-done.18.refs_14_), channel_id=1, source_target_pairs={{0,1},{1,0},{2,3},{3,2},{4,5},{5,4},{6,7},{7,6},{8,9},{9,8},{10,11... | collective-permute-start | bytes 1572872 | tf_op jit(solution)/shard_map/ppermute | solution.py:473
  118.6 23.3 %collective-permute-start.22 = (bf16[128,2048]{1,0:T(8,128)(2,1)}, bf16[128,2048]{1,0:T(8,128)(2,1)}, u32[]{:S(2)}, u32[]{:S(2)}) collective-permute-start(bf16[128,2048]{1,0:T(8,128)(2,1)} %collective-permute-done.19.refs_15_), channel_id=1, source_target_pairs={{0,1},{1,0},{2,3},{3,2},{4,5},{5,4},{6,7},{7,6},{8,9},{9,8},{10,11... | collective-permute-start | bytes 1572872 | tf_op jit(solution)/shard_map/ppermute | solution.py:473
  129.8 12.2 %collective-permute-start.15 = (bf16[2048,128]{1,0:T(8,128)(2,1)}, bf16[2048,128]{1,0:T(8,128)(2,1)}, u32[]{:S(2)}, u32[]{:S(2)}) collective-permute-start(bf16[2048,128]{1,0:T(8,128)(2,1)} %collective-permute-done.12.refs_8_), channel_id=1, source_target_pairs={{0,1},{1,0},{2,3},{3,2},{4,5},{5,4},{6,7},{7,6},{8,9},{9,8},{10,11... | collective-permute-start | bytes 1572872 | tf_op jit(solution)/shard_map/ppermute | solution.py:473
  132.6 54.0 %collective-permute-start.3 = (bf16[64,32,512]{2,1,0:T(8,128)(2,1)S(1)}, bf16[64,32,512]{2,1,0:T(8,128)(2,1)}, u32[]{:S(2)}, u32[]{:S(2)}) collective-permute-start(bf16[64,32,512]{2,1,0:T(8,128)(2,1)S(1)} %bitcast.17), channel_id=1, source_target_pairs={{0,1},{1,0},{2,3},{3,2},{4,5},{5,4},{6,7},{7,6},{8,9},{9,8},{10,11... | collective-permute-start | bytes 6291464 | tf_op jit(solution)/shard_map/ppermute | solution.py:473
  134.8 24.0 %all-to-all-start.2 = ((bf16[16,16,2048]{2,1,0:T(8,128)(2,1)}), bf16[16,16,2048]{2,1,0:T(8,128)(2,1)S(1)}, u32[]{:S(2)}, u32[]{:S(2)}) async-start(bf16[16,16,2048]{2,1,0:T(8,128)(2,1)} %copy-done.3), calls=%async_computation.2 | async-start | bytes 2097152 | tf_op jit(solution)/shard_map/all_to_all | solution.py:483
  144.4 42.1 %collective-permute-start.1 = (bf16[64,16,512]{2,1,0:T(8,128)(2,1)}, bf16[64,16,512]{2,1,0:T(8,128)(2,1)}, u32[]{:S(2)}, u32[]{:S(2)}) collective-permute-start(bf16[64,16,512]{2,1,0:T(8,128)(2,1)} %bitcast.23), channel_id=1, source_target_pairs={{0,1},{1,0},{2,3},{3,2},{4,5},{5,4},{6,7},{7,6},{8,9},{9,8},{10,11... | collective-permute-start | bytes 3145736 | tf_op jit(solution)/shard_map/ppermute | solution.py:473
  145.6 41.0 %collective-permute-start.2 = (bf16[64,16,512]{2,1,0:T(8,128)(2,1)}, bf16[64,16,512]{2,1,0:T(8,128)(2,1)}, u32[]{:S(2)}, u32[]{:S(2)}) collective-permute-start(bf16[64,16,512]{2,1,0:T(8,128)(2,1)} %collective-permute-done.refs_1_.z_ref), channel_id=1, source_target_pairs={{0,1},{1,0},{2,3},{3,2},{4,5},{5,4},{6,7},{7,6},{8,9},{9,8},{10,11... | collective-permute-start | bytes 3145736 | tf_op jit(solution)/shard_map/ppermute | solution.py:473
  182.1 20.0 %all-to-all-start.3 = ((bf16[16,16,2048]{2,1,0:T(8,128)(2,1)}), bf16[16,16,2048]{2,1,0:T(8,128)(2,1)}, u32[]{:S(2)}, u32[]{:S(2)}) async-start(bf16[16,16,2048]{2,1,0:T(8,128)(2,1)} %bitcast.20), calls=%async_computation.3 | async-start | bytes 2097152 | tf_op jit(solution)/shard_map/all_to_all | solution.py:483
  (51 other events, 446.4 us)

commit v8 on v7

--- a/solution.py
+++ b/solution.py
@@ -423,6 +423,36 @@
     )(parts, stream)
 
 
+def join_kernel(mine_ref, *refs):
+    out_ref = refs[4]
+    rows = refs[0].shape[0]
+    m = mine_ref[0]
+    core, side = lax.rem(m, 2), m // 2
+    for k, ref in enumerate(refs[:4]):
+        c = 1 - core if k % 2 else core
+        z = 1 - side if k >= 2 else side
+        first = pl.multiple_of((2 * z + c) * rows, rows)
+        out_ref[pl.ds(first, rows), :] = ref[...]
+
+
+def join(mine, parts):
+    rows, d = parts[0].shape
+    spec = pl.BlockSpec((rows, d), lambda i, *_: (0, 0))
+    return pl.pallas_call(
+        join_kernel,
+        grid_spec=pltpu.PrefetchScalarGridSpec(
+            num_scalar_prefetch=1,
+            grid=(1,),
+            in_specs=[spec] * 4,
+            out_specs=pl.BlockSpec((4 * rows, d), lambda i, *_: (0, 0)),
+        ),
+        out_shape=jax.ShapeDtypeStruct((4 * rows, d), parts[0].dtype),
+        compiler_params=params(4),
+        cost_estimate=cost(1),
+        name="join",
+    )(mine, *parts)
+
+
 def assemble_kernel(mine_ref, *refs):
     out_ref = refs[6]
     m = mine_ref[0]
@@ -515,7 +545,9 @@
     diag_down = send(far_down, side)
     w_diag = (diag_gate, diag_up, diag_down)
     w_far_core = each(w_far, core)
-    w_diag_core = each(w_diag, core)
+    diag_core_up, diag_core_down = send(diag_up, core), send(diag_down, core)
+    diag_core_gate = send(diag_gate, core)
+    w_diag_core = (diag_core_gate, diag_core_up, diag_core_down)
     blocks = [
         weights, w_core, w_side, w_side_core, w_far, w_far_core, w_diag, w_diag_core
     ]
@@ -537,7 +569,10 @@
     parts = ffn(x.reshape(peers * rows, d), blocks)
     back = exchange(parts.reshape(peers, rows, d), planes)
     quarter = finish(back, stream)
-    layer_out = lax.all_gather(quarter, "mp", axis=0, tiled=True)
+    other_side = send(quarter, side)
+    other_core = send(quarter, core)
+    other_both = send(other_side, core)
+    layer_out = join(mine, (quarter, other_core, other_side, other_both))
     return arrived, layer_out
 
 

time: 214 us -> 220 us (1.028)
  starting transfers between devices: 46.6 us -> 55.4 us
  blocking collectives: 38 us -> 29.4 us
  waiting for transfers between devices: 67.8 us -> 74.3 us
    ppermute x29 -> x32, starting transfers between devices: 31.4 us -> 40.1 us  [step(): send = lambda a, pairs: lax.ppermute(a, axes, pairs)]
    all_gather x1 -> x0, blocking collectives: 8.63 us -> none  [step(): layer_out = lax.all_gather(quarter, 'mp', axis=0, tiled=True)]
    all_to_all x3, waiting for transfers between devices: 34.5 us -> 38.4 us  [step(): lax.all_to_all(a, axes, 0, 0, tiled=True, axis_index_groups=who)]
    ppermute x29 -> x32, waiting for transfers between devices: 33.3 us -> 35.9 us  [step(): send = lambda a, pairs: lax.ppermute(a, axes, pairs)]
    unnamed x88 -> x83, local copies, waits for them, and re-layouts: 24.7 us -> 22.8 us
  transfers between devices with their start and end apart: 32 -> 35, of which waited for: 11 -> 11; matrix products, arithmetic and copies ran while one was open for 0% -> 0% of each run, Pallas kernels for 13% -> 13%
where the time goes in v8:
time: 220 us; the launch traced here: 218 us
  waiting for transfers between devices  74.3 us (34%)
  starting transfers between devices  55.4 us (25%)
  Pallas kernels  35.3 us (16%)
  blocking collectives  29.4 us (13%)
  local copies, waits for them, and re-layouts  23 us (10%)
    ppermute x32, starting transfers between devices, step(): send = lambda a, pairs: lax.ppermute(a, axes, pairs)  40.1 us
    all_to_all x3, waiting for transfers between devices, step(): lax.all_to_all(a, axes, 0, 0, tiled=True, axis_index_groups=who)  38.4 us
    ppermute x32, waiting for transfers between devices, step(): send = lambda a, pairs: lax.ppermute(a, axes, pairs)  35.9 us
    all_to_all x1, blocking collectives, step(): lax.all_to_all(a, axes, 0, 0, tiled=True, axis_index_groups=who)  29.4 us
    unnamed x83, local copies, waits for them, and re-layouts  22.8 us
    all_to_all x3, starting transfers between devices, step(): lax.all_to_all(a, axes, 0, 0, tiled=True, axis_index_groups=who)  15.2 us
    pallas_call x1, Pallas kernels, assemble(): pl.pallas_call(assemble_kernel, grid_spec=pltpu.PrefetchScalarGridSpec(nu...  7.87 us
    pallas_call x1, Pallas kernels, ffn(): pl.pallas_call(ffn_kernel, in_specs=[vmem] * (1 + 3 * n), out_specs=vmem,...  6.77 us
  transfers between devices with their start and end apart: 35, of which 11 were waited for; matrix products, arithmetic and copies ran while one was open for 0% of the time, Pallas kernels for 13%

profile of v8, /device:TPU:1, one launch (start us, length us, event | category | flops | bytes accessed | tf_op | source)
XLA Modules:
  0.0 218.4 jit_solution(12331214110057532515)
XLA Ops:
  2.0 5.7 %outgoing.1 = (bf16[64,16,512]{2,1,0:T(8,128)(2,1)}, bf16[64,32,512]{2,1,0:T(8,128)(2,1)}) custom-call(s32[1]{0:T(128)} %bitcast.mine_ref, s32[1]{0:T(128)S(6)} %select_n.17.twist_ref, s32[32,2]{1,0:T(8,128)} %copy.15.slot_ref, s32[32]{0:T(128)} %bitcast.31, bf16[64,128,512]{2,1,0:T(8,128)(2,1)} %pool_ref.3), custom_call_target="tpu_custom_call" | custom-call | flops 1200000000 | bytes 6000000 | tf_op jit(solution)/shard_map/outgoing/pallas_call | solution.py:62
  7.8 29.4 %all_to_all.20 = bf16[32,2,16,512]{3,2,1,0:T(8,128)(2,1)S(1)} all-to-all(bf16[32,2,16,512]{3,2,1,0:T(8,128)(2,1)} %bitcast.29), channel_id=1, replica_groups={{0,6,8,14,16,22,24,30,32,38,40,46,48,54,56,62,64,70,72,78,80,86,88,94,9..., dimensions={0} | all-to-all | bytes 2097152 | tf_op jit(solution)/shard_map/all_to_all | solution.py:513
  37.2 4.2 %all-to-all-start.1 = ((bf16[32,2,32,512]{3,2,1,0:T(8,128)(2,1)}), bf16[32,2,32,512]{3,2,1,0:T(8,128)(2,1)S(1)}, u32[]{:S(2)}, u32[]{:S(2)}) async-start(bf16[32,2,32,512]{3,2,1,0:T(8,128)(2,1)} %bitcast.28), calls=%async_computation.1 | async-start | bytes 4194304 | tf_op jit(solution)/shard_map/all_to_all | solution.py:513
  43.5 2.6 %collective-permute-start.18 = (bf16[2048,128]{1,0:T(8,128)(2,1)}, bf16[2048,128]{1,0:T(8,128)(2,1)}, u32[]{:S(2)}, u32[]{:S(2)}) collective-permute-start(bf16[2048,128]{1,0:T(8,128)(2,1)} %refs_2_.1), channel_id=1, source_target_pairs={{0,6},{1,7},{2,4},{3,5},{4,2},{5,3},{6,0},{7,1},{8,14},{9,15},{10,... | collective-permute-start | bytes 1572872 | tf_op jit(solution)/shard_map/ppermute | solution.py:503
  48.1 5.8 %resident.1 = (f32[256,256]{1,0:T(8,128)S(1)}, f32[8,256]{1,0:T(8,128)S(1)}, bf16[256,256]{1,0:T(8,128)(2,1)S(1)}) custom-call(s32[1]{0:T(128)S(6)} %select_n.18.half_ref, bf16[128,256]{1,0:T(8,128)(2,1)S(1)} %bitcast.26, bf16[128,256]{1,0:T(8,128)(2,1)S(1)} %collective-permute-done.4.qb_ref, bf16[64,512]{1,0:T(8,128)(2,1)S(1)} %copy-done.34, ...), custom_call_target="tpu_custom_call" | custom-call | flops 3200000000 | bytes 16000000 | tf_op jit(solution)/shard_map/resident/pallas_call | solution.py:184
  54.6 15.6 %all-to-all-done.1 = bf16[32,2,32,512]{3,2,1,0:T(8,128)(2,1)S(1)} async-done(((bf16[32,2,32,512]{3,2,1,0:T(8,128)(2,1)}), bf16[32,2,32,512]{3,2,1,0:T(8,128)(2,1)S(1)}, u32[]{:S(2)}, u32[]{:S(2)}) %all-to-all-start.1) | async-done | bytes 2097184 | tf_op jit(solution)/shard_map/all_to_all | solution.py:513
  71.2 6.2 %moved.1 = (f32[264,128]{1,0:T(8,128)S(1)}, f32[264,128]{1,0:T(8,128)S(1)}) custom-call(s32[1]{0:T(128)} %bitcast.mine_ref, bf16[256,256]{1,0:T(8,128)(2,1)S(1)} %get-tuple-element.15.qt_ref, s32[16,256]{1,0:T(8,128)S(1)} %tile.18.tab_ref, s32[1,256]{1,0:T(1,128)S(1)} %tile.20.len_ref, f32[256,256]{1,0:T(8,128)S(1)} %copy-done.37, ...), custom_call_target="tpu_custom_call" | custom-call | flops 3200000000 | bytes 16000000 | tf_op jit(solution)/shard_map/moved/pallas_call | solution.py:253
  77.4 2.6 %collective-permute-start.5 = (f32[264,128]{1,0:T(8,128)S(1)}, f32[264,128]{1,0:T(8,128)S(1)}, u32[]{:S(2)}, u32[]{:S(2)}) collective-permute-start(f32[264,128]{1,0:T(8,128)S(1)} %get-tuple-element.19), channel_id=1, source_target_pairs={{0,1},{1,0},{2,3},{3,2},{4,5},{5,4},{6,7},{7,6},{8,9},{9,8},{10,11... | collective-permute-start | bytes 405512 | tf_op jit(solution)/shard_map/ppermute | solution.py:503
  80.0 6.8 %collective-permute-done.11.refs_7_ = bf16[2048,128]{1,0:T(8,128)(2,1)} collective-permute-done((bf16[2048,128]{1,0:T(8,128)(2,1)}, bf16[2048,128]{1,0:T(8,128)(2,1)}, u32[]{:S(2)}, u32[]{:S(2)}) %collective-permute-start.11) | collective-permute-done | bytes 524320 | tf_op jit(solution)/shard_map/ppermute | solution.py:503
  90.2 2.2 %collective-permute-start.10 = (bf16[128,2048]{1,0:T(8,128)(2,1)S(1)}, bf16[128,2048]{1,0:T(8,128)(2,1)S(1)}, u32[]{:S(2)}, u32[]{:S(2)}) collective-permute-start(bf16[128,2048]{1,0:T(8,128)(2,1)S(1)} %copy-done.8), channel_id=1, source_target_pairs={{0,1},{1,0},{2,3},{3,2},{4,5},{5,4},{6,7},{7,6},{8,9},{9,8},{10,11... | collective-permute-start | bytes 1572872 | tf_op jit(solution)/shard_map/ppermute | solution.py:503
  93.7 3.9 %collective-permute-done.13.refs_9_ = bf16[128,2048]{1,0:T(8,128)(2,1)} collective-permute-done((bf16[128,2048]{1,0:T(8,128)(2,1)S(1)}, bf16[128,2048]{1,0:T(8,128)(2,1)}, u32[]{:S(2)}, u32[]{:S(2)}) %collective-permute-start.13) | collective-permute-done | bytes 524320 | tf_op jit(solution)/shard_map/ppermute | solution.py:503
  97.6 3.7 %collective-permute-start.9 = (bf16[2048,128]{1,0:T(8,128)(2,1)S(1)}, bf16[2048,128]{1,0:T(8,128)(2,1)S(1)}, u32[]{:S(2)}, u32[]{:S(2)}) collective-permute-start(bf16[2048,128]{1,0:T(8,128)(2,1)S(1)} %copy-done.6), channel_id=1, source_target_pairs={{0,1},{1,0},{2,3},{3,2},{4,5},{5,4},{6,7},{7,6},{8,9},{9,8},{10,11... | collective-permute-start | bytes 1572872 | tf_op jit(solution)/shard_map/ppermute | solution.py:503
  106.8 7.9 %collective-permute-done.23.refs_19_ = bf16[2048,128]{1,0:T(8,128)(2,1)S(1)} collective-permute-done((bf16[2048,128]{1,0:T(8,128)(2,1)}, bf16[2048,128]{1,0:T(8,128)(2,1)S(1)}, u32[]{:S(2)}, u32[]{:S(2)}) %collective-permute-start.23) | collective-permute-done | bytes 524320 | tf_op jit(solution)/shard_map/ppermute | solution.py:503
  114.7 2.2 %collective-permute-start.21 = (bf16[2048,128]{1,0:T(8,128)(2,1)}, bf16[2048,128]{1,0:T(8,128)(2,1)}, u32[]{:S(2)}, u32[]{:S(2)}) collective-permute-start(bf16[2048,128]{1,0:T(8,128)(2,1)} %collective-permute-done.18.refs_14_), channel_id=1, source_target_pairs={{0,1},{1,0},{2,3},{3,2},{4,5},{5,4},{6,7},{7,6},{8,9},{9,8},{10,11... | collective-permute-start | bytes 1572872 | tf_op jit(solution)/shard_map/ppermute | solution.py:503
  120.1 9.7 %collective-permute-done.25.refs_21_ = bf16[128,2048]{1,0:T(8,128)(2,1)S(1)} collective-permute-done((bf16[128,2048]{1,0:T(8,128)(2,1)}, bf16[128,2048]{1,0:T(8,128)(2,1)S(1)}, u32[]{:S(2)}, u32[]{:S(2)}) %collective-permute-start.25) | collective-permute-done | bytes 524320 | tf_op jit(solution)/shard_map/ppermute | solution.py:503
  134.8 6.6 %all-to-all-start.2 = ((bf16[16,16,2048]{2,1,0:T(8,128)(2,1)}), bf16[16,16,2048]{2,1,0:T(8,128)(2,1)S(1)}, u32[]{:S(2)}, u32[]{:S(2)}) async-start(bf16[16,16,2048]{2,1,0:T(8,128)(2,1)} %copy-done.3), calls=%async_computation.2 | async-start | bytes 2097152 | tf_op jit(solution)/shard_map/all_to_all | solution.py:513
  142.8 3.6 %collective-permute-done.20.refs_16_ = bf16[2048,128]{1,0:T(8,128)(2,1)S(1)} collective-permute-done((bf16[2048,128]{1,0:T(8,128)(2,1)}, bf16[2048,128]{1,0:T(8,128)(2,1)S(1)}, u32[]{:S(2)}, u32[]{:S(2)}) %collective-permute-start.20) | collective-permute-done | bytes 524320 | tf_op jit(solution)/shard_map/ppermute | solution.py:503
  149.6 9.1 %all-to-all-done.2 = bf16[16,16,2048]{2,1,0:T(8,128)(2,1)S(1)} async-done(((bf16[16,16,2048]{2,1,0:T(8,128)(2,1)}), bf16[16,16,2048]{2,1,0:T(8,128)(2,1)S(1)}, u32[]{:S(2)}, u32[]{:S(2)}) %all-to-all-start.2) | async-done | bytes 1048608 | tf_op jit(solution)/shard_map/all_to_all | solution.py:513
  173.3 6.8 %ffn.1 = bf16[256,2048]{1,0:T(8,128)(2,1)S(1)} custom-call(bf16[256,2048]{1,0:T(8,128)(2,1)S(1)} %bitcast.19, bf16[2048,128]{1,0:T(8,128)(2,1)S(1)} %copy-done.5, bf16[2048,128]{1,0:T(8,128)(2,1)S(1)} %copy-done.7, bf16[128,2048]{1,0:T(8,128)(2,1)S(1)} %copy-done.9, bf16[2048,128]{1,0:T(8,128)(2,1)S(1)} %copy-done.15, bf16[2048,128]{1,0:T(8,128)(2,1)S(1)} %copy-done.17, ...), custom_call_target="tpu_custom_call" | custom-call | flops 3200000000 | bytes 16000000 | tf_op jit(solution)/shard_map/ffn/pallas_call | solution.py:394
  181.1 4.5 %all-to-all-start.3 = ((bf16[16,16,2048]{2,1,0:T(8,128)(2,1)}), bf16[16,16,2048]{2,1,0:T(8,128)(2,1)}, u32[]{:S(2)}, u32[]{:S(2)}) async-start(bf16[16,16,2048]{2,1,0:T(8,128)(2,1)} %bitcast.20), calls=%async_computation.3 | async-start | bytes 2097152 | tf_op jit(solution)/shard_map/all_to_all | solution.py:513
  187.3 13.8 %all-to-all-done.3.parts_ref = bf16[16,16,2048]{2,1,0:T(8,128)(2,1)} async-done(((bf16[16,16,2048]{2,1,0:T(8,128)(2,1)}), bf16[16,16,2048]{2,1,0:T(8,128)(2,1)}, u32[]{:S(2)}, u32[]{:S(2)}) %all-to-all-start.3) | async-done | bytes 1048608 | tf_op jit(solution)/shard_map/all_to_all | solution.py:513
  202.5 3.3 %collective-permute-start.29 = (bf16[16,2048]{1,0:T(8,128)(2,1)S(1)}, bf16[16,2048]{1,0:T(8,128)(2,1)S(1)}, u32[]{:S(2)}, u32[]{:S(2)}) collective-permute-start(bf16[16,2048]{1,0:T(8,128)(2,1)S(1)} %finish.1.refs_0_), channel_id=1, source_target_pairs={{0,1},{1,0},{2,3},{3,2},{4,5},{5,4},{6,7},{7,6},{8,9},{9,8},{10,11... | collective-permute-start | bytes 196616 | tf_op jit(solution)/shard_map/ppermute | solution.py:503
  205.8 4.0 %collective-permute-start.31 = (bf16[16,2048]{1,0:T(8,128)(2,1)S(1)}, bf16[16,2048]{1,0:T(8,128)(2,1)S(1)}, u32[]{:S(2)}, u32[]{:S(2)}) collective-permute-start(bf16[16,2048]{1,0:T(8,128)(2,1)S(1)} %collective-permute-done.30.refs_2_), channel_id=1, source_target_pairs={{0,1},{1,0},{2,3},{3,2},{4,5},{5,4},{6,7},{7,6},{8,9},{9,8},{10,11... | collective-permute-start | bytes 196616 | tf_op jit(solution)/shard_map/ppermute | solution.py:503
  209.8 7.9 %assemble.1 = bf16[64,128,512]{2,1,0:T(8,128)(2,1)} custom-call(s32[1]{0:T(128)} %bitcast.mine_ref, bf16[64,16,512]{2,1,0:T(8,128)(2,1)S(1)} %bitcast.24, bf16[64,16,512]{2,1,0:T(8,128)(2,1)} %collective-permute-done.refs_1_.z_ref, bf16[64,32,512]{2,1,0:T(8,128)(2,1)S(1)} %bitcast.18, bf16[64,16,512]{2,1,0:T(8,128)(2,1)} %collective-permute-done.1.refs_3_, ...), custom_call_target="tpu_custom_call" | custom-call | flops 2400000000 | bytes 12000000 | tf_op jit(solution)/shard_map/assemble/pallas_call | solution.py:475
  (146 shorter events, 49.5 us)
Async XLA Ops:
  37.2 33.1 %all-to-all-start.1 = ((bf16[32,2,32,512]{3,2,1,0:T(8,128)(2,1)}), bf16[32,2,32,512]{3,2,1,0:T(8,128)(2,1)S(1)}, u32[]{:S(2)}, u32[]{:S(2)}) async-start(bf16[32,2,32,512]{3,2,1,0:T(8,128)(2,1)} %bitcast.28), calls=%async_computation.1 | async-start | bytes 4194304 | tf_op jit(solution)/shard_map/all_to_all | solution.py:513
  41.3 28.9 %collective-permute-start = (bf16[64,16,512]{2,1,0:T(8,128)(2,1)S(1)}, bf16[64,16,512]{2,1,0:T(8,128)(2,1)}, u32[]{:S(2)}, u32[]{:S(2)}) collective-permute-start(bf16[64,16,512]{2,1,0:T(8,128)(2,1)S(1)} %bitcast.21), channel_id=1, source_target_pairs={{0,2},{1,3},{2,0},{3,1},{4,6},{5,7},{6,4},{7,5},{8,10},{9,11},{10,... | collective-permute-start | bytes 3145736 | tf_op jit(solution)/shard_map/ppermute | solution.py:503
  43.5 43.5 %collective-permute-start.18 = (bf16[2048,128]{1,0:T(8,128)(2,1)}, bf16[2048,128]{1,0:T(8,128)(2,1)}, u32[]{:S(2)}, u32[]{:S(2)}) collective-permute-start(bf16[2048,128]{1,0:T(8,128)(2,1)} %refs_2_.1), channel_id=1, source_target_pairs={{0,6},{1,7},{2,4},{3,5},{4,2},{5,3},{6,0},{7,1},{8,14},{9,15},{10,... | collective-permute-start | bytes 1572872 | tf_op jit(solution)/shard_map/ppermute | solution.py:503
  46.2 47.0 %collective-permute-start.12 = (bf16[2048,128]{1,0:T(8,128)(2,1)}, bf16[2048,128]{1,0:T(8,128)(2,1)}, u32[]{:S(2)}, u32[]{:S(2)}) collective-permute-start(bf16[2048,128]{1,0:T(8,128)(2,1)} %refs_2_.1), channel_id=1, source_target_pairs={{0,2},{1,3},{2,0},{3,1},{4,6},{5,7},{6,4},{7,5},{8,10},{9,11},{10,... | collective-permute-start | bytes 1572872 | tf_op jit(solution)/shard_map/ppermute | solution.py:503
  47.3 39.5 %collective-permute-start.11 = (bf16[2048,128]{1,0:T(8,128)(2,1)}, bf16[2048,128]{1,0:T(8,128)(2,1)}, u32[]{:S(2)}, u32[]{:S(2)}) collective-permute-start(bf16[2048,128]{1,0:T(8,128)(2,1)} %refs_1_.1), channel_id=1, source_target_pairs={{0,2},{1,3},{2,0},{3,1},{4,6},{5,7},{6,4},{7,5},{8,10},{9,11},{10,... | collective-permute-start | bytes 1572872 | tf_op jit(solution)/shard_map/ppermute | solution.py:503
  47.8 42.4 %collective-permute-start.19 = (bf16[128,2048]{1,0:T(8,128)(2,1)}, bf16[128,2048]{1,0:T(8,128)(2,1)}, u32[]{:S(2)}, u32[]{:S(2)}) collective-permute-start(bf16[128,2048]{1,0:T(8,128)(2,1)} %refs_3_.1), channel_id=1, source_target_pairs={{0,6},{1,7},{2,4},{3,5},{4,2},{5,3},{6,0},{7,1},{8,14},{9,15},{10,... | collective-permute-start | bytes 1572872 | tf_op jit(solution)/shard_map/ppermute | solution.py:503
  77.4 15.1 %collective-permute-start.5 = (f32[264,128]{1,0:T(8,128)S(1)}, f32[264,128]{1,0:T(8,128)S(1)}, u32[]{:S(2)}, u32[]{:S(2)}) collective-permute-start(f32[264,128]{1,0:T(8,128)S(1)} %get-tuple-element.19), channel_id=1, source_target_pairs={{0,1},{1,0},{2,3},{3,2},{4,5},{5,4},{6,7},{7,6},{8,9},{9,8},{10,11... | collective-permute-start | bytes 405512 | tf_op jit(solution)/shard_map/ppermute | solution.py:503
  87.1 14.2 %collective-permute-start.17 = (bf16[2048,128]{1,0:T(8,128)(2,1)S(1)}, bf16[2048,128]{1,0:T(8,128)(2,1)S(1)}, u32[]{:S(2)}, u32[]{:S(2)}) collective-permute-start(bf16[2048,128]{1,0:T(8,128)(2,1)S(1)} %copy-done.4), channel_id=1, source_target_pairs={{0,6},{1,7},{2,4},{3,5},{4,2},{5,3},{6,0},{7,1},{8,14},{9,15},{10,... | collective-permute-start | bytes 1572872 | tf_op jit(solution)/shard_map/ppermute | solution.py:503
  90.2 13.0 %collective-permute-start.10 = (bf16[128,2048]{1,0:T(8,128)(2,1)S(1)}, bf16[128,2048]{1,0:T(8,128)(2,1)S(1)}, u32[]{:S(2)}, u32[]{:S(2)}) collective-permute-start(bf16[128,2048]{1,0:T(8,128)(2,1)S(1)} %copy-done.8), channel_id=1, source_target_pairs={{0,1},{1,0},{2,3},{3,2},{4,5},{5,4},{6,7},{7,6},{8,9},{9,8},{10,11... | collective-permute-start | bytes 1572872 | tf_op jit(solution)/shard_map/ppermute | solution.py:503
  92.5 12.5 %collective-permute-start.8 = (bf16[2048,128]{1,0:T(8,128)(2,1)S(1)}, bf16[2048,128]{1,0:T(8,128)(2,1)S(1)}, u32[]{:S(2)}, u32[]{:S(2)}) collective-permute-start(bf16[2048,128]{1,0:T(8,128)(2,1)S(1)} %copy-done.4), channel_id=1, source_target_pairs={{0,1},{1,0},{2,3},{3,2},{4,5},{5,4},{6,7},{7,6},{8,9},{9,8},{10,11... | collective-permute-start | bytes 1572872 | tf_op jit(solution)/shard_map/ppermute | solution.py:503
  101.2 13.5 %collective-permute-start.23 = (bf16[2048,128]{1,0:T(8,128)(2,1)}, bf16[2048,128]{1,0:T(8,128)(2,1)S(1)}, u32[]{:S(2)}, u32[]{:S(2)}) collective-permute-start(bf16[2048,128]{1,0:T(8,128)(2,1)} %collective-permute-done.11.refs_7_), channel_id=1, source_target_pairs={{0,6},{1,7},{2,4},{3,5},{4,2},{5,3},{6,0},{7,1},{8,14},{9,15},{10,... | collective-permute-start | bytes 1572872 | tf_op jit(solution)/shard_map/ppermute | solution.py:503
  103.3 38.1 %collective-permute-start.14 = (bf16[2048,128]{1,0:T(8,128)(2,1)}, bf16[2048,128]{1,0:T(8,128)(2,1)}, u32[]{:S(2)}, u32[]{:S(2)}) collective-permute-start(bf16[2048,128]{1,0:T(8,128)(2,1)} %collective-permute-done.11.refs_7_), channel_id=1, source_target_pairs={{0,1},{1,0},{2,3},{3,2},{4,5},{5,4},{6,7},{7,6},{8,9},{9,8},{10,11... | collective-permute-start | bytes 1572872 | tf_op jit(solution)/shard_map/ppermute | solution.py:503
  105.0 13.6 %collective-permute-start.24 = (bf16[2048,128]{1,0:T(8,128)(2,1)}, bf16[2048,128]{1,0:T(8,128)(2,1)S(1)}, u32[]{:S(2)}, u32[]{:S(2)}) collective-permute-start(bf16[2048,128]{1,0:T(8,128)(2,1)} %collective-permute-done.18.refs_14_), channel_id=1, source_target_pairs={{0,2},{1,3},{2,0},{3,1},{4,6},{5,7},{6,4},{7,5},{8,10},{9,11},{10,... | collective-permute-start | bytes 1572872 | tf_op jit(solution)/shard_map/ppermute | solution.py:503
  105.0 24.8 %collective-permute-start.25 = (bf16[128,2048]{1,0:T(8,128)(2,1)}, bf16[128,2048]{1,0:T(8,128)(2,1)S(1)}, u32[]{:S(2)}, u32[]{:S(2)}) collective-permute-start(bf16[128,2048]{1,0:T(8,128)(2,1)} %collective-permute-done.19.refs_15_), channel_id=1, source_target_pairs={{0,2},{1,3},{2,0},{3,1},{4,6},{5,7},{6,4},{7,5},{8,10},{9,11},{10,... | collective-permute-start | bytes 1572872 | tf_op jit(solution)/shard_map/ppermute | solution.py:503
  106.5 26.1 %collective-permute-start.7 = (f32[16,2048]{1,0:T(8,128)S(1)}, f32[16,2048]{1,0:T(8,128)S(1)}, u32[]{:S(2)}, u32[]{:S(2)}) collective-permute-start(f32[16,2048]{1,0:T(8,128)S(1)} %fusion), channel_id=1, source_target_pairs={{0,2},{1,3},{2,0},{3,1},{4,6},{5,7},{6,4},{7,5},{8,10},{9,11},{10,... | collective-permute-start | bytes 393224 | tf_op jit(solution)/shard_map/ppermute | solution.py:503
  114.7 27.1 %collective-permute-start.21 = (bf16[2048,128]{1,0:T(8,128)(2,1)}, bf16[2048,128]{1,0:T(8,128)(2,1)}, u32[]{:S(2)}, u32[]{:S(2)}) collective-permute-start(bf16[2048,128]{1,0:T(8,128)(2,1)} %collective-permute-done.18.refs_14_), channel_id=1, source_target_pairs={{0,1},{1,0},{2,3},{3,2},{4,5},{5,4},{6,7},{7,6},{8,9},{9,8},{10,11... | collective-permute-start | bytes 1572872 | tf_op jit(solution)/shard_map/ppermute | solution.py:503
  118.6 23.5 %collective-permute-start.22 = (bf16[128,2048]{1,0:T(8,128)(2,1)}, bf16[128,2048]{1,0:T(8,128)(2,1)}, u32[]{:S(2)}, u32[]{:S(2)}) collective-permute-start(bf16[128,2048]{1,0:T(8,128)(2,1)} %collective-permute-done.19.refs_15_), channel_id=1, source_target_pairs={{0,1},{1,0},{2,3},{3,2},{4,5},{5,4},{6,7},{7,6},{8,9},{9,8},{10,11... | collective-permute-start | bytes 1572872 | tf_op jit(solution)/shard_map/ppermute | solution.py:503
  129.8 12.5 %collective-permute-start.15 = (bf16[2048,128]{1,0:T(8,128)(2,1)}, bf16[2048,128]{1,0:T(8,128)(2,1)}, u32[]{:S(2)}, u32[]{:S(2)}) collective-permute-start(bf16[2048,128]{1,0:T(8,128)(2,1)} %collective-permute-done.12.refs_8_), channel_id=1, source_target_pairs={{0,1},{1,0},{2,3},{3,2},{4,5},{5,4},{6,7},{7,6},{8,9},{9,8},{10,11... | collective-permute-start | bytes 1572872 | tf_op jit(solution)/shard_map/ppermute | solution.py:503
  134.8 24.0 %all-to-all-start.2 = ((bf16[16,16,2048]{2,1,0:T(8,128)(2,1)}), bf16[16,16,2048]{2,1,0:T(8,128)(2,1)S(1)}, u32[]{:S(2)}, u32[]{:S(2)}) async-start(bf16[16,16,2048]{2,1,0:T(8,128)(2,1)} %copy-done.3), calls=%async_computation.2 | async-start | bytes 2097152 | tf_op jit(solution)/shard_map/all_to_all | solution.py:513
  141.4 68.4 %collective-permute-start.3 = (bf16[64,32,512]{2,1,0:T(8,128)(2,1)S(1)}, bf16[64,32,512]{2,1,0:T(8,128)(2,1)}, u32[]{:S(2)}, u32[]{:S(2)}) collective-permute-start(bf16[64,32,512]{2,1,0:T(8,128)(2,1)S(1)} %bitcast.17), channel_id=1, source_target_pairs={{0,1},{1,0},{2,3},{3,2},{4,5},{5,4},{6,7},{7,6},{8,9},{9,8},{10,11... | collective-permute-start | bytes 6291464 | tf_op jit(solution)/shard_map/ppermute | solution.py:503
  181.1 19.9 %all-to-all-start.3 = ((bf16[16,16,2048]{2,1,0:T(8,128)(2,1)}), bf16[16,16,2048]{2,1,0:T(8,128)(2,1)}, u32[]{:S(2)}, u32[]{:S(2)}) async-start(bf16[16,16,2048]{2,1,0:T(8,128)(2,1)} %bitcast.20), calls=%async_computation.3 | async-start | bytes 2097152 | tf_op jit(solution)/shard_map/all_to_all | solution.py:513
  185.6 24.2 %collective-permute-start.1 = (bf16[64,16,512]{2,1,0:T(8,128)(2,1)S(1)}, bf16[64,16,512]{2,1,0:T(8,128)(2,1)}, u32[]{:S(2)}, u32[]{:S(2)}) collective-permute-start(bf16[64,16,512]{2,1,0:T(8,128)(2,1)S(1)} %bitcast.23), channel_id=1, source_target_pairs={{0,1},{1,0},{2,3},{3,2},{4,5},{5,4},{6,7},{7,6},{8,9},{9,8},{10,11... | collective-permute-start | bytes 3145736 | tf_op jit(solution)/shard_map/ppermute | solution.py:503
  187.2 22.6 %collective-permute-start.2 = (bf16[64,16,512]{2,1,0:T(8,128)(2,1)}, bf16[64,16,512]{2,1,0:T(8,128)(2,1)}, u32[]{:S(2)}, u32[]{:S(2)}) collective-permute-start(bf16[64,16,512]{2,1,0:T(8,128)(2,1)} %collective-permute-done.refs_1_.z_ref), channel_id=1, source_target_pairs={{0,1},{1,0},{2,3},{3,2},{4,5},{5,4},{6,7},{7,6},{8,9},{9,8},{10,11... | collective-permute-start | bytes 3145736 | tf_op jit(solution)/shard_map/ppermute | solution.py:503
  202.5 15.1 %collective-permute-start.29 = (bf16[16,2048]{1,0:T(8,128)(2,1)S(1)}, bf16[16,2048]{1,0:T(8,128)(2,1)S(1)}, u32[]{:S(2)}, u32[]{:S(2)}) collective-permute-start(bf16[16,2048]{1,0:T(8,128)(2,1)S(1)} %finish.1.refs_0_), channel_id=1, source_target_pairs={{0,1},{1,0},{2,3},{3,2},{4,5},{5,4},{6,7},{7,6},{8,9},{9,8},{10,11... | collective-permute-start | bytes 196616 | tf_op jit(solution)/shard_map/ppermute | solution.py:503
  (52 other events, 477.3 us)

commit v9 on v8

--- a/solution.py
+++ b/solution.py
@@ -1,3 +1,5 @@
+import functools
+
 import jax
 import jax.numpy as jnp
 from jax import lax
@@ -19,56 +21,46 @@
     return pl.CostEstimate(flops=int(us * 4e8), bytes_accessed=int(us * 2e6), transcendentals=0)
 
 
-def outgoing_kernel(
-    mine_ref, twist_ref, slot_ref, count_ref, pool_ref, a_ref, b_ref, sems
-):
-    pages, quarter, _ = a_ref.shape
-    rest = b_ref.shape[1]
+def outgoing_kernel(by_quarter, mine_ref, twist_ref, slot_ref, count_ref, pool_ref, out_ref, sems):
+    pages, rows, _ = out_ref.shape
     caps = pages // count_ref.shape[0]
     core = lax.rem(mine_ref[0], 2)
-    low = pl.multiple_of(4 * quarter + core * rest, rest)
-
-    def copies(i):
+
+    def copy(i):
         page = slot_ref[i // caps, i % caps]
-        side = lax.rem(twist_ref[0] + (i // caps) % 2, 2)
-        first = pl.multiple_of((2 * side + core) * quarter, quarter)
-        return (
-            pltpu.make_async_copy(
-                pool_ref.at[page, pl.ds(first, quarter), :], a_ref.at[i], sems.at[2 * i]
-            ),
-            pltpu.make_async_copy(
-                pool_ref.at[page, pl.ds(low, rest), :], b_ref.at[i], sems.at[2 * i + 1]
-            ),
-        )
-
-    pending = [copies(i) for i in range(pages)]
-    for pair in pending:
-        for c in pair:
-            c.start()
-    for i, pair in enumerate(pending):
-        for c in pair:
-            c.wait()
+        if by_quarter:
+            side = lax.rem(twist_ref[0] + (i // caps) % 2, 2)
+            first = (2 * side + core) * rows
+        else:
+            first = (2 + core) * rows
+        src = pool_ref.at[page, pl.ds(pl.multiple_of(first, rows), rows), :]
+        return pltpu.make_async_copy(src, out_ref.at[i], sems.at[i])
+
+    pending = [copy(i) for i in range(pages)]
+    for c in pending:
+        c.start()
+    for i, c in enumerate(pending):
+        c.wait()
 
         @pl.when(i % caps >= count_ref[i // caps])
         def _():
-            a_ref[i] = jnp.zeros(a_ref.shape[1:], a_ref.dtype)
-            b_ref[i] = jnp.zeros(b_ref.shape[1:], b_ref.dtype)
-
-
-def outgoing_pages(mine, twist, slots, counts, pool):
+            out_ref[i] = jnp.zeros(out_ref.shape[1:], out_ref.dtype)
+
+
+def outgoing_pages(by_quarter, mine, twist, slots, counts, pool):
     pages = slots.size
     page_len, width = pool.shape[1:]
-    shapes = [(pages, page_len // 8, width), (pages, page_len // 4, width)]
-    return pl.pallas_call(
-        outgoing_kernel,
+    shape = (pages, page_len // (8 if by_quarter else 4), width)
+    return pl.pallas_call(
+        functools.partial(outgoing_kernel, by_quarter),
         grid_spec=pltpu.PrefetchScalarGridSpec(
             num_scalar_prefetch=4,
             grid=(1,),
             in_specs=[pl.BlockSpec(memory_space=pltpu.HBM)],
-            out_specs=[pl.BlockSpec(x, lambda i, *_: (0, 0, 0)) for x in shapes],
-            scratch_shapes=[pltpu.SemaphoreType.DMA((2 * pages,))],
-        ),
-        out_shape=[jax.ShapeDtypeStruct(x, pool.dtype) for x in shapes],
+            out_specs=pl.BlockSpec(shape, lambda i, *_: (0, 0, 0)),
+            scratch_shapes=[pltpu.SemaphoreType.DMA((pages,))],
+        ),
+        out_shape=jax.ShapeDtypeStruct(shape, pool.dtype),
         compiler_params=params(60),
         cost_estimate=cost(3),
         name="outgoing",
@@ -515,7 +507,9 @@
     )
 
     twist = (mine // 2 + lax.axis_index("dp")) % 2
-    out_a, out_b = outgoing_pages(mine, twist, send_slots, move_count.reshape(-1), page_pool)
+    plan = (mine, twist, send_slots, move_count.reshape(-1), page_pool)
+    out_a = outgoing_pages(True, *plan)
+    out_b = outgoing_pages(False, *plan)
     spread_out = lambda a: exchange(a.reshape(n_dp, -1, *a.shape[1:]), groups).reshape(a.shape)
     got_a = spread_out(out_a)
     got_b = spread_out(out_b)
@@ -538,7 +532,8 @@
     side_core_gate, side_core_up = send(side_gate, core), send(side_up, core)
     side_core_down = send(side_down, core)
     w_side_core = (side_core_gate, side_core_up, side_core_down)
-    far_up, far_down, far_gate = (send(weights[k], far) for k in (1, 2, 0))
+    far_up = send(weights[1], far)
+    far_down, far_gate = send(weights[2], far), send(weights[0], far)
     w_far = (far_gate, far_up, far_down)
     diag_gate = send(w_side[0], far)
     diag_up = send(far_up, side)

time: 220 us -> 218 us (level)
  blocking collectives: 29.4 us -> 0 us
  waiting for transfers between devices: 74.3 us -> 87.9 us
  starting transfers between devices: 55.4 us -> 66.7 us
  Pallas kernels: 35.3 us -> 37.8 us
    all_to_all x1 -> x0, blocking collectives: 29.4 us -> none  [step(): lax.all_to_all(a, axes, 0, 0, tiled=True, axis_index_groups=who)]
    all_to_all x3 -> x4, waiting for transfers between devices: 38.4 us -> 52 us  [step(): lax.all_to_all(a, axes, 0, 0, tiled=True, axis_index_groups=who)]
    all_to_all x3 -> x4, starting transfers between devices: 15.2 us -> 26.5 us  [step(): lax.all_to_all(a, axes, 0, 0, tiled=True, axis_index_groups=who)]
    pallas_call x1 -> x2, Pallas kernels: 5.75 us -> 8.25 us  [outgoing_pages(): pl.pallas_call(functools.partial(outgoing_kernel, by_quarter), grid_spec=...]
  transfers between devices with their start and end apart: 35 -> 36, of which waited for: 11 -> 12; matrix products, arithmetic and copies ran while one was open for 0% -> 0% of each run, Pallas kernels for 13% -> 15%
where the time goes in v9:
time: 218 us; the launch traced here: 216 us
  waiting for transfers between devices  87.9 us (40%)
  starting transfers between devices  66.7 us (31%)
  Pallas kernels  37.8 us (17%)
  local copies, waits for them, and re-layouts  23 us (11%)
    all_to_all x4, waiting for transfers between devices, step(): lax.all_to_all(a, axes, 0, 0, tiled=True, axis_index_groups=who)  52 us
    ppermute x32, starting transfers between devices, step(): send = lambda a, pairs: lax.ppermute(a, axes, pairs)  40.2 us
    ppermute x32, waiting for transfers between devices, step(): send = lambda a, pairs: lax.ppermute(a, axes, pairs)  35.9 us
    all_to_all x4, starting transfers between devices, step(): lax.all_to_all(a, axes, 0, 0, tiled=True, axis_index_groups=who)  26.5 us
    unnamed x83, local copies, waits for them, and re-layouts  22.8 us
    pallas_call x2, Pallas kernels, outgoing_pages(): pl.pallas_call(functools.partial(outgoing_kernel, by_quarter), grid_spec=...  8.25 us
    pallas_call x1, Pallas kernels, assemble(): pl.pallas_call(assemble_kernel, grid_spec=pltpu.PrefetchScalarGridSpec(nu...  7.87 us
    pallas_call x1, Pallas kernels, ffn(): pl.pallas_call(ffn_kernel, in_specs=[vmem] * (1 + 3 * n), out_specs=vmem,...  6.77 us
  transfers between devices with their start and end apart: 36, of which 12 were waited for; matrix products, arithmetic and copies ran while one was open for 0% of the time, Pallas kernels for 15%

profile of v9, /device:TPU:1, one launch (start us, length us, event | category | flops | bytes accessed | tf_op | source)
XLA Modules:
  0.0 216.4 jit_solution(7968193381540593759)
XLA Ops:
  2.0 3.8 %outgoing.2 = bf16[64,16,512]{2,1,0:T(8,128)(2,1)} custom-call(s32[1]{0:T(128)} %bitcast.mine_ref, s32[1]{0:T(128)S(6)} %select_n.17.twist_ref, s32[32,2]{1,0:T(8,128)} %copy.15.slot_ref, s32[32]{0:T(128)} %bitcast.31, bf16[64,128,512]{2,1,0:T(8,128)(2,1)} %pool_ref.5), custom_call_target="tpu_custom_call" | custom-call | flops 1200000000 | bytes 6000000 | tf_op jit(solution)/shard_map/outgoing/pallas_call | solution.py:54
  5.8 11.3 %all-to-all-start = ((bf16[32,2,16,512]{3,2,1,0:T(8,128)(2,1)}), bf16[32,2,16,512]{3,2,1,0:T(8,128)(2,1)S(1)}, u32[]{:S(2)}, u32[]{:S(2)}) async-start(bf16[32,2,16,512]{3,2,1,0:T(8,128)(2,1)} %bitcast.29), calls=%async_computation | async-start | bytes 2097152 | tf_op jit(solution)/shard_map/all_to_all | solution.py:505
  17.1 4.4 %outgoing.3 = bf16[64,32,512]{2,1,0:T(8,128)(2,1)} custom-call(s32[1]{0:T(128)} %bitcast.mine_ref, s32[1]{0:T(128)S(6)} %select_n.17.twist_ref, s32[32,2]{1,0:T(8,128)} %copy.15.slot_ref, s32[32]{0:T(128)} %bitcast.32, bf16[64,128,512]{2,1,0:T(8,128)(2,1)} %pool_ref.5), custom_call_target="tpu_custom_call" | custom-call | flops 1200000000 | bytes 6000000 | tf_op jit(solution)/shard_map/outgoing/pallas_call | solution.py:54
  21.6 13.6 %all-to-all-done = bf16[32,2,16,512]{3,2,1,0:T(8,128)(2,1)S(1)} async-done(((bf16[32,2,16,512]{3,2,1,0:T(8,128)(2,1)}), bf16[32,2,16,512]{3,2,1,0:T(8,128)(2,1)S(1)}, u32[]{:S(2)}, u32[]{:S(2)}) %all-to-all-start) | async-done | bytes 1048608 | tf_op jit(solution)/shard_map/all_to_all | solution.py:505
  35.2 4.2 %all-to-all-start.1 = ((bf16[32,2,32,512]{3,2,1,0:T(8,128)(2,1)}), bf16[32,2,32,512]{3,2,1,0:T(8,128)(2,1)S(1)}, u32[]{:S(2)}, u32[]{:S(2)}) async-start(bf16[32,2,32,512]{3,2,1,0:T(8,128)(2,1)} %bitcast.28), calls=%async_computation.1 | async-start | bytes 4194304 | tf_op jit(solution)/shard_map/all_to_all | solution.py:505
  41.6 2.6 %collective-permute-start.18 = (bf16[2048,128]{1,0:T(8,128)(2,1)}, bf16[2048,128]{1,0:T(8,128)(2,1)}, u32[]{:S(2)}, u32[]{:S(2)}) collective-permute-start(bf16[2048,128]{1,0:T(8,128)(2,1)} %refs_2_.1), channel_id=1, source_target_pairs={{0,6},{1,7},{2,4},{3,5},{4,2},{5,3},{6,0},{7,1},{8,14},{9,15},{10,... | collective-permute-start | bytes 1572872 | tf_op jit(solution)/shard_map/ppermute | solution.py:495
  46.1 5.8 %resident.1 = (f32[256,256]{1,0:T(8,128)S(1)}, f32[8,256]{1,0:T(8,128)S(1)}, bf16[256,256]{1,0:T(8,128)(2,1)S(1)}) custom-call(s32[1]{0:T(128)S(6)} %select_n.18.half_ref, bf16[128,256]{1,0:T(8,128)(2,1)S(1)} %bitcast.26, bf16[128,256]{1,0:T(8,128)(2,1)S(1)} %collective-permute-done.4.qb_ref, bf16[64,512]{1,0:T(8,128)(2,1)S(1)} %copy-done.34, ...), custom_call_target="tpu_custom_call" | custom-call | flops 3200000000 | bytes 16000000 | tf_op jit(solution)/shard_map/resident/pallas_call | solution.py:176
  52.7 15.6 %all-to-all-done.1 = bf16[32,2,32,512]{3,2,1,0:T(8,128)(2,1)S(1)} async-done(((bf16[32,2,32,512]{3,2,1,0:T(8,128)(2,1)}), bf16[32,2,32,512]{3,2,1,0:T(8,128)(2,1)S(1)}, u32[]{:S(2)}, u32[]{:S(2)}) %all-to-all-start.1) | async-done | bytes 2097184 | tf_op jit(solution)/shard_map/all_to_all | solution.py:505
  69.2 6.2 %moved.1 = (f32[264,128]{1,0:T(8,128)S(1)}, f32[264,128]{1,0:T(8,128)S(1)}) custom-call(s32[1]{0:T(128)} %bitcast.mine_ref, bf16[256,256]{1,0:T(8,128)(2,1)S(1)} %get-tuple-element.11.qt_ref, s32[16,256]{1,0:T(8,128)S(1)} %tile.18.tab_ref, s32[1,256]{1,0:T(1,128)S(1)} %tile.20.len_ref, f32[256,256]{1,0:T(8,128)S(1)} %copy-done.37, ...), custom_call_target="tpu_custom_call" | custom-call | flops 3200000000 | bytes 16000000 | tf_op jit(solution)/shard_map/moved/pallas_call | solution.py:245
  75.4 2.6 %collective-permute-start.5 = (f32[264,128]{1,0:T(8,128)S(1)}, f32[264,128]{1,0:T(8,128)S(1)}, u32[]{:S(2)}, u32[]{:S(2)}) collective-permute-start(f32[264,128]{1,0:T(8,128)S(1)} %get-tuple-element.15), channel_id=1, source_target_pairs={{0,1},{1,0},{2,3},{3,2},{4,5},{5,4},{6,7},{7,6},{8,9},{9,8},{10,11... | collective-permute-start | bytes 405512 | tf_op jit(solution)/shard_map/ppermute | solution.py:495
  78.0 6.7 %collective-permute-done.11.refs_7_ = bf16[2048,128]{1,0:T(8,128)(2,1)} collective-permute-done((bf16[2048,128]{1,0:T(8,128)(2,1)}, bf16[2048,128]{1,0:T(8,128)(2,1)}, u32[]{:S(2)}, u32[]{:S(2)}) %collective-permute-start.11) | collective-permute-done | bytes 524320 | tf_op jit(solution)/shard_map/ppermute | solution.py:495
  91.7 3.8 %collective-permute-done.13.refs_9_ = bf16[128,2048]{1,0:T(8,128)(2,1)} collective-permute-done((bf16[128,2048]{1,0:T(8,128)(2,1)S(1)}, bf16[128,2048]{1,0:T(8,128)(2,1)}, u32[]{:S(2)}, u32[]{:S(2)}) %collective-permute-start.13) | collective-permute-done | bytes 524320 | tf_op jit(solution)/shard_map/ppermute | solution.py:495
  95.5 3.7 %collective-permute-start.9 = (bf16[2048,128]{1,0:T(8,128)(2,1)S(1)}, bf16[2048,128]{1,0:T(8,128)(2,1)S(1)}, u32[]{:S(2)}, u32[]{:S(2)}) collective-permute-start(bf16[2048,128]{1,0:T(8,128)(2,1)S(1)} %copy-done.6), channel_id=1, source_target_pairs={{0,1},{1,0},{2,3},{3,2},{4,5},{5,4},{6,7},{7,6},{8,9},{9,8},{10,11... | collective-permute-start | bytes 1572872 | tf_op jit(solution)/shard_map/ppermute | solution.py:495
  104.8 7.9 %collective-permute-done.23.refs_19_ = bf16[2048,128]{1,0:T(8,128)(2,1)S(1)} collective-permute-done((bf16[2048,128]{1,0:T(8,128)(2,1)}, bf16[2048,128]{1,0:T(8,128)(2,1)S(1)}, u32[]{:S(2)}, u32[]{:S(2)}) %collective-permute-start.23) | collective-permute-done | bytes 524320 | tf_op jit(solution)/shard_map/ppermute | solution.py:495
  118.0 9.7 %collective-permute-done.25.refs_21_ = bf16[128,2048]{1,0:T(8,128)(2,1)S(1)} collective-permute-done((bf16[128,2048]{1,0:T(8,128)(2,1)}, bf16[128,2048]{1,0:T(8,128)(2,1)S(1)}, u32[]{:S(2)}, u32[]{:S(2)}) %collective-permute-start.25) | collective-permute-done | bytes 524320 | tf_op jit(solution)/shard_map/ppermute | solution.py:495
  132.8 6.6 %all-to-all-start.2 = ((bf16[16,16,2048]{2,1,0:T(8,128)(2,1)}), bf16[16,16,2048]{2,1,0:T(8,128)(2,1)S(1)}, u32[]{:S(2)}, u32[]{:S(2)}) async-start(bf16[16,16,2048]{2,1,0:T(8,128)(2,1)} %copy-done.3), calls=%async_computation.2 | async-start | bytes 2097152 | tf_op jit(solution)/shard_map/all_to_all | solution.py:505
  140.8 3.6 %collective-permute-done.20.refs_16_ = bf16[2048,128]{1,0:T(8,128)(2,1)S(1)} collective-permute-done((bf16[2048,128]{1,0:T(8,128)(2,1)}, bf16[2048,128]{1,0:T(8,128)(2,1)S(1)}, u32[]{:S(2)}, u32[]{:S(2)}) %collective-permute-start.20) | collective-permute-done | bytes 524320 | tf_op jit(solution)/shard_map/ppermute | solution.py:495
  147.6 9.1 %all-to-all-done.2 = bf16[16,16,2048]{2,1,0:T(8,128)(2,1)S(1)} async-done(((bf16[16,16,2048]{2,1,0:T(8,128)(2,1)}), bf16[16,16,2048]{2,1,0:T(8,128)(2,1)S(1)}, u32[]{:S(2)}, u32[]{:S(2)}) %all-to-all-start.2) | async-done | bytes 1048608 | tf_op jit(solution)/shard_map/all_to_all | solution.py:505
  171.3 6.8 %ffn.1 = bf16[256,2048]{1,0:T(8,128)(2,1)S(1)} custom-call(bf16[256,2048]{1,0:T(8,128)(2,1)S(1)} %bitcast.19, bf16[2048,128]{1,0:T(8,128)(2,1)S(1)} %copy-done.5, bf16[2048,128]{1,0:T(8,128)(2,1)S(1)} %copy-done.7, bf16[128,2048]{1,0:T(8,128)(2,1)S(1)} %copy-done.9, bf16[2048,128]{1,0:T(8,128)(2,1)S(1)} %copy-done.15, bf16[2048,128]{1,0:T(8,128)(2,1)S(1)} %copy-done.17, ...), custom_call_target="tpu_custom_call" | custom-call | flops 3200000000 | bytes 16000000 | tf_op jit(solution)/shard_map/ffn/pallas_call | solution.py:386
  179.1 4.5 %all-to-all-start.3 = ((bf16[16,16,2048]{2,1,0:T(8,128)(2,1)}), bf16[16,16,2048]{2,1,0:T(8,128)(2,1)}, u32[]{:S(2)}, u32[]{:S(2)}) async-start(bf16[16,16,2048]{2,1,0:T(8,128)(2,1)} %bitcast.20), calls=%async_computation.3 | async-start | bytes 2097152 | tf_op jit(solution)/shard_map/all_to_all | solution.py:505
  185.3 13.8 %all-to-all-done.3.parts_ref = bf16[16,16,2048]{2,1,0:T(8,128)(2,1)} async-done(((bf16[16,16,2048]{2,1,0:T(8,128)(2,1)}), bf16[16,16,2048]{2,1,0:T(8,128)(2,1)}, u32[]{:S(2)}, u32[]{:S(2)}) %all-to-all-start.3) | async-done | bytes 1048608 | tf_op jit(solution)/shard_map/all_to_all | solution.py:505
  200.5 3.3 %collective-permute-start.29 = (bf16[16,2048]{1,0:T(8,128)(2,1)S(1)}, bf16[16,2048]{1,0:T(8,128)(2,1)S(1)}, u32[]{:S(2)}, u32[]{:S(2)}) collective-permute-start(bf16[16,2048]{1,0:T(8,128)(2,1)S(1)} %finish.1.refs_0_), channel_id=1, source_target_pairs={{0,1},{1,0},{2,3},{3,2},{4,5},{5,4},{6,7},{7,6},{8,9},{9,8},{10,11... | collective-permute-start | bytes 196616 | tf_op jit(solution)/shard_map/ppermute | solution.py:495
  203.8 4.0 %collective-permute-start.31 = (bf16[16,2048]{1,0:T(8,128)(2,1)S(1)}, bf16[16,2048]{1,0:T(8,128)(2,1)S(1)}, u32[]{:S(2)}, u32[]{:S(2)}) collective-permute-start(bf16[16,2048]{1,0:T(8,128)(2,1)S(1)} %collective-permute-done.30.refs_2_), channel_id=1, source_target_pairs={{0,1},{1,0},{2,3},{3,2},{4,5},{5,4},{6,7},{7,6},{8,9},{9,8},{10,11... | collective-permute-start | bytes 196616 | tf_op jit(solution)/shard_map/ppermute | solution.py:495
  207.8 7.9 %assemble.1 = bf16[64,128,512]{2,1,0:T(8,128)(2,1)} custom-call(s32[1]{0:T(128)} %bitcast.mine_ref, bf16[64,16,512]{2,1,0:T(8,128)(2,1)S(1)} %bitcast.24, bf16[64,16,512]{2,1,0:T(8,128)(2,1)} %collective-permute-done.refs_1_.z_ref, bf16[64,32,512]{2,1,0:T(8,128)(2,1)S(1)} %bitcast.18, bf16[64,16,512]{2,1,0:T(8,128)(2,1)} %collective-permute-done.1.refs_3_, ...), custom_call_target="tpu_custom_call" | custom-call | flops 2400000000 | bytes 12000000 | tf_op jit(solution)/shard_map/assemble/pallas_call | solution.py:467
  (148 shorter events, 54.0 us)
Async XLA Ops:
  5.8 29.3 %all-to-all-start = ((bf16[32,2,16,512]{3,2,1,0:T(8,128)(2,1)}), bf16[32,2,16,512]{3,2,1,0:T(8,128)(2,1)S(1)}, u32[]{:S(2)}, u32[]{:S(2)}) async-start(bf16[32,2,16,512]{3,2,1,0:T(8,128)(2,1)} %bitcast.29), calls=%async_computation | async-start | bytes 2097152 | tf_op jit(solution)/shard_map/all_to_all | solution.py:505
  35.2 33.1 %all-to-all-start.1 = ((bf16[32,2,32,512]{3,2,1,0:T(8,128)(2,1)}), bf16[32,2,32,512]{3,2,1,0:T(8,128)(2,1)S(1)}, u32[]{:S(2)}, u32[]{:S(2)}) async-start(bf16[32,2,32,512]{3,2,1,0:T(8,128)(2,1)} %bitcast.28), calls=%async_computation.1 | async-start | bytes 4194304 | tf_op jit(solution)/shard_map/all_to_all | solution.py:505
  39.3 28.9 %collective-permute-start = (bf16[64,16,512]{2,1,0:T(8,128)(2,1)S(1)}, bf16[64,16,512]{2,1,0:T(8,128)(2,1)}, u32[]{:S(2)}, u32[]{:S(2)}) collective-permute-start(bf16[64,16,512]{2,1,0:T(8,128)(2,1)S(1)} %bitcast.21), channel_id=1, source_target_pairs={{0,2},{1,3},{2,0},{3,1},{4,6},{5,7},{6,4},{7,5},{8,10},{9,11},{10,... | collective-permute-start | bytes 3145736 | tf_op jit(solution)/shard_map/ppermute | solution.py:495
  41.6 43.5 %collective-permute-start.18 = (bf16[2048,128]{1,0:T(8,128)(2,1)}, bf16[2048,128]{1,0:T(8,128)(2,1)}, u32[]{:S(2)}, u32[]{:S(2)}) collective-permute-start(bf16[2048,128]{1,0:T(8,128)(2,1)} %refs_2_.1), channel_id=1, source_target_pairs={{0,6},{1,7},{2,4},{3,5},{4,2},{5,3},{6,0},{7,1},{8,14},{9,15},{10,... | collective-permute-start | bytes 1572872 | tf_op jit(solution)/shard_map/ppermute | solution.py:495
  44.2 47.0 %collective-permute-start.12 = (bf16[2048,128]{1,0:T(8,128)(2,1)}, bf16[2048,128]{1,0:T(8,128)(2,1)}, u32[]{:S(2)}, u32[]{:S(2)}) collective-permute-start(bf16[2048,128]{1,0:T(8,128)(2,1)} %refs_2_.1), channel_id=1, source_target_pairs={{0,2},{1,3},{2,0},{3,1},{4,6},{5,7},{6,4},{7,5},{8,10},{9,11},{10,... | collective-permute-start | bytes 1572872 | tf_op jit(solution)/shard_map/ppermute | solution.py:495
  45.3 39.4 %collective-permute-start.11 = (bf16[2048,128]{1,0:T(8,128)(2,1)}, bf16[2048,128]{1,0:T(8,128)(2,1)}, u32[]{:S(2)}, u32[]{:S(2)}) collective-permute-start(bf16[2048,128]{1,0:T(8,128)(2,1)} %refs_1_.1), channel_id=1, source_target_pairs={{0,2},{1,3},{2,0},{3,1},{4,6},{5,7},{6,4},{7,5},{8,10},{9,11},{10,... | collective-permute-start | bytes 1572872 | tf_op jit(solution)/shard_map/ppermute | solution.py:495
  45.8 42.4 %collective-permute-start.19 = (bf16[128,2048]{1,0:T(8,128)(2,1)}, bf16[128,2048]{1,0:T(8,128)(2,1)}, u32[]{:S(2)}, u32[]{:S(2)}) collective-permute-start(bf16[128,2048]{1,0:T(8,128)(2,1)} %refs_3_.1), channel_id=1, source_target_pairs={{0,6},{1,7},{2,4},{3,5},{4,2},{5,3},{6,0},{7,1},{8,14},{9,15},{10,... | collective-permute-start | bytes 1572872 | tf_op jit(solution)/shard_map/ppermute | solution.py:495
  75.4 15.1 %collective-permute-start.5 = (f32[264,128]{1,0:T(8,128)S(1)}, f32[264,128]{1,0:T(8,128)S(1)}, u32[]{:S(2)}, u32[]{:S(2)}) collective-permute-start(f32[264,128]{1,0:T(8,128)S(1)} %get-tuple-element.15), channel_id=1, source_target_pairs={{0,1},{1,0},{2,3},{3,2},{4,5},{5,4},{6,7},{7,6},{8,9},{9,8},{10,11... | collective-permute-start | bytes 405512 | tf_op jit(solution)/shard_map/ppermute | solution.py:495
  85.0 14.2 %collective-permute-start.17 = (bf16[2048,128]{1,0:T(8,128)(2,1)S(1)}, bf16[2048,128]{1,0:T(8,128)(2,1)S(1)}, u32[]{:S(2)}, u32[]{:S(2)}) collective-permute-start(bf16[2048,128]{1,0:T(8,128)(2,1)S(1)} %copy-done.4), channel_id=1, source_target_pairs={{0,6},{1,7},{2,4},{3,5},{4,2},{5,3},{6,0},{7,1},{8,14},{9,15},{10,... | collective-permute-start | bytes 1572872 | tf_op jit(solution)/shard_map/ppermute | solution.py:495
  88.2 13.0 %collective-permute-start.10 = (bf16[128,2048]{1,0:T(8,128)(2,1)S(1)}, bf16[128,2048]{1,0:T(8,128)(2,1)S(1)}, u32[]{:S(2)}, u32[]{:S(2)}) collective-permute-start(bf16[128,2048]{1,0:T(8,128)(2,1)S(1)} %copy-done.8), channel_id=1, source_target_pairs={{0,1},{1,0},{2,3},{3,2},{4,5},{5,4},{6,7},{7,6},{8,9},{9,8},{10,11... | collective-permute-start | bytes 1572872 | tf_op jit(solution)/shard_map/ppermute | solution.py:495
  99.2 13.5 %collective-permute-start.23 = (bf16[2048,128]{1,0:T(8,128)(2,1)}, bf16[2048,128]{1,0:T(8,128)(2,1)S(1)}, u32[]{:S(2)}, u32[]{:S(2)}) collective-permute-start(bf16[2048,128]{1,0:T(8,128)(2,1)} %collective-permute-done.11.refs_7_), channel_id=1, source_target_pairs={{0,6},{1,7},{2,4},{3,5},{4,2},{5,3},{6,0},{7,1},{8,14},{9,15},{10,... | collective-permute-start | bytes 1572872 | tf_op jit(solution)/shard_map/ppermute | solution.py:495
  101.3 38.1 %collective-permute-start.14 = (bf16[2048,128]{1,0:T(8,128)(2,1)}, bf16[2048,128]{1,0:T(8,128)(2,1)}, u32[]{:S(2)}, u32[]{:S(2)}) collective-permute-start(bf16[2048,128]{1,0:T(8,128)(2,1)} %collective-permute-done.11.refs_7_), channel_id=1, source_target_pairs={{0,1},{1,0},{2,3},{3,2},{4,5},{5,4},{6,7},{7,6},{8,9},{9,8},{10,11... | collective-permute-start | bytes 1572872 | tf_op jit(solution)/shard_map/ppermute | solution.py:495
  102.9 13.6 %collective-permute-start.24 = (bf16[2048,128]{1,0:T(8,128)(2,1)}, bf16[2048,128]{1,0:T(8,128)(2,1)S(1)}, u32[]{:S(2)}, u32[]{:S(2)}) collective-permute-start(bf16[2048,128]{1,0:T(8,128)(2,1)} %collective-permute-done.18.refs_14_), channel_id=1, source_target_pairs={{0,2},{1,3},{2,0},{3,1},{4,6},{5,7},{6,4},{7,5},{8,10},{9,11},{10,... | collective-permute-start | bytes 1572872 | tf_op jit(solution)/shard_map/ppermute | solution.py:495
  103.0 24.8 %collective-permute-start.25 = (bf16[128,2048]{1,0:T(8,128)(2,1)}, bf16[128,2048]{1,0:T(8,128)(2,1)S(1)}, u32[]{:S(2)}, u32[]{:S(2)}) collective-permute-start(bf16[128,2048]{1,0:T(8,128)(2,1)} %collective-permute-done.19.refs_15_), channel_id=1, source_target_pairs={{0,2},{1,3},{2,0},{3,1},{4,6},{5,7},{6,4},{7,5},{8,10},{9,11},{10,... | collective-permute-start | bytes 1572872 | tf_op jit(solution)/shard_map/ppermute | solution.py:495
  104.4 26.1 %collective-permute-start.7 = (f32[16,2048]{1,0:T(8,128)S(1)}, f32[16,2048]{1,0:T(8,128)S(1)}, u32[]{:S(2)}, u32[]{:S(2)}) collective-permute-start(f32[16,2048]{1,0:T(8,128)S(1)} %fusion), channel_id=1, source_target_pairs={{0,2},{1,3},{2,0},{3,1},{4,6},{5,7},{6,4},{7,5},{8,10},{9,11},{10,... | collective-permute-start | bytes 393224 | tf_op jit(solution)/shard_map/ppermute | solution.py:495
  112.7 27.1 %collective-permute-start.21 = (bf16[2048,128]{1,0:T(8,128)(2,1)}, bf16[2048,128]{1,0:T(8,128)(2,1)}, u32[]{:S(2)}, u32[]{:S(2)}) collective-permute-start(bf16[2048,128]{1,0:T(8,128)(2,1)} %collective-permute-done.18.refs_14_), channel_id=1, source_target_pairs={{0,1},{1,0},{2,3},{3,2},{4,5},{5,4},{6,7},{7,6},{8,9},{9,8},{10,11... | collective-permute-start | bytes 1572872 | tf_op jit(solution)/shard_map/ppermute | solution.py:495
  116.5 23.5 %collective-permute-start.22 = (bf16[128,2048]{1,0:T(8,128)(2,1)}, bf16[128,2048]{1,0:T(8,128)(2,1)}, u32[]{:S(2)}, u32[]{:S(2)}) collective-permute-start(bf16[128,2048]{1,0:T(8,128)(2,1)} %collective-permute-done.19.refs_15_), channel_id=1, source_target_pairs={{0,1},{1,0},{2,3},{3,2},{4,5},{5,4},{6,7},{7,6},{8,9},{9,8},{10,11... | collective-permute-start | bytes 1572872 | tf_op jit(solution)/shard_map/ppermute | solution.py:495
  127.8 12.5 %collective-permute-start.15 = (bf16[2048,128]{1,0:T(8,128)(2,1)}, bf16[2048,128]{1,0:T(8,128)(2,1)}, u32[]{:S(2)}, u32[]{:S(2)}) collective-permute-start(bf16[2048,128]{1,0:T(8,128)(2,1)} %collective-permute-done.12.refs_8_), channel_id=1, source_target_pairs={{0,1},{1,0},{2,3},{3,2},{4,5},{5,4},{6,7},{7,6},{8,9},{9,8},{10,11... | collective-permute-start | bytes 1572872 | tf_op jit(solution)/shard_map/ppermute | solution.py:495
  132.8 24.0 %all-to-all-start.2 = ((bf16[16,16,2048]{2,1,0:T(8,128)(2,1)}), bf16[16,16,2048]{2,1,0:T(8,128)(2,1)S(1)}, u32[]{:S(2)}, u32[]{:S(2)}) async-start(bf16[16,16,2048]{2,1,0:T(8,128)(2,1)} %copy-done.3), calls=%async_computation.2 | async-start | bytes 2097152 | tf_op jit(solution)/shard_map/all_to_all | solution.py:505
  139.4 68.4 %collective-permute-start.3 = (bf16[64,32,512]{2,1,0:T(8,128)(2,1)S(1)}, bf16[64,32,512]{2,1,0:T(8,128)(2,1)}, u32[]{:S(2)}, u32[]{:S(2)}) collective-permute-start(bf16[64,32,512]{2,1,0:T(8,128)(2,1)S(1)} %bitcast.17), channel_id=1, source_target_pairs={{0,1},{1,0},{2,3},{3,2},{4,5},{5,4},{6,7},{7,6},{8,9},{9,8},{10,11... | collective-permute-start | bytes 6291464 | tf_op jit(solution)/shard_map/ppermute | solution.py:495
  179.1 20.0 %all-to-all-start.3 = ((bf16[16,16,2048]{2,1,0:T(8,128)(2,1)}), bf16[16,16,2048]{2,1,0:T(8,128)(2,1)}, u32[]{:S(2)}, u32[]{:S(2)}) async-start(bf16[16,16,2048]{2,1,0:T(8,128)(2,1)} %bitcast.20), calls=%async_computation.3 | async-start | bytes 2097152 | tf_op jit(solution)/shard_map/all_to_all | solution.py:505
  183.6 24.2 %collective-permute-start.1 = (bf16[64,16,512]{2,1,0:T(8,128)(2,1)S(1)}, bf16[64,16,512]{2,1,0:T(8,128)(2,1)}, u32[]{:S(2)}, u32[]{:S(2)}) collective-permute-start(bf16[64,16,512]{2,1,0:T(8,128)(2,1)S(1)} %bitcast.23), channel_id=1, source_target_pairs={{0,1},{1,0},{2,3},{3,2},{4,5},{5,4},{6,7},{7,6},{8,9},{9,8},{10,11... | collective-permute-start | bytes 3145736 | tf_op jit(solution)/shard_map/ppermute | solution.py:495
  185.2 22.6 %collective-permute-start.2 = (bf16[64,16,512]{2,1,0:T(8,128)(2,1)}, bf16[64,16,512]{2,1,0:T(8,128)(2,1)}, u32[]{:S(2)}, u32[]{:S(2)}) collective-permute-start(bf16[64,16,512]{2,1,0:T(8,128)(2,1)} %collective-permute-done.refs_1_.z_ref), channel_id=1, source_target_pairs={{0,1},{1,0},{2,3},{3,2},{4,5},{5,4},{6,7},{7,6},{8,9},{9,8},{10,11... | collective-permute-start | bytes 3145736 | tf_op jit(solution)/shard_map/ppermute | solution.py:495
  200.5 15.1 %collective-permute-start.29 = (bf16[16,2048]{1,0:T(8,128)(2,1)S(1)}, bf16[16,2048]{1,0:T(8,128)(2,1)S(1)}, u32[]{:S(2)}, u32[]{:S(2)}) collective-permute-start(bf16[16,2048]{1,0:T(8,128)(2,1)S(1)} %finish.1.refs_0_), channel_id=1, source_target_pairs={{0,1},{1,0},{2,3},{3,2},{4,5},{5,4},{6,7},{7,6},{8,9},{9,8},{10,11... | collective-permute-start | bytes 196616 | tf_op jit(solution)/shard_map/ppermute | solution.py:495
  (53 other events, 489.7 us)
